TPU v7x, 256 devices: a whole 4x4x8 slice. The times are simulated.
256 devices in a mesh: par: 16 (over x, z_hi, core), freq: 16 (over z_lo, y).
Axes of the slice: x: 4, y: 4, z: 8 (z_hi: 2, z_lo: 4; z = z_hi * 4 + z_lo), core: 2. Of those that a mesh axis runs over, the one named last changes fastest.
Arguments:
- probes: bfloat16 [64, 600, 420], P('freq'), may hold values from -6 to 6
- map_real: bfloat16 [224, 600, 4096], P('freq', None, 'par'), may hold values from -0.09375 to 0.09375
- map_imag: bfloat16 [224, 600, 4096], P('freq', None, 'par'), may hold values from -0.09375 to 0.09375
- prior_var: float32 [4096], P('par'), may hold values from 0.05 to 13, as said below
Outputs:
- applied: bfloat16 [64, 600, 420], P('freq')
Inputs may be any that keep to these rules, and one draw needn't show every extreme that they name: `prior_var`: prior variances are positive.
All inputs are finite; a program needn't handle non-finite values.
Results may differ from a plain program's by a relative error of at most 0.014.
Values may be sent and summed in bfloat16 or wider, within the bound.
No kernel may reach another device: no remote copies, remote signals or barrier semaphores. Data moves between devices by JAX's collectives and lax.ppermute only.
A program may use at most 64 MiB of HBM per device.

v0:
```python
import functools

import jax
import jax.numpy as jnp
from jax import lax
from jax.sharding import Mesh
from jax.sharding import PartitionSpec as P

SENSORS = 600
STEPS = 420
PERIOD = 840
PROBES = 64
FREQ = ("freq_0", "freq_1")
PAR_FREQ = ("par_0", "par_1", "par_2", "freq_0", "freq_1")
PAR = ("par_0", "par_1", "par_2")


noise_ratio = 0.5


def one_axis_at_a_time(shard, axes):
    return functools.reduce(lax.psum, axes, shard)


def split_up(shard, dim, length):
    dims = shard.shape
    parts = shard.reshape(*dims[:dim], length, dims[dim] // length, *dims[dim + 1 :])
    return jnp.moveaxis(parts, dim, 0)


def summed_on_arrival(shard, axis, dim):
    length = lax.axis_size(axis)
    parts = lax.all_to_all(split_up(shard, dim, length), axis, 0, 0, tiled=True)
    return jnp.sum(parts.astype(jnp.float32), axis=0)


def sum_by_axis(shard, axes, dim):
    far, near = axes
    parts = split_up(shard, dim, lax.axis_size(far))
    nearer = summed_on_arrival(parts, near, dim + 1)
    arrived = lax.all_to_all(
        nearer.astype(jnp.bfloat16), far, split_axis=0, concat_axis=0, tiled=True
    )
    return arrived.astype(jnp.float32).sum(axis=0)


def sent_to_all(shard, axis):
    copies = jnp.broadcast_to(shard, (lax.axis_size(axis), *shard.shape))
    return lax.all_to_all(copies, axis, split_axis=0, concat_axis=0, tiled=True)


def joined_along(parts, dim):
    parts = jnp.moveaxis(parts, 0, dim)
    dims = parts.shape
    return parts.reshape(*dims[:dim], dims[dim] * dims[dim + 1], *dims[dim + 2 :])


def gather_axes(shard, axes, dim):
    far, near = axes
    parts = sent_to_all(sent_to_all(shard, far), near)
    return joined_along(parts.swapaxes(0, 1).reshape(-1, *shard.shape), dim)


def split_product(left, table):
    upper = table.astype(jnp.bfloat16)
    lower = (table - upper.astype(jnp.float32)).astype(jnp.bfloat16)
    return jnp.dot(left, upper, preferred_element_type=jnp.float32) + jnp.dot(
        left, lower, preferred_element_type=jnp.float32
    )


def shards(probes, map_real, map_imag, prior_var):
    freq_count = lax.axis_size(FREQ)
    bins_dev = map_real.shape[0]
    probe_block = probes.shape[0]
    total_bins = bins_dev * freq_count
    time_steps = jnp.arange(STEPS, dtype=jnp.int32)
    bin_index = jnp.arange(total_bins, dtype=jnp.int32)
    product_index = time_steps[:, None] * bin_index[None, :] % PERIOD
    angles = product_index.astype(jnp.float32) * (2.0 * jnp.pi / PERIOD)
    norm_scale = 1.0 / jnp.sqrt(jnp.float32(PERIOD))
    cosines = jnp.cos(angles) * norm_scale
    sines = jnp.sin(angles) * norm_scale
    forward = jnp.stack([cosines, -sines], axis=2).reshape(STEPS, 2 * total_bins)
    all_weight = jnp.where(bin_index == 0, 1.0, 2.0).astype(jnp.float32)
    inverse = jnp.stack([cosines * all_weight[None, :], -sines * all_weight[None, :]], axis=2)
    inverse = inverse.reshape(STEPS, 2 * total_bins).T
    flattened = probes.reshape(probe_block * SENSORS, STEPS)
    spectrum = split_product(flattened, forward).astype(jnp.bfloat16)
    spectrum = spectrum.reshape(probe_block, SENSORS, 2 * total_bins)
    exchanged = lax.all_to_all(spectrum, FREQ, split_axis=2, concat_axis=0, tiled=True)
    all_probes = exchanged.shape[0]
    operand = exchanged.reshape(all_probes, SENSORS, bins_dev, 2).transpose(2, 1, 3, 0)
    operand = operand.reshape(bins_dev, SENSORS, 2 * all_probes)
    left_real = jnp.einsum("ksp,ksc->kpc", map_real, operand, preferred_element_type=jnp.float32)
    left_imag = jnp.einsum("ksp,ksc->kpc", map_imag, operand, preferred_element_type=jnp.float32)
    u_real = left_real[..., :all_probes] + left_imag[..., all_probes:]
    u_imag = left_real[..., all_probes:] - left_imag[..., :all_probes]
    global_bin = lax.axis_index(FREQ) * bins_dev + jnp.arange(bins_dev, dtype=jnp.int32)
    bin_weight = jnp.where(global_bin == 0, 1.0, 2.0).astype(jnp.float32)
    quadratic = jnp.sum(
        bin_weight[:, None, None] * prior_var[None, :, None] * (u_real * u_real + u_imag * u_imag)
    )
    trace_est = one_axis_at_a_time(quadratic, PAR_FREQ) / (PROBES * SENSORS * STEPS)
    scaled = (jnp.concatenate([u_real, u_imag], axis=-1) * prior_var[None, :, None]).astype(
        jnp.bfloat16
    )
    right_real = jnp.einsum("ksp,kpc->ksc", map_real, scaled, preferred_element_type=jnp.float32)
    right_imag = jnp.einsum("ksp,kpc->ksc", map_imag, scaled, preferred_element_type=jnp.float32)
    w_partial = jnp.concatenate(
        [
            right_real[..., :all_probes] - right_imag[..., all_probes:],
            right_real[..., all_probes:] + right_imag[..., :all_probes],
        ],
        axis=-1,
    )
    share_sum = sum_by_axis(
        w_partial.astype(jnp.bfloat16), (("par_0", "par_1"), "par_2"), 2
    ).astype(jnp.bfloat16)
    summed = gather_axes(share_sum, (("par_0", "par_1"), "par_2"), 2)
    outgoing = summed.reshape(bins_dev, SENSORS, 2, all_probes).transpose(3, 1, 0, 2)
    outgoing = outgoing.reshape(all_probes, SENSORS, 2 * bins_dev)
    by_probe = lax.all_to_all(outgoing, FREQ, split_axis=0, concat_axis=2, tiled=True)
    by_rows = by_probe.reshape(probe_block * SENSORS, 2 * total_bins)
    response = split_product(by_rows, inverse).reshape(probe_block, SENSORS, STEPS)
    return (response + noise_ratio * trace_est * probes.astype(jnp.float32)).astype(jnp.bfloat16)


def solution(mesh):
    torus = Mesh(
        mesh.devices.reshape(4, 2, 2, 4, 4), ("par_0", "par_1", "par_2", "freq_0", "freq_1")
    )
    in_specs = (P(FREQ, None, None), P(FREQ, None, PAR), P(FREQ, None, PAR), P(PAR))
    out_specs = P(FREQ, None, None)
    return jax.shard_map(
        shards, mesh=torus, in_specs=in_specs, out_specs=out_specs, check_vma=False
    )
```

profile of v0, /device:TPU:2, one launch (start us, length us, event | category | flops | bytes accessed | tf_op | source)
XLA Modules:
  0.0 322.4 jit_solution(3733244251413938132)
XLA Ops:
  0.0 15.6 %multiply_negate_fusion = (f32[420,224,1]{0,2,1:T(1,128)S(1)}, f32[420,224,1]{0,2,1:T(1,128)S(1)}) fusion(), kind=kLoop, calls=%fused_computation.29 | loop fusion | flops 1128960 | bytes 752640 | tf_op jit(solution)/shard_map/neg | solution.py:84
  17.8 3.1 reshape.209
  21.3 3.1 fusion.20
  25.8 3.6 %reshape.210 = bf16[4,600,448]{1,0,2:T(4,128)(2,1)} reshape(bf16[2400,448]{0,1:T(8,128)(2,1)S(1)} %fusion.3) | data formatting | bytes 4300800 | tf_op jit(solution)/shard_map/reshape | solution.py:90
  29.3 8.8 %all-to-all-start = ((bf16[4,600,448]{1,0,2:T(4,128)(2,1)}), bf16[4,600,448]{1,0,2:T(4,128)(2,1)S(1)}, u32[]{:S(2)}, u32[]{:S(2)}) async-start(bf16[4,600,448]{1,0,2:T(4,128)(2,1)} %reshape.210), calls=%async_computation | async-start | bytes 4587520 | tf_op jit(solution)/shard_map/all_to_all | solution.py:91
  38.2 46.3 %all-to-all-done = bf16[4,600,448]{1,0,2:T(4,128)(2,1)S(1)} async-done(((bf16[4,600,448]{1,0,2:T(4,128)(2,1)}), bf16[4,600,448]{1,0,2:T(4,128)(2,1)S(1)}, u32[]{:S(2)}, u32[]{:S(2)}) %all-to-all-start) | async-done | bytes 2150432 | tf_op jit(solution)/shard_map/all_to_all | solution.py:91
  84.5 2.6 copy.26
  87.1 3.8 %reshape.211 = bf16[64,600,14,2]{1,0,3,2:T(8,128)(2,1)S(1)} reshape(bf16[16,4,600,28]{2,1,0,3:T(4,128)(2,1)} %copy.26) | data formatting | bytes 4300800 | tf_op jit(solution)/shard_map/reshape | solution.py:93
  91.0 3.3 %convolution_bitcast_fusion.2 = f32[14,256,128]{1,2,0:T(8,128)S(1)} fusion(bf16[14,600,128]{1,2,0:T(8,128)(2,1)S(1)} %bitcast.85, bf16[14,600,256]{2,1,0:T(8,128)(2,1)} %param.6), kind=kOutput, calls=%fused_computation.16 | convolution fusion | flops 550502400 | bytes 8286208 | tf_op jit(solution)/shard_map/ksp,ksc->kpc/dot_general | solution.py:96
  94.2 3.2 convolution_bitcast_fusion.3
  101.2 3.4 %fusion.2 = (bf16[14,600,64]{2,1,0:T(8,128)(2,1)}, bf16[14,600,64]{2,1,0:T(8,128)(2,1)S(1)}) fusion(f32[14,600,128]{2,1,0:T(8,128)S(1)} %convolution_bitcast_fusion, f32[14,600,128]{2,1,0:T(8,128)S(1)} %convolution_bitcast_fusion.1), kind=kLoop, calls=%fused_computation.6 | loop fusion | flops 2150400 | bytes 10752000 | tf_op jit(solution)/shard_map/convert.5
  104.6 3.1 copy.31
  107.7 2.9 copy.32
  112.4 5.6 %all_to_all.50 = bf16[2,8,14,600,8]{3,4,2,1,0:T(8,128)(2,1)S(1)} all-to-all(bf16[2,8,14,600,8]{3,4,2,1,0:T(8,128)(2,1)S(1)} %copy.34), channel_id=1, replica_groups=mesh['par_0'=4,'par_1'=2,'par_2'=2,'freq_0'=4,'freq_1'=4] {'par_2'}, dimensions={0} | all-to-all | bytes 4300800 | tf_op jit(solution)/shard_map/all_to_all | solution.py:33
  119.2 39.4 %all_to_all.51 = bf16[8,14,600,8]{2,3,1,0:T(8,128)(2,1)S(1)} all-to-all(bf16[8,14,600,8]{2,3,1,0:T(8,128)(2,1)S(1)} %reduce_sum.33), channel_id=1, replica_groups=mesh['par_0'=4,'par_1'=2,'par_2'=2,'freq_0'=4,'freq_1'=4] {'par_0','par_1'}, dimensions={0} | all-to-all | bytes 2150400 | tf_op jit(solution)/shard_map/all_to_all | solution.py:41
  158.9 29.6 %all_to_all.52 = bf16[8,14,600,8]{2,3,1,0:T(8,128)(2,1)S(1)} all-to-all(bf16[8,14,600,8]{2,3,1,0:T(8,128)(2,1)S(1)} %broadcast_in_dim.29), channel_id=1, replica_groups=mesh['par_0'=4,'par_1'=2,'par_2'=2,'freq_0'=4,'freq_1'=4] {'par_0','par_1'}, dimensions={0} | all-to-all | bytes 2150400 | tf_op jit(solution)/shard_map/all_to_all | solution.py:49
  188.6 5.6 %all_to_all.53 = bf16[2,8,14,600,8]{3,4,2,1,0:T(8,128)(2,1)S(1)} all-to-all(bf16[2,8,14,600,8]{3,4,2,1,0:T(8,128)(2,1)S(1)} %broadcast_in_dim.30), channel_id=1, replica_groups=mesh['par_0'=4,'par_1'=2,'par_2'=2,'freq_0'=4,'freq_1'=4] {'par_2'}, dimensions={0} | all-to-all | bytes 4300800 | tf_op jit(solution)/shard_map/all_to_all | solution.py:49
  194.7 2.8 copy.38
  197.5 11.0 %all-to-all-start.5 = ((bf16[64,600,28]{1,2,0:T(8,128)(2,1)}), bf16[64,600,28]{1,2,0:T(8,128)(2,1)S(1)}, u32[]{:S(2)}, u32[]{:S(2)}) async-start(bf16[64,600,28]{1,2,0:T(8,128)(2,1)} %copy.38), calls=%async_computation.5 | async-start | bytes 5242880 | tf_op jit(solution)/shard_map/all_to_all | solution.py:123
  208.5 10.1 %psum.35 = f32[]{:T(128)} all-reduce(f32[]{:T(128)} %get-tuple-element.5), channel_id=1, replica_groups=mesh['par_0'=4,'par_1'=2,'par_2'=2,'freq_0'=4,'freq_1'=4] {'par_0'}, use_global_device_ids=true, to_apply=%region_3.4 | all-reduce | flops 1 | bytes 8 | tf_op jit(solution)/shard_map/psum | solution.py:22
  218.6 34.9 %psum.36 = f32[]{:T(128)} all-reduce(f32[]{:T(128)} %psum.35), channel_id=1, replica_groups=mesh['par_0'=4,'par_1'=2,'par_2'=2,'freq_0'=4,'freq_1'=4] {'par_1'}, use_global_device_ids=true, to_apply=%region_4.5 | all-reduce | flops 1 | bytes 8 | tf_op jit(solution)/shard_map/psum | solution.py:22
  253.5 16.0 %broadcast_multiply_fusion = (f32[420,224,1]{0,2,1:T(1,128)S(1)}, f32[420,224,1]{0,2,1:T(1,128)S(1)}) fusion(f32[224]{0:T(256)S(1)} %compare_select_fusion.1, f32[224]{0:T(256)S(1)} %broadcast_multiply_fusion.4), kind=kLoop, calls=%fused_computation.31 | loop fusion | flops 1223040 | bytes 754432 | tf_op jit(solution)/shard_map/mul | solution.py:86
  269.6 3.1 psum.37
  272.7 1.8 pad_maximum_fusion.1
  274.5 12.5 %psum.38 = f32[]{:T(128)} all-reduce(f32[]{:T(128)} %psum.37), channel_id=1, replica_groups=mesh['par_0'=4,'par_1'=2,'par_2'=2,'freq_0'=4,'freq_1'=4] {'freq_0'}, use_global_device_ids=true, to_apply=%region_6.7 | all-reduce | flops 1 | bytes 8 | tf_op jit(solution)/shard_map/psum | solution.py:22
  287.0 1.8 reshape.217
  288.9 11.0 %psum.39 = f32[]{:T(128)} all-reduce(f32[]{:T(128)} %psum.38), channel_id=1, replica_groups=mesh['par_0'=4,'par_1'=2,'par_2'=2,'freq_0'=4,'freq_1'=4] {'freq_1'}, use_global_device_ids=true, to_apply=%region_7.8 | all-reduce | flops 1 | bytes 8 | tf_op jit(solution)/shard_map/psum | solution.py:22
  300.5 2.6 copy.47
  303.1 3.5 %reshape.216 = bf16[2400,448]{0,1:T(8,128)(2,1)S(1)} reshape(bf16[4,600,16,28]{1,0,3,2:T(4,128)(2,1)} %bitcast.95) | data formatting | bytes 4300800 | tf_op jit(solution)/shard_map/reshape | solution.py:124
  308.0 3.4 %convolution_add_fusion.1 = f32[2400,420]{0,1:T(8,128)} fusion(f32[2400,420]{0,1:T(8,128)S(1)} %fusion.17, bf16[2400,448]{0,1:T(8,128)(2,1)S(1)} %reshape.216, f32[420,448]{0,1:T(8,128)S(1)} %reshape.217), kind=kOutput, calls=%fused_computation.1 | convolution fusion | flops 904928640 | bytes 10967040 | tf_op jit(solution)/shard_map/dot_general | solution.py:67
  311.4 6.3 %reshape.218 = f32[4,600,420]{1,0,2:T(4,128)} reshape(f32[2400,420]{0,1:T(8,128)} %convolution_add_fusion.1) | data formatting | bytes 8064000 | tf_op jit(solution)/shard_map/reshape | solution.py:125
  317.7 4.7 %add_convert_fusion = bf16[4,600,420]{1,0,2:T(4,128)(2,1)} fusion(f32[4,600,420]{1,0,2:T(4,128)} %reshape.218, bf16[4,600,420]{1,0,2:T(4,128)(2,1)S(1)} %copy-done.1, f32[]{:T(128)S(6)} %mul_shard_map.3), kind=kLoop, calls=%fused_computation.7 | loop fusion | flops 4032000 | bytes 8064004 | tf_op jit(solution)/shard_map/convert_element_type | solution.py:126
  (40 shorter events, 13.0 us)
Async XLA Ops:
  0.0 17.8 %copy-start = (bf16[4,600,420]{1,0,2:T(4,128)(2,1)S(1)}, bf16[4,600,420]{1,0,2:T(4,128)(2,1)}, u32[]{:S(2)}) copy-start(bf16[4,600,420]{1,0,2:T(4,128)(2,1)} %param.4) | copy-start | bytes 6048004
  21.3 3.1 copy-start.2
  29.3 8.8 %copy-start.3 = (f32[256]{0:T(256)S(1)}, f32[256]{0:T(256)}, u32[]{:S(2)}) copy-start(f32[256]{0:T(256)} %param.7) | copy-start | bytes 3076
  29.3 55.2 %all-to-all-start = ((bf16[4,600,448]{1,0,2:T(4,128)(2,1)}), bf16[4,600,448]{1,0,2:T(4,128)(2,1)S(1)}, u32[]{:S(2)}, u32[]{:S(2)}) async-start(bf16[4,600,448]{1,0,2:T(4,128)(2,1)} %reshape.210), calls=%async_computation | async-start | bytes 4587520 | tf_op jit(solution)/shard_map/all_to_all | solution.py:91
  90.9 7.5 %slice-start = ((s8[4300800]{0:T(1024)(128)(4,1)}), s8[4194304]{0:T(1024)(128)(4,1)S(1)}, s32[]{:S(2)}) async-start(s8[4300800]{0:T(1024)(128)(4,1)} %bitcast.87), calls=%async_computation.6 | async-start | bytes 8388608
  94.2 4.2 %slice-start.1 = ((s8[4300800]{0:T(1024)(128)(4,1)}), s8[106496]{0:T(1024)(128)(4,1)S(1)}, s32[]{:S(2)}) async-start(s8[4300800]{0:T(1024)(128)(4,1)} %bitcast.87), calls=%async_computation.7 | async-start | bytes 212992
  97.4 2.3 slice-start.2
  98.4 1.4 slice-start.3
  197.5 103.0 %all-to-all-start.5 = ((bf16[64,600,28]{1,2,0:T(8,128)(2,1)}), bf16[64,600,28]{1,2,0:T(8,128)(2,1)S(1)}, u32[]{:S(2)}, u32[]{:S(2)}) async-start(bf16[64,600,28]{1,2,0:T(8,128)(2,1)} %copy.38), calls=%async_computation.5 | async-start | bytes 5242880 | tf_op jit(solution)/shard_map/all_to_all | solution.py:123
  311.4 6.3 %copy-start.1 = (bf16[4,600,420]{1,0,2:T(4,128)(2,1)S(1)}, bf16[4,600,420]{1,0,2:T(4,128)(2,1)}, u32[]{:S(2)}) copy-start(bf16[4,600,420]{1,0,2:T(4,128)(2,1)} %param.4) | copy-start | bytes 6048004
where the time goes:
time: 323 us; the launch traced here: 322 us
  blocking collectives  152 us (47%)
  other arithmetic  47.3 us (15%)
  waiting for transfers between devices  46.3 us (14%)
  local copies, waits for them, and re-layouts  37.9 us (12%)
  starting transfers between devices  19.8 us (6%)
  matrix products  18.3 us (6%)
    psum x5, blocking collectives, one_axis_at_a_time(): return functools.reduce(lax.psum, axes, shard)  71.7 us
    all_to_all x1, waiting for transfers between devices, shards(): lax.all_to_all(spectrum, FREQ, split_axis=2, concat_axis=0, tiled=True)  46.3 us
    all_to_all x1, blocking collectives, sum_by_axis(): lax.all_to_all(nearer.astype(jnp.bfloat16), far, split_axis=0, concat_axi...  39.4 us
    all_to_all x2, blocking collectives, sent_to_all(): return lax.all_to_all(copies, axis, split_axis=0, concat_axis=0, tiled=True)  35.1 us
    mul x1, other arithmetic, shards(): -sines * all_weight[None, :]  16 us
    neg x1, other arithmetic, shards(): -sines  15.6 us
    all_to_all x1, starting transfers between devices, shards(): lax.all_to_all(outgoing, FREQ, split_axis=0, concat_axis=2, tiled=True)  11 us
    all_to_all x1, starting transfers between devices, shards(): lax.all_to_all(spectrum, FREQ, split_axis=2, concat_axis=0, tiled=True)  8.77 us
  transfers between devices with their start and end apart: 2, of which 1 were waited for; matrix products, arithmetic and copies ran while one was open for 6% of the time, Pallas kernels for 0%

commit v1 on v0

v1 whole, which is shorter than its diff:
```python
import functools

import jax
import jax.numpy as jnp
import numpy as np
from jax import lax
from jax.experimental import pallas as pl
from jax.experimental.pallas import tpu as pltpu
from jax.sharding import Mesh
from jax.sharding import PartitionSpec as P

SENSORS = 600
STEPS = 420
PERIOD = 840
PROBES = 64
BINS = 224
FREQ = ("zl", "y")
PAR = ("x", "h", "c")
BLOCKS = 16
BIN_DEV = BINS // BLOCKS
BIN_PAD = 16
ROWS = BLOCKS * BIN_PAD
XS = 4
NOISE = 0.5
TRACE_ROW = BIN_DEV
HALF = 208
SPAN = 216
UNROLL = 7

f32 = jnp.float32
bf16 = jnp.bfloat16
VMEM = pl.BlockSpec(memory_space=pltpu.VMEM)


def two_parts(values):
    values = values.astype(np.float32)
    upper = values.astype(bf16)
    return upper, (values - upper.astype(np.float32)).astype(bf16)


def tables():
    bins = np.arange(BINS)
    turn = (np.arange(STEPS)[:, None] * bins[None, :]) % PERIOD
    angle = turn * (2.0 * np.pi / PERIOD)
    both = np.stack([np.cos(angle), -np.sin(angle)]) / np.sqrt(float(PERIOD))
    both = both * np.where(bins == 0, 1.0, 2.0)
    both = both.reshape(2, STEPS, BLOCKS, BIN_DEV)
    both = np.pad(both, ((0, 0), (0, HALF + SPAN - STEPS), (0, 0), (0, BIN_PAD - BIN_DEV)))
    return np.stack(two_parts(both.reshape(2, HALF + SPAN, ROWS)), axis=1)


def dft_kernel(table, probes, out):
    probe = probes[lax.axis_index("x")]
    c = lax.axis_index("c")
    tn = (((0,), (0,)), ((), ()))
    d = sum(
        lax.dot_general(table[c, piece, :STEPS], probe, tn, preferred_element_type=f32)
        for piece in range(2)
    )
    row = lax.broadcasted_iota(jnp.int32, (ROWS, 1), 0)
    out[...] = (d * jnp.where(row == 0, 1.0, 0.5)).astype(bf16)


def middle_kernel(*refs):
    own, oth = refs[:XS], refs[XS : 2 * XS]
    map_real, map_imag, prior = refs[2 * XS : 2 * XS + 3]
    outs = refs[2 * XS + 3 :]
    w_own, w_oth, trace, scaled = outs[:XS], outs[XS : 2 * XS], outs[2 * XS], outs[2 * XS + 1]
    sigma = jnp.where(lax.axis_index("c") == 0, 1.0, -1.0).astype(f32)
    first = lax.axis_index(FREQ) == 0
    half = XS * BLOCKS
    nt = (((1,), (1,)), ((), ()))
    p = prior[...]

    def left(k):
        weight = jnp.where(first & (k == 0), 1.0, 2.0).astype(f32)
        v = jnp.concatenate([r[k] for r in own] + [r[k] for r in oth], axis=0)
        ar = jnp.dot(v, map_real[k], preferred_element_type=f32)
        ai = jnp.dot(v, map_imag[k], preferred_element_type=f32)
        u_own = ar[:half] + sigma * ai[half:]
        u_oth = ar[half:] - sigma * ai[:half]
        scaled[k, :half] = (u_own * p).astype(bf16)
        scaled[k, half:] = (u_oth * p).astype(bf16)
        return weight * p * jnp.sum(u_own * u_own + u_oth * u_oth, axis=0, keepdims=True)

    def right(k):
        a = scaled[k]
        br = lax.dot_general(a, map_real[k], nt, preferred_element_type=f32)
        bi = lax.dot_general(a, map_imag[k], nt, preferred_element_type=f32)
        to_own = (br[:half] - sigma * bi[half:]).astype(bf16)
        to_oth = (br[half:] + sigma * bi[:half]).astype(bf16)
        for j in range(XS):
            rows = slice(j * BLOCKS, (j + 1) * BLOCKS)
            w_own[j][k] = to_own[rows]
            w_oth[j][k] = to_oth[rows]

    def lefts(i, total):
        return total + sum(left(UNROLL * i + n) for n in range(UNROLL))

    def rights(i, _):
        for n in range(UNROLL):
            right(UNROLL * i + n)
        return 0

    trace[...] = lax.fori_loop(0, BIN_DEV // UNROLL, lefts, jnp.zeros(p.shape, f32))
    lax.fori_loop(0, BIN_DEV // UNROLL, rights, 0)


def trace_line(total):
    lane = lax.broadcasted_iota(jnp.int32, (1, SENSORS), 1)
    whole = jnp.full((1, SENSORS), total, f32)
    upper = whole.astype(bf16).astype(f32)
    return jnp.where(lane == 0, upper, jnp.where(lane == 1, whole - upper, 0.0)).astype(bf16)


def read_trace(ref, row):
    line = ref[row : row + 1, 0:2].astype(f32)
    return line[0, 0] + line[0, 1]


def inverse_kernel(table, own, oth, out):
    c = lax.axis_index("c")
    row = lax.broadcasted_iota(jnp.int32, (ROWS, 128), 0)
    lane = lax.broadcasted_iota(jnp.int32, (ROWS, 128), 1)
    marked = (row % BIN_PAD == TRACE_ROW) & (lane < 2)
    span = pl.ds(pl.multiple_of(c * HALF, 16), SPAN)
    total = jnp.zeros((), f32)
    r = jnp.zeros((SPAN, SENSORS), f32)
    for ref, part in ((own, c), (oth, 1 - c)):
        v = ref[0].astype(f32) + ref[1].astype(f32)
        total = total + jnp.sum(jnp.where(marked, v[:, :128], 0.0))
        v = v.astype(bf16)
        for piece in range(2):
            r = r + jnp.dot(table[part, piece, span], v, preferred_element_type=f32)
    out[...] = r.astype(bf16)
    out[SPAN - 1 : SPAN, :] = trace_line(total)


def finish_kernel(*refs):
    own, oth = refs[:XS], refs[XS : 2 * XS]
    probes, out = refs[2 * XS :]
    x, c = lax.axis_index("x"), lax.axis_index("c")
    total = sum(read_trace(r, SPAN - 1) for r in own)
    trace = total * (NOISE / (PROBES * SENSORS * STEPS))
    for j in range(XS):
        p = lax.rem(x + j, XS)
        for ref, half in ((own[j], c), (oth[j], 1 - c)):
            rows = pl.ds(pl.multiple_of(half * HALF, 16), HALF)
            out[p, rows, :] = (ref[0:HALF].astype(f32) + trace * probes[p, rows, :].astype(f32)).astype(bf16)
        rest = STEPS - 2 * HALF
        last = jnp.where(c == 1, own[j][HALF : HALF + rest].astype(f32), oth[j][HALF : HALF + rest].astype(f32))
        out[p, 2 * HALF :, :] = (last + trace * probes[p, 2 * HALF :, :].astype(f32)).astype(bf16)


def shift(value, axis, by):
    n = lax.axis_size(axis)
    return lax.ppermute(value, axis, [(i, (i + by) % n) for i in range(n)])


def swap_core(value):
    return lax.ppermute(value, "c", [(0, 1), (1, 0)])


def call(kernel, name, operands, outs, limit, scratch=()):
    return pl.pallas_call(
        kernel,
        in_specs=[VMEM] * len(operands),
        out_specs=[VMEM] * len(outs),
        out_shape=[jax.ShapeDtypeStruct(*o) for o in outs],
        scratch_shapes=list(scratch),
        name=name,
        compiler_params=pltpu.CompilerParams(vmem_limit_bytes=limit << 20),
    )(*operands)


def shards(probes, map_real, map_imag, prior_var):
    table = jnp.asarray(tables())
    by_time, probes = lax.optimization_barrier((probes.transpose(0, 2, 1), probes))
    (spectra,) = call(dft_kernel, "dft", (table, by_time), [((ROWS, SENSORS), bf16)], 4)
    arrived = lax.all_to_all(spectra.reshape(BLOCKS, BIN_PAD, SENSORS), FREQ, 0, 0, tiled=True)
    arrived = arrived.transpose(1, 0, 2)[:BIN_DEV]
    away = {j: shift(arrived, "x", -j) for j in (2, 1, 3)}
    own = [arrived] + [away[j] for j in range(1, XS)]
    other = [swap_core(v) for v in own]

    prior = prior_var[None, :]
    block = ((BIN_DEV, BLOCKS, SENSORS), bf16)
    *w, trace = call(
        middle_kernel,
        "middle",
        [*own, *other, map_real, map_imag, prior],
        [block] * (2 * XS) + [(prior.shape, f32)],
        4,
        [pltpu.VMEM((BIN_DEV, 2 * XS * BLOCKS, prior.shape[1]), bf16)],
    )
    both = {j: (w[j].astype(f32) + swap_core(w[XS + j]).astype(f32)).astype(bf16) for j in (2, 1, 3, 0)}
    total = both[0].astype(f32)
    for j in (2, 1, 3):
        total = total + shift(both[j], "x", j).astype(f32)
    total = total.astype(bf16).transpose(1, 0, 2)
    quad = jnp.sum(trace)
    quad_up = quad.astype(bf16)
    quad_low = (quad - quad_up.astype(f32)).astype(bf16)
    lane = jnp.arange(SENSORS)
    line = jnp.where(lane == 0, quad_up, jnp.where(lane == 1, quad_low, jnp.zeros((), bf16)))
    extra = jnp.where(
        jnp.arange(BIN_PAD - BIN_DEV)[None, :, None] == 0, line[None, None, :], jnp.zeros((), bf16)
    )
    extra = jnp.broadcast_to(extra, (BLOCKS, BIN_PAD - BIN_DEV, SENSORS))
    outgoing = jnp.concatenate([total, extra], axis=1)
    outgoing = jnp.broadcast_to(outgoing[None], (2, BLOCKS, BIN_PAD, SENSORS))
    outgoing = outgoing.reshape(2 * BLOCKS, BIN_PAD, SENSORS)
    arrived = lax.all_to_all(outgoing, ("h",) + FREQ, 0, 0, tiled=True)
    pieces = [v.reshape(2, ROWS, SENSORS) for v in (arrived, swap_core(arrived))]
    (part,) = call(inverse_kernel, "inverse", (table, *pieces), [((SPAN, SENSORS), bf16)], 4)
    away = {j: shift(part, "x", -j) for j in (2, 1, 3)}
    own = [part] + [away[j] for j in range(1, XS)]
    other = [swap_core(v) for v in own]
    (out,) = call(finish_kernel, "finish", (*own, *other, probes.transpose(0, 2, 1)), [((XS, STEPS, SENSORS), bf16)], 4)
    return out.transpose(0, 2, 1)


def solution(mesh):
    torus = Mesh(mesh.devices.reshape(4, 2, 2, 4, 4), ("x", "h", "c", "zl", "y"))
    in_specs = (P(FREQ, None, None), P(FREQ, None, PAR), P(FREQ, None, PAR), P(PAR))
    return jax.shard_map(
        shards, mesh=torus, in_specs=in_specs, out_specs=P(FREQ, None, None), check_vma=False
    )
```

time: 323 us -> 120 us (0.37)
  blocking collectives: 152 us -> 47.7 us
  other arithmetic: 47.3 us -> 2.14 us
  local copies, waits for them, and re-layouts: 37.9 us -> 4.7 us
  matrix products: 18.3 us -> 0 us
  Pallas kernels: 0 us -> 7.5 us
  waiting for transfers between devices: 46.3 us -> 39.5 us
  starting transfers between devices: 19.8 us -> 14.8 us
    psum x5 -> x0, blocking collectives: 71.7 us -> none  [one_axis_at_a_time(): return functools.reduce(lax.psum, axes, shard)]
    all_to_all x2 -> x0, waiting for transfers between devices: 46.3 us -> none  [the longest x1 46.3 us: shards(): lax.all_to_all(spectrum, FREQ, split_axis=2, concat_axis=0, tiled=True)]
    ppermute x0 -> x22, waiting for transfers between devices: none -> 39.5 us  [the longest x9 34.6 us: shift(): return lax.ppermute(value, axis, [(i, (i + by) % n) for i in range(n)])]
    all_to_all x4 -> x2, blocking collectives: 80.1 us -> 47.7 us  [the longest x1 27.3 us: shards(): arrived = lax.all_to_all(outgoing, ('h',) + FREQ, 0, 0, tiled=True)]
    reshape x7 -> x0, local copies, waits for them, and re-layouts: 25 us -> none  [the longest x1 6.3 us: shards(): split_product(by_rows, inverse).reshape(probe_block, SENSORS, STEPS)]
    all_to_all x2 -> x0, starting transfers between devices: 19.8 us -> none  [the longest x1 11 us: shards(): lax.all_to_all(outgoing, FREQ, split_axis=0, concat_axis=2, tiled=True)]
    dot_general x8 -> x0, matrix products: 18.3 us -> none  [the longest x2 4.73 us: split_product(): jnp.dot(left, lower, preferred_element_type=jnp.float32)]
    mul x3 -> x0, other arithmetic: 16.1 us -> none  [the longest x1 16 us: shards(): -sines * all_weight[None, :]]
  transfers between devices with their start and end apart: 2 -> 22, of which waited for: 1 -> 12; matrix products, arithmetic and copies ran while one was open for 6% -> 2% of each run, Pallas kernels for 0% -> 0%
where the time goes in v1:
time: 120 us; the launch traced here: 118 us
  blocking collectives  47.7 us (40%)
  waiting for transfers between devices  39.5 us (33%)
  starting transfers between devices  14.8 us (12%)
  Pallas kernels  7.5 us (6%)
  local copies, waits for them, and re-layouts  4.7 us (4%)
  other arithmetic  2.14 us (2%)
  between operations  1.48 us (1%)
    ppermute x9, waiting for transfers between devices, shift(): return lax.ppermute(value, axis, [(i, (i + by) % n) for i in range(n)])  34.6 us
    all_to_all x1, blocking collectives, shards(): arrived = lax.all_to_all(outgoing, ('h',) + FREQ, 0, 0, tiled=True)  27.3 us
    all_to_all x1, blocking collectives, shards(): lax.all_to_all(spectra.reshape(BLOCKS, BIN_PAD, SENSORS), FREQ, 0, 0, til...  20.4 us
    ppermute x9, starting transfers between devices, shift(): return lax.ppermute(value, axis, [(i, (i + by) % n) for i in range(n)])  13.6 us
    pallas_call x4, Pallas kernels, call(): pl.pallas_call(kernel, in_specs=[VMEM] * len(operands), out_specs=[VMEM]...  7.5 us
    ppermute x13, waiting for transfers between devices, swap_core(): return lax.ppermute(value, 'c', [(0, 1), (1, 0)])  4.9 us
  transfers between devices with their start and end apart: 22, of which 12 were waited for; matrix products, arithmetic and copies ran while one was open for 2% of the time, Pallas kernels for 0%

profile of v1, /device:TPU:2, one launch (start us, length us, event | category | flops | bytes accessed | tf_op | source)
XLA Modules:
  0.0 117.8 jit_solution(13172929957819676092)
XLA Ops:
  0.0 2.0 %copy.24 = bf16[4,600,420]{1,2,0:T(8,128)(2,1)S(1)} copy(bf16[4,600,420]{1,0,2:T(4,128)(2,1)} %param.5) | data formatting | bytes 4032000 | tf_op args[0]
  2.1 0.6 dft.1
  2.7 20.4 %all_to_all.10 = bf16[16,16,600]{2,1,0:T(8,128)(2,1)S(1)} all-to-all(bf16[16,16,600]{2,1,0:T(8,128)(2,1)S(1)} %bitcast.21), channel_id=1, replica_groups=mesh['x'=4,'h'=2,'c'=2,'zl'=4,'y'=4] {'zl','y'}, dimensions={0} | all-to-all | bytes 614400 | tf_op jit(solution)/shard_map/all_to_all | solution.py:180
  23.2 1.6 %collective-permute-start.2 = (bf16[14,16,600]{2,1,0:T(8,128)(2,1)S(1)}, bf16[14,16,600]{2,1,0:T(8,128)(2,1)S(1)}, u32[]{:S(2)}, u32[]{:S(2)}) collective-permute-start(bf16[14,16,600]{2,1,0:T(8,128)(2,1)S(1)} %slice.4.refs_0_), channel_id=1, source_target_pairs={{0,64},{64,128},{128,192},{192,0},{1,65},{65,129},{129,193},{193,1... | collective-permute-start | bytes 806408 | tf_op jit(solution)/shard_map/ppermute | solution.py:157
  24.8 1.1 collective-permute-start.1
  25.9 2.2 %collective-permute-start = (bf16[14,16,600]{2,1,0:T(8,128)(2,1)S(1)}, bf16[14,16,600]{2,1,0:T(8,128)(2,1)S(1)}, u32[]{:S(2)}, u32[]{:S(2)}) collective-permute-start(bf16[14,16,600]{2,1,0:T(8,128)(2,1)S(1)} %slice.4.refs_0_), channel_id=1, source_target_pairs={{0,192},{64,0},{128,64},{192,128},{1,193},{65,1},{129,65},{193,129... | collective-permute-start | bytes 806408 | tf_op jit(solution)/shard_map/ppermute | solution.py:157
  28.0 4.9 %collective-permute-done.2.refs_3_ = bf16[14,16,600]{2,1,0:T(8,128)(2,1)S(1)} collective-permute-done((bf16[14,16,600]{2,1,0:T(8,128)(2,1)S(1)}, bf16[14,16,600]{2,1,0:T(8,128)(2,1)S(1)}, u32[]{:S(2)}, u32[]{:S(2)}) %collective-permute-start.2) | collective-permute-done | bytes 268832 | tf_op jit(solution)/shard_map/ppermute | solution.py:157
  33.0 3.0 %collective-permute-done.1.refs_2_ = bf16[14,16,600]{2,1,0:T(8,128)(2,1)S(1)} collective-permute-done((bf16[14,16,600]{2,1,0:T(8,128)(2,1)S(1)}, bf16[14,16,600]{2,1,0:T(8,128)(2,1)S(1)}, u32[]{:S(2)}, u32[]{:S(2)}) %collective-permute-start.1) | collective-permute-done | bytes 268832 | tf_op jit(solution)/shard_map/ppermute | solution.py:157
  36.0 2.6 %collective-permute-done.refs_1_ = bf16[14,16,600]{2,1,0:T(8,128)(2,1)S(1)} collective-permute-done((bf16[14,16,600]{2,1,0:T(8,128)(2,1)S(1)}, bf16[14,16,600]{2,1,0:T(8,128)(2,1)S(1)}, u32[]{:S(2)}, u32[]{:S(2)}) %collective-permute-start) | collective-permute-done | bytes 268832 | tf_op jit(solution)/shard_map/ppermute | solution.py:157
  38.6 1.5 %collective-permute-done.4.refs_5_ = bf16[14,16,600]{2,1,0:T(8,128)(2,1)S(1)} collective-permute-done((bf16[14,16,600]{2,1,0:T(8,128)(2,1)S(1)}, bf16[14,16,600]{2,1,0:T(8,128)(2,1)S(1)}, u32[]{:S(2)}, u32[]{:S(2)}) %collective-permute-start.4) | collective-permute-done | bytes 268832 | tf_op jit(solution)/shard_map/ppermute | solution.py:161
  40.2 5.0 %middle.1 = (bf16[14,16,600]{2,1,0:T(8,128)(2,1)S(1)}, bf16[14,16,600]{2,1,0:T(8,128)(2,1)S(1)}, bf16[14,16,600]{2,1,0:T(8,128)(2,1)S(1)}, bf16[14,16,600]{2,1,0...) custom-call(bf16[14,16,600]{2,1,0:T(8,128)(2,1)S(1)} %slice.4.refs_0, ...), custom_call_target="tpu_custom_call" | custom-call | tf_op jit(solution)/shard_map/middle/pallas_call | solution.py:165
  45.4 0.4 collective-permute-start.10
  45.8 0.6 reduce_sum.9
  47.9 0.4 collective-permute-start.12
  48.3 1.0 add_convert_fusion.3
  49.3 1.9 %collective-permute-start.9 = (bf16[14,16,600]{2,1,0:T(8,128)(2,1)S(1)}, bf16[14,16,600]{2,1,0:T(8,128)(2,1)S(1)}, u32[]{:S(2)}, u32[]{:S(2)}) collective-permute-start(bf16[14,16,600]{2,1,0:T(8,128)(2,1)S(1)} %add_convert_fusion.3), channel_id=1, source_target_pairs={{0,128},{64,192},{128,0},{192,64},{1,129},{65,193},{129,1},{193,65... | collective-permute-start | bytes 806408 | tf_op jit(solution)/shard_map/ppermute | solution.py:157
  51.3 0.9 collective-permute-start.11
  52.2 1.5 %collective-permute-start.13 = (bf16[14,16,600]{2,1,0:T(8,128)(2,1)S(1)}, bf16[14,16,600]{2,1,0:T(8,128)(2,1)S(1)}, u32[]{:S(2)}, u32[]{:S(2)}) collective-permute-start(bf16[14,16,600]{2,1,0:T(8,128)(2,1)S(1)} %add_convert_fusion.1), channel_id=1, source_target_pairs={{0,192},{64,0},{128,64},{192,128},{1,193},{65,1},{129,65},{193,129... | collective-permute-start | bytes 806408 | tf_op jit(solution)/shard_map/ppermute | solution.py:157
  53.8 6.8 %collective-permute-done.9 = bf16[14,16,600]{2,1,0:T(8,128)(2,1)S(1)} collective-permute-done((bf16[14,16,600]{2,1,0:T(8,128)(2,1)S(1)}, bf16[14,16,600]{2,1,0:T(8,128)(2,1)S(1)}, u32[]{:S(2)}, u32[]{:S(2)}) %collective-permute-start.9) | collective-permute-done | bytes 268832 | tf_op jit(solution)/shard_map/ppermute | solution.py:157
  60.7 5.1 %collective-permute-done.11 = bf16[14,16,600]{2,1,0:T(8,128)(2,1)S(1)} collective-permute-done((bf16[14,16,600]{2,1,0:T(8,128)(2,1)S(1)}, bf16[14,16,600]{2,1,0:T(8,128)(2,1)S(1)}, u32[]{:S(2)}, u32[]{:S(2)}) %collective-permute-start.11) | collective-permute-done | bytes 268832 | tf_op jit(solution)/shard_map/ppermute | solution.py:157
  66.4 27.3 %all_to_all.11 = bf16[32,16,600]{2,1,0:T(8,128)(2,1)S(1)} all-to-all(bf16[32,16,600]{2,1,0:T(8,128)(2,1)S(1)} %bitcast.24), channel_id=1, replica_groups=mesh['x'=4,'h'=2,'c'=2,'zl'=4,'y'=4] {'h','zl','y'}, dimensions={0} | all-to-all | bytes 1228800 | tf_op jit(solution)/shard_map/all_to_all | solution.py:213
  93.6 2.1 %collective-permute-done.14 = bf16[32,16,600]{2,1,0:T(8,128)(2,1)S(1)} collective-permute-done((bf16[32,16,600]{2,1,0:T(8,128)(2,1)S(1)}, bf16[32,16,600]{2,1,0:T(8,128)(2,1)S(1)}, u32[]{:S(2)}, u32[]{:S(2)}) %collective-permute-start.14) | collective-permute-done | bytes 614432 | tf_op jit(solution)/shard_map/ppermute | solution.py:161
  95.7 0.6 inverse.1.refs_0_
  96.3 0.7 collective-permute-start.17
  97.0 2.6 %collective-permute-start.16 = (bf16[216,600]{1,0:T(8,128)(2,1)S(1)}, bf16[216,600]{1,0:T(8,128)(2,1)S(1)}, u32[]{:S(2)}, u32[]{:S(2)}) collective-permute-start(bf16[216,600]{1,0:T(8,128)(2,1)S(1)} %inverse.1.refs_0_), channel_id=1, source_target_pairs={{0,128},{64,192},{128,0},{192,64},{1,129},{65,193},{129,1},{193,65... | collective-permute-start | bytes 777608 | tf_op jit(solution)/shard_map/ppermute | solution.py:157
  99.5 1.3 %collective-permute-start.15 = (bf16[216,600]{1,0:T(8,128)(2,1)S(1)}, bf16[216,600]{1,0:T(8,128)(2,1)S(1)}, u32[]{:S(2)}, u32[]{:S(2)}) collective-permute-start(bf16[216,600]{1,0:T(8,128)(2,1)S(1)} %inverse.1.refs_0_), channel_id=1, source_target_pairs={{0,192},{64,0},{128,64},{192,128},{1,193},{65,1},{129,65},{193,129... | collective-permute-start | bytes 777608 | tf_op jit(solution)/shard_map/ppermute | solution.py:157
  100.8 5.1 %collective-permute-done.17.refs_3_ = bf16[216,600]{1,0:T(8,128)(2,1)S(1)} collective-permute-done((bf16[216,600]{1,0:T(8,128)(2,1)S(1)}, bf16[216,600]{1,0:T(8,128)(2,1)S(1)}, u32[]{:S(2)}, u32[]{:S(2)}) %collective-permute-start.17) | collective-permute-done | bytes 259232 | tf_op jit(solution)/shard_map/ppermute | solution.py:157
  105.9 2.1 %collective-permute-done.16.refs_2_ = bf16[216,600]{1,0:T(8,128)(2,1)S(1)} collective-permute-done((bf16[216,600]{1,0:T(8,128)(2,1)S(1)}, bf16[216,600]{1,0:T(8,128)(2,1)S(1)}, u32[]{:S(2)}, u32[]{:S(2)}) %collective-permute-start.16) | collective-permute-done | bytes 259232 | tf_op jit(solution)/shard_map/ppermute | solution.py:157
  108.0 4.8 %collective-permute-done.15.refs_1_ = bf16[216,600]{1,0:T(8,128)(2,1)S(1)} collective-permute-done((bf16[216,600]{1,0:T(8,128)(2,1)S(1)}, bf16[216,600]{1,0:T(8,128)(2,1)S(1)}, u32[]{:S(2)}, u32[]{:S(2)}) %collective-permute-start.15) | collective-permute-done | bytes 259232 | tf_op jit(solution)/shard_map/ppermute | solution.py:157
  113.1 1.2 %collective-permute-done.19.refs_5_ = bf16[216,600]{1,0:T(8,128)(2,1)S(1)} collective-permute-done((bf16[216,600]{1,0:T(8,128)(2,1)S(1)}, bf16[216,600]{1,0:T(8,128)(2,1)S(1)}, u32[]{:S(2)}, u32[]{:S(2)}) %collective-permute-start.19) | collective-permute-done | bytes 259232 | tf_op jit(solution)/shard_map/ppermute | solution.py:161
  114.3 1.3 %finish.1 = bf16[4,420,600]{2,1,0:T(8,128)(2,1)S(1)} custom-call(bf16[216,600]{1,0:T(8,128)(2,1)S(1)} %inverse.1.refs_0_, bf16[216,600]{1,0:T(8,128)(2,1)S(1)} %collective-permute-done.15.refs_1_, bf16[216,600]{1,0:T(8,128)(2,1)S(1)} %collective-permute-done.16.refs_2_, bf16[216,600]{1,0:T(8,128)(2,1)S(1)} %collective-permute-done.17.refs_3_, ...), custom_call_target="tpu_custom_call" | custom-call | tf_op jit(solution)/shard_map/finish/pallas_call | solution.py:165
  115.6 2.2 %copy.19 = bf16[4,600,420]{1,0,2:T(4,128)(2,1)} copy(bf16[4,600,420]{1,2,0:T(8,128)(2,1)S(1)} %bitcast.18) | data formatting | bytes 4032000 | tf_op jit(solution)/shard_map/transpose | solution.py:220
  (45 shorter events, 1.6 us)
Async XLA Ops:
  0.0 2.0 %copy-start.2 = (bf16[2,2,424,256]{3,2,1,0:T(8,128)(2,1)S(1)}, bf16[2,2,424,256]{3,2,1,0:T(8,128)(2,1)}, u32[]{:S(2)}) copy-start(bf16[2,2,424,256]{3,2,1,0:T(8,128)(2,1)} %constant.4.clone.table) | copy-start | bytes 2605060
  0.0 40.2 %copy-start.1 = (bf16[14,600,256]{2,1,0:T(8,128)(2,1)S(1)}, bf16[14,600,256]{2,1,0:T(8,128)(2,1)}, u32[]{:S(2)}) copy-start(bf16[14,600,256]{2,1,0:T(8,128)(2,1)} %refs_9_.1) | copy-start | bytes 12902404
  2.0 38.1 %copy-start = (bf16[14,600,256]{2,1,0:T(8,128)(2,1)S(1)}, bf16[14,600,256]{2,1,0:T(8,128)(2,1)}, u32[]{:S(2)}) copy-start(bf16[14,600,256]{2,1,0:T(8,128)(2,1)} %refs_8_.1) | copy-start | bytes 12902404
  2.1 38.1 %copy-start.3 = (f32[256]{0:T(256)S(1)}, f32[256]{0:T(256)}, u32[]{:S(2)}) copy-start(f32[256]{0:T(256)} %param.8) | copy-start | bytes 3076
  23.2 9.8 %collective-permute-start.2 = (bf16[14,16,600]{2,1,0:T(8,128)(2,1)S(1)}, bf16[14,16,600]{2,1,0:T(8,128)(2,1)S(1)}, u32[]{:S(2)}, u32[]{:S(2)}) collective-permute-start(bf16[14,16,600]{2,1,0:T(8,128)(2,1)S(1)} %slice.4.refs_0_), channel_id=1, source_target_pairs={{0,64},{64,128},{128,192},{192,0},{1,65},{65,129},{129,193},{193,1... | collective-permute-start | bytes 806408 | tf_op jit(solution)/shard_map/ppermute | solution.py:157
  24.8 11.2 %collective-permute-start.1 = (bf16[14,16,600]{2,1,0:T(8,128)(2,1)S(1)}, bf16[14,16,600]{2,1,0:T(8,128)(2,1)S(1)}, u32[]{:S(2)}, u32[]{:S(2)}) collective-permute-start(bf16[14,16,600]{2,1,0:T(8,128)(2,1)S(1)} %slice.4.refs_0_), channel_id=1, source_target_pairs={{0,128},{64,192},{128,0},{192,64},{1,129},{65,193},{129,1},{193,65... | collective-permute-start | bytes 806408 | tf_op jit(solution)/shard_map/ppermute | solution.py:157
  25.9 12.7 %collective-permute-start = (bf16[14,16,600]{2,1,0:T(8,128)(2,1)S(1)}, bf16[14,16,600]{2,1,0:T(8,128)(2,1)S(1)}, u32[]{:S(2)}, u32[]{:S(2)}) collective-permute-start(bf16[14,16,600]{2,1,0:T(8,128)(2,1)S(1)} %slice.4.refs_0_), channel_id=1, source_target_pairs={{0,192},{64,0},{128,64},{192,128},{1,193},{65,1},{129,65},{193,129... | collective-permute-start | bytes 806408 | tf_op jit(solution)/shard_map/ppermute | solution.py:157
  28.0 10.6 %collective-permute-start.3 = (bf16[14,16,600]{2,1,0:T(8,128)(2,1)S(1)}, bf16[14,16,600]{2,1,0:T(8,128)(2,1)S(1)}, u32[]{:S(2)}, u32[]{:S(2)}) collective-permute-start(bf16[14,16,600]{2,1,0:T(8,128)(2,1)S(1)} %slice.4.refs_0_), channel_id=1, source_target_pairs={{0,16},{16,0},{1,17},{17,1},{2,18},{18,2},{3,19},{19,3},{4,20},{20... | collective-permute-start | bytes 806408 | tf_op jit(solution)/shard_map/ppermute | solution.py:161
  33.0 5.6 %collective-permute-start.6 = (bf16[14,16,600]{2,1,0:T(8,128)(2,1)S(1)}, bf16[14,16,600]{2,1,0:T(8,128)(2,1)S(1)}, u32[]{:S(2)}, u32[]{:S(2)}) collective-permute-start(bf16[14,16,600]{2,1,0:T(8,128)(2,1)S(1)} %collective-permute-done.2.refs_3_), channel_id=1, source_target_pairs={{0,16},{16,0},{1,17},{17,1},{2,18},{18,2},{3,19},{19,3},{4,20},{20... | collective-permute-start | bytes 806408 | tf_op jit(solution)/shard_map/ppermute | solution.py:161
  36.0 2.6 %collective-permute-start.5 = (bf16[14,16,600]{2,1,0:T(8,128)(2,1)S(1)}, bf16[14,16,600]{2,1,0:T(8,128)(2,1)S(1)}, u32[]{:S(2)}, u32[]{:S(2)}) collective-permute-start(bf16[14,16,600]{2,1,0:T(8,128)(2,1)S(1)} %collective-permute-done.1.refs_2_), channel_id=1, source_target_pairs={{0,16},{16,0},{1,17},{17,1},{2,18},{18,2},{3,19},{19,3},{4,20},{20... | collective-permute-start | bytes 806408 | tf_op jit(solution)/shard_map/ppermute | solution.py:161
  38.6 1.6 %collective-permute-start.4 = (bf16[14,16,600]{2,1,0:T(8,128)(2,1)S(1)}, bf16[14,16,600]{2,1,0:T(8,128)(2,1)S(1)}, u32[]{:S(2)}, u32[]{:S(2)}) collective-permute-start(bf16[14,16,600]{2,1,0:T(8,128)(2,1)S(1)} %collective-permute-done.refs_1_), channel_id=1, source_target_pairs={{0,16},{16,0},{1,17},{17,1},{2,18},{18,2},{3,19},{19,3},{4,20},{20... | collective-permute-start | bytes 806408 | tf_op jit(solution)/shard_map/ppermute | solution.py:161
  45.2 3.1 %collective-permute-start.8 = (bf16[14,16,600]{2,1,0:T(8,128)(2,1)S(1)}, bf16[14,16,600]{2,1,0:T(8,128)(2,1)}, u32[]{:S(2)}, u32[]{:S(2)}) collective-permute-start(bf16[14,16,600]{2,1,0:T(8,128)(2,1)S(1)} %get-tuple-element.20), channel_id=1, source_target_pairs={{0,16},{16,0},{1,17},{17,1},{2,18},{18,2},{3,19},{19,3},{4,20},{20... | collective-permute-start | bytes 806408 | tf_op jit(solution)/shard_map/ppermute | solution.py:161
  45.4 5.8 %collective-permute-start.10 = (bf16[14,16,600]{2,1,0:T(8,128)(2,1)S(1)}, bf16[14,16,600]{2,1,0:T(8,128)(2,1)S(1)}, u32[]{:S(2)}, u32[]{:S(2)}) collective-permute-start(bf16[14,16,600]{2,1,0:T(8,128)(2,1)S(1)} %get-tuple-element.22), channel_id=1, source_target_pairs={{0,16},{16,0},{1,17},{17,1},{2,18},{18,2},{3,19},{19,3},{4,20},{20... | collective-permute-start | bytes 806408 | tf_op jit(solution)/shard_map/ppermute | solution.py:161
  47.7 6.1 %collective-permute-start.7 = (bf16[14,16,600]{2,1,0:T(8,128)(2,1)S(1)}, bf16[14,16,600]{2,1,0:T(8,128)(2,1)S(1)}, u32[]{:S(2)}, u32[]{:S(2)}) collective-permute-start(bf16[14,16,600]{2,1,0:T(8,128)(2,1)S(1)} %get-tuple-element.18), channel_id=1, source_target_pairs={{0,16},{16,0},{1,17},{17,1},{2,18},{18,2},{3,19},{19,3},{4,20},{20... | collective-permute-start | bytes 806408 | tf_op jit(solution)/shard_map/ppermute | solution.py:161
  47.9 4.3 %collective-permute-start.12 = (bf16[14,16,600]{2,1,0:T(8,128)(2,1)S(1)}, bf16[14,16,600]{2,1,0:T(8,128)(2,1)S(1)}, u32[]{:S(2)}, u32[]{:S(2)}) collective-permute-start(bf16[14,16,600]{2,1,0:T(8,128)(2,1)S(1)} %get-tuple-element.24), channel_id=1, source_target_pairs={{0,16},{16,0},{1,17},{17,1},{2,18},{18,2},{3,19},{19,3},{4,20},{20... | collective-permute-start | bytes 806408 | tf_op jit(solution)/shard_map/ppermute | solution.py:161
  49.3 11.3 %collective-permute-start.9 = (bf16[14,16,600]{2,1,0:T(8,128)(2,1)S(1)}, bf16[14,16,600]{2,1,0:T(8,128)(2,1)S(1)}, u32[]{:S(2)}, u32[]{:S(2)}) collective-permute-start(bf16[14,16,600]{2,1,0:T(8,128)(2,1)S(1)} %add_convert_fusion.3), channel_id=1, source_target_pairs={{0,128},{64,192},{128,0},{192,64},{1,129},{65,193},{129,1},{193,65... | collective-permute-start | bytes 806408 | tf_op jit(solution)/shard_map/ppermute | solution.py:157
  51.3 14.5 %collective-permute-start.11 = (bf16[14,16,600]{2,1,0:T(8,128)(2,1)S(1)}, bf16[14,16,600]{2,1,0:T(8,128)(2,1)S(1)}, u32[]{:S(2)}, u32[]{:S(2)}) collective-permute-start(bf16[14,16,600]{2,1,0:T(8,128)(2,1)S(1)} %add_convert_fusion.2), channel_id=1, source_target_pairs={{0,64},{64,128},{128,192},{192,0},{1,65},{65,129},{129,193},{193,1... | collective-permute-start | bytes 806408 | tf_op jit(solution)/shard_map/ppermute | solution.py:157
  52.2 13.7 %collective-permute-start.13 = (bf16[14,16,600]{2,1,0:T(8,128)(2,1)S(1)}, bf16[14,16,600]{2,1,0:T(8,128)(2,1)S(1)}, u32[]{:S(2)}, u32[]{:S(2)}) collective-permute-start(bf16[14,16,600]{2,1,0:T(8,128)(2,1)S(1)} %add_convert_fusion.1), channel_id=1, source_target_pairs={{0,192},{64,0},{128,64},{192,128},{1,193},{65,1},{129,65},{193,129... | collective-permute-start | bytes 806408 | tf_op jit(solution)/shard_map/ppermute | solution.py:157
  66.3 46.5 %copy-start.4 = (bf16[4,600,420]{1,0,2:T(4,128)(2,1)S(1)}, bf16[4,600,420]{1,0,2:T(4,128)(2,1)}, u32[]{:S(2)}) copy-start(bf16[4,600,420]{1,0,2:T(4,128)(2,1)} %param.5) | copy-start | bytes 6048004
  93.6 2.1 %collective-permute-start.14 = (bf16[32,16,600]{2,1,0:T(8,128)(2,1)S(1)}, bf16[32,16,600]{2,1,0:T(8,128)(2,1)S(1)}, u32[]{:S(2)}, u32[]{:S(2)}) collective-permute-start(bf16[32,16,600]{2,1,0:T(8,128)(2,1)S(1)} %all_to_all.11), channel_id=1, source_target_pairs={{0,16},{16,0},{1,17},{17,1},{2,18},{18,2},{3,19},{19,3},{4,20},{20... | collective-permute-start | bytes 1843208 | tf_op jit(solution)/shard_map/ppermute | solution.py:161
  96.3 9.6 %collective-permute-start.17 = (bf16[216,600]{1,0:T(8,128)(2,1)S(1)}, bf16[216,600]{1,0:T(8,128)(2,1)S(1)}, u32[]{:S(2)}, u32[]{:S(2)}) collective-permute-start(bf16[216,600]{1,0:T(8,128)(2,1)S(1)} %inverse.1.refs_0_), channel_id=1, source_target_pairs={{0,64},{64,128},{128,192},{192,0},{1,65},{65,129},{129,193},{193,1... | collective-permute-start | bytes 777608 | tf_op jit(solution)/shard_map/ppermute | solution.py:157
  97.0 11.0 %collective-permute-start.16 = (bf16[216,600]{1,0:T(8,128)(2,1)S(1)}, bf16[216,600]{1,0:T(8,128)(2,1)S(1)}, u32[]{:S(2)}, u32[]{:S(2)}) collective-permute-start(bf16[216,600]{1,0:T(8,128)(2,1)S(1)} %inverse.1.refs_0_), channel_id=1, source_target_pairs={{0,128},{64,192},{128,0},{192,64},{1,129},{65,193},{129,1},{193,65... | collective-permute-start | bytes 777608 | tf_op jit(solution)/shard_map/ppermute | solution.py:157
  99.5 13.2 %collective-permute-start.15 = (bf16[216,600]{1,0:T(8,128)(2,1)S(1)}, bf16[216,600]{1,0:T(8,128)(2,1)S(1)}, u32[]{:S(2)}, u32[]{:S(2)}) collective-permute-start(bf16[216,600]{1,0:T(8,128)(2,1)S(1)} %inverse.1.refs_0_), channel_id=1, source_target_pairs={{0,192},{64,0},{128,64},{192,128},{1,193},{65,1},{129,65},{193,129... | collective-permute-start | bytes 777608 | tf_op jit(solution)/shard_map/ppermute | solution.py:157
  100.8 12.3 %collective-permute-start.18 = (bf16[216,600]{1,0:T(8,128)(2,1)S(1)}, bf16[216,600]{1,0:T(8,128)(2,1)S(1)}, u32[]{:S(2)}, u32[]{:S(2)}) collective-permute-start(bf16[216,600]{1,0:T(8,128)(2,1)S(1)} %inverse.1.refs_0_), channel_id=1, source_target_pairs={{0,16},{16,0},{1,17},{17,1},{2,18},{18,2},{3,19},{19,3},{4,20},{20... | collective-permute-start | bytes 777608 | tf_op jit(solution)/shard_map/ppermute | solution.py:161
  105.9 7.2 %collective-permute-start.21 = (bf16[216,600]{1,0:T(8,128)(2,1)S(1)}, bf16[216,600]{1,0:T(8,128)(2,1)S(1)}, u32[]{:S(2)}, u32[]{:S(2)}) collective-permute-start(bf16[216,600]{1,0:T(8,128)(2,1)S(1)} %collective-permute-done.17.refs_3_), channel_id=1, source_target_pairs={{0,16},{16,0},{1,17},{17,1},{2,18},{18,2},{3,19},{19,3},{4,20},{20... | collective-permute-start | bytes 777608 | tf_op jit(solution)/shard_map/ppermute | solution.py:161
  108.0 5.1 %collective-permute-start.20 = (bf16[216,600]{1,0:T(8,128)(2,1)S(1)}, bf16[216,600]{1,0:T(8,128)(2,1)S(1)}, u32[]{:S(2)}, u32[]{:S(2)}) collective-permute-start(bf16[216,600]{1,0:T(8,128)(2,1)S(1)} %collective-permute-done.16.refs_2_), channel_id=1, source_target_pairs={{0,16},{16,0},{1,17},{17,1},{2,18},{18,2},{3,19},{19,3},{4,20},{20... | collective-permute-start | bytes 777608 | tf_op jit(solution)/shard_map/ppermute | solution.py:161
  112.8 1.6 %collective-permute-start.19 = (bf16[216,600]{1,0:T(8,128)(2,1)S(1)}, bf16[216,600]{1,0:T(8,128)(2,1)S(1)}, u32[]{:S(2)}, u32[]{:S(2)}) collective-permute-start(bf16[216,600]{1,0:T(8,128)(2,1)S(1)} %collective-permute-done.15.refs_1_), channel_id=1, source_target_pairs={{0,16},{16,0},{1,17},{17,1},{2,18},{18,2},{3,19},{19,3},{4,20},{20... | collective-permute-start | bytes 777608 | tf_op jit(solution)/shard_map/ppermute | solution.py:161

commit v2 on v1

--- a/solution.py
+++ b/solution.py
@@ -25,7 +25,9 @@
 TRACE_ROW = BIN_DEV
 HALF = 208
 SPAN = 216
-UNROLL = 7
+HALF_BINS = BIN_DEV // 2
+FLOPS = 2_000_000_000
+
 
 f32 = jnp.float32
 bf16 = jnp.bfloat16
@@ -61,11 +63,11 @@
     out[...] = (d * jnp.where(row == 0, 1.0, 0.5)).astype(bf16)
 
 
-def middle_kernel(*refs):
+def middle_kernel(base, *refs):
     own, oth = refs[:XS], refs[XS : 2 * XS]
     map_real, map_imag, prior = refs[2 * XS : 2 * XS + 3]
-    outs = refs[2 * XS + 3 :]
-    w_own, w_oth, trace, scaled = outs[:XS], outs[XS : 2 * XS], outs[2 * XS], outs[2 * XS + 1]
+    before = refs[2 * XS + 3] if base else None
+    w_own, w_oth, trace, scaled = refs[2 * XS + 3 + (base > 0) :]
     sigma = jnp.where(lax.axis_index("c") == 0, 1.0, -1.0).astype(f32)
     first = lax.axis_index(FREQ) == 0
     half = XS * BLOCKS
@@ -73,10 +75,10 @@
     p = prior[...]
 
     def left(k):
-        weight = jnp.where(first & (k == 0), 1.0, 2.0).astype(f32)
-        v = jnp.concatenate([r[k] for r in own] + [r[k] for r in oth], axis=0)
-        ar = jnp.dot(v, map_real[k], preferred_element_type=f32)
-        ai = jnp.dot(v, map_imag[k], preferred_element_type=f32)
+        weight = jnp.where(first, 1.0, 2.0).astype(f32) if base + k == 0 else 2.0
+        v = jnp.concatenate([own[j][k] for j in range(XS)] + [oth[0][base + k]] + [oth[j][k] for j in range(1, XS)], axis=0)
+        ar = jnp.dot(v, map_real[base + k], preferred_element_type=f32)
+        ai = jnp.dot(v, map_imag[base + k], preferred_element_type=f32)
         u_own = ar[:half] + sigma * ai[half:]
         u_oth = ar[half:] - sigma * ai[:half]
         scaled[k, :half] = (u_own * p).astype(bf16)
@@ -85,25 +87,22 @@
 
     def right(k):
         a = scaled[k]
-        br = lax.dot_general(a, map_real[k], nt, preferred_element_type=f32)
-        bi = lax.dot_general(a, map_imag[k], nt, preferred_element_type=f32)
+        br = lax.dot_general(a, map_real[base + k], nt, preferred_element_type=f32)
+        bi = lax.dot_general(a, map_imag[base + k], nt, preferred_element_type=f32)
         to_own = (br[:half] - sigma * bi[half:]).astype(bf16)
         to_oth = (br[half:] + sigma * bi[:half]).astype(bf16)
         for j in range(XS):
             rows = slice(j * BLOCKS, (j + 1) * BLOCKS)
-            w_own[j][k] = to_own[rows]
-            w_oth[j][k] = to_oth[rows]
-
-    def lefts(i, total):
-        return total + sum(left(UNROLL * i + n) for n in range(UNROLL))
-
-    def rights(i, _):
-        for n in range(UNROLL):
-            right(UNROLL * i + n)
-        return 0
-
-    trace[...] = lax.fori_loop(0, BIN_DEV // UNROLL, lefts, jnp.zeros(p.shape, f32))
-    lax.fori_loop(0, BIN_DEV // UNROLL, rights, 0)
+            w_own[j, k] = to_own[rows]
+            w_oth[j, k] = to_oth[rows]
+
+    quad = sum(left(k) for k in range(HALF_BINS))
+    for k in range(HALF_BINS):
+        right(k)
+    if base:
+        trace[...] = trace_line(jnp.sum(quad + before[...]))
+    else:
+        trace[...] = quad
 
 
 def trace_line(total):
@@ -161,68 +160,65 @@
     return lax.ppermute(value, "c", [(0, 1), (1, 0)])
 
 
-def call(kernel, name, operands, outs, limit, scratch=()):
+def call(kernel, operands, outs, limit, scratch=(), flops=0):
     return pl.pallas_call(
         kernel,
         in_specs=[VMEM] * len(operands),
         out_specs=[VMEM] * len(outs),
         out_shape=[jax.ShapeDtypeStruct(*o) for o in outs],
         scratch_shapes=list(scratch),
-        name=name,
+        cost_estimate=pl.CostEstimate(flops=flops, bytes_accessed=0, transcendentals=0) if flops else None,
         compiler_params=pltpu.CompilerParams(vmem_limit_bytes=limit << 20),
     )(*operands)
 
 
-def shards(probes, map_real, map_imag, prior_var):
+def steps(probes, map_real, map_imag, prior_var):
     table = jnp.asarray(tables())
     by_time, probes = lax.optimization_barrier((probes.transpose(0, 2, 1), probes))
-    (spectra,) = call(dft_kernel, "dft", (table, by_time), [((ROWS, SENSORS), bf16)], 4)
+    (spectra,) = call(dft_kernel, (table, by_time), [((ROWS, SENSORS), bf16)], 4)
     arrived = lax.all_to_all(spectra.reshape(BLOCKS, BIN_PAD, SENSORS), FREQ, 0, 0, tiled=True)
     arrived = arrived.transpose(1, 0, 2)[:BIN_DEV]
-    away = {j: shift(arrived, "x", -j) for j in (2, 1, 3)}
-    own = [arrived] + [away[j] for j in range(1, XS)]
-    other = [swap_core(v) for v in own]
+    parts = [arrived[:HALF_BINS], arrived[HALF_BINS:]]
+    away = [{j: shift(part, "x", -j) for j in (2, 1, 3)} for part in parts]
+    own_other = swap_core(arrived)
 
     prior = prior_var[None, :]
-    block = ((BIN_DEV, BLOCKS, SENSORS), bf16)
-    *w, trace = call(
-        middle_kernel,
-        "middle",
-        [*own, *other, map_real, map_imag, prior],
-        [block] * (2 * XS) + [(prior.shape, f32)],
-        4,
-        [pltpu.VMEM((BIN_DEV, 2 * XS * BLOCKS, prior.shape[1]), bf16)],
-    )
-    both = {j: (w[j].astype(f32) + swap_core(w[XS + j]).astype(f32)).astype(bf16) for j in (2, 1, 3, 0)}
-    total = both[0].astype(f32)
-    for j in (2, 1, 3):
-        total = total + shift(both[j], "x", j).astype(f32)
-    total = total.astype(bf16).transpose(1, 0, 2)
-    quad = jnp.sum(trace)
-    quad_up = quad.astype(bf16)
-    quad_low = (quad - quad_up.astype(f32)).astype(bf16)
-    lane = jnp.arange(SENSORS)
-    line = jnp.where(lane == 0, quad_up, jnp.where(lane == 1, quad_low, jnp.zeros((), bf16)))
-    extra = jnp.where(
-        jnp.arange(BIN_PAD - BIN_DEV)[None, :, None] == 0, line[None, None, :], jnp.zeros((), bf16)
-    )
-    extra = jnp.broadcast_to(extra, (BLOCKS, BIN_PAD - BIN_DEV, SENSORS))
-    outgoing = jnp.concatenate([total, extra], axis=1)
+    block = ((XS, HALF_BINS, BLOCKS, SENSORS), bf16)
+    trace = None
+    totals = []
+    for at, part in enumerate(parts):
+        near = [away[at][j] for j in range(1, XS)]
+        w_own, w_oth, trace = call(
+            functools.partial(middle_kernel, at * HALF_BINS),
+            [part, *near, own_other, *[swap_core(v) for v in near], map_real, map_imag, prior]
+            + ([] if trace is None else [trace]),
+            [block] * 2 + [((1, SENSORS), bf16) if at else (prior.shape, f32)],
+            4,
+            [pltpu.VMEM((HALF_BINS, 2 * XS * BLOCKS, prior.shape[1]), bf16)],
+            FLOPS,
+        )
+        from_core = swap_core(w_oth)
+        both = [(w_own[j].astype(f32) + from_core[j].astype(f32)).astype(bf16) for j in range(XS)]
+        total = both[0].astype(f32)
+        for j in (2, 1, 3):
+            total = total + shift(both[j], "x", j).astype(f32)
+        totals.append(total.astype(bf16))
+    extra = jnp.concatenate([trace, jnp.zeros_like(trace)])[:, None, :]
+    extra = jnp.broadcast_to(extra, (BIN_PAD - BIN_DEV, BLOCKS, SENSORS))
+    outgoing = jnp.concatenate([*totals, extra]).transpose(1, 0, 2)
     outgoing = jnp.broadcast_to(outgoing[None], (2, BLOCKS, BIN_PAD, SENSORS))
     outgoing = outgoing.reshape(2 * BLOCKS, BIN_PAD, SENSORS)
     arrived = lax.all_to_all(outgoing, ("h",) + FREQ, 0, 0, tiled=True)
     pieces = [v.reshape(2, ROWS, SENSORS) for v in (arrived, swap_core(arrived))]
-    (part,) = call(inverse_kernel, "inverse", (table, *pieces), [((SPAN, SENSORS), bf16)], 4)
+    (part,) = call(inverse_kernel, (table, *pieces), [((SPAN, SENSORS), bf16)], 4)
     away = {j: shift(part, "x", -j) for j in (2, 1, 3)}
     own = [part] + [away[j] for j in range(1, XS)]
     other = [swap_core(v) for v in own]
-    (out,) = call(finish_kernel, "finish", (*own, *other, probes.transpose(0, 2, 1)), [((XS, STEPS, SENSORS), bf16)], 4)
+    (out,) = call(finish_kernel, (*own, *other, probes.transpose(0, 2, 1)), [((XS, STEPS, SENSORS), bf16)], 4)
     return out.transpose(0, 2, 1)
 
 
 def solution(mesh):
     torus = Mesh(mesh.devices.reshape(4, 2, 2, 4, 4), ("x", "h", "c", "zl", "y"))
     in_specs = (P(FREQ, None, None), P(FREQ, None, PAR), P(FREQ, None, PAR), P(PAR))
-    return jax.shard_map(
-        shards, mesh=torus, in_specs=in_specs, out_specs=P(FREQ, None, None), check_vma=False
-    )
+    return jax.shard_map(steps, mesh=torus, in_specs=in_specs, out_specs=P(FREQ, None, None), check_vma=False)

time: 120 us -> 117 us (0.975)
  starting transfers between devices: 14.8 us -> 26.6 us
  waiting for transfers between devices: 39.5 us -> 29.4 us
  other arithmetic: 2.14 us -> 0.48 us
  between operations: 1.48 us -> 0.24 us
    ppermute x9 -> x15, starting transfers between devices: 13.6 us -> 24.6 us  [shift(): return lax.ppermute(value, axis, [(i, (i + by) % n) for i in range(n)])]
    ppermute x9 -> x15, waiting for transfers between devices: 34.6 us -> 24.6 us  [shift(): return lax.ppermute(value, axis, [(i, (i + by) % n) for i in range(n)])]
    pallas_call x4 -> x5, Pallas kernels: 7.5 us -> 7.2 us  [call(): pl.pallas_call(kernel, in_specs=[VMEM] * len(operands), out_specs=[VMEM]...]
    ppermute x13 -> x14, waiting for transfers between devices: 4.9 us -> 4.81 us  [swap_core(): return lax.ppermute(value, 'c', [(0, 1), (1, 0)])]
  transfers between devices with their start and end apart: 22 -> 29, of which waited for: 12 -> 13; matrix products, arithmetic and copies ran while one was open for 2% -> 1% of each run, Pallas kernels for 0% -> 2%
where the time goes in v2:
time: 117 us; the launch traced here: 116 us
  blocking collectives  47 us (40%)
  waiting for transfers between devices  29.4 us (25%)
  starting transfers between devices  26.6 us (23%)
  Pallas kernels  7.2 us (6%)
  local copies, waits for them, and re-layouts  4.73 us (4%)
    all_to_all x1, blocking collectives, steps(): arrived = lax.all_to_all(outgoing, ('h',) + FREQ, 0, 0, tiled=True)  26.6 us
    ppermute x15, starting transfers between devices, shift(): return lax.ppermute(value, axis, [(i, (i + by) % n) for i in range(n)])  24.6 us
    ppermute x15, waiting for transfers between devices, shift(): return lax.ppermute(value, axis, [(i, (i + by) % n) for i in range(n)])  24.6 us
    all_to_all x1, blocking collectives, steps(): lax.all_to_all(spectra.reshape(BLOCKS, BIN_PAD, SENSORS), FREQ, 0, 0, til...  20.4 us
    pallas_call x5, Pallas kernels, call(): pl.pallas_call(kernel, in_specs=[VMEM] * len(operands), out_specs=[VMEM]...  7.2 us
    ppermute x14, waiting for transfers between devices, swap_core(): return lax.ppermute(value, 'c', [(0, 1), (1, 0)])  4.81 us
  transfers between devices with their start and end apart: 29, of which 13 were waited for; matrix products, arithmetic and copies ran while one was open for 1% of the time, Pallas kernels for 2%

profile of v2, /device:TPU:2, one launch (start us, length us, event | category | flops | bytes accessed | tf_op | source)
XLA Modules:
  0.0 115.7 jit_solution(2589018461307704786)
XLA Ops:
  0.0 2.0 %copy.24 = bf16[4,600,420]{1,2,0:T(8,128)(2,1)S(1)} copy(bf16[4,600,420]{1,0,2:T(4,128)(2,1)} %param.5) | data formatting | bytes 4032000 | tf_op args[0]
  2.7 20.4 %all_to_all.10 = bf16[16,16,600]{2,1,0:T(8,128)(2,1)S(1)} all-to-all(bf16[16,16,600]{2,1,0:T(8,128)(2,1)S(1)} %bitcast.43), channel_id=1, replica_groups=mesh['x'=4,'h'=2,'c'=2,'zl'=4,'y'=4] {'zl','y'}, dimensions={0} | all-to-all | bytes 614400 | tf_op jit(solution)/shard_map/all_to_all | solution.py:179
  23.2 1.6 %collective-permute-start.2 = (bf16[7,16,600]{2,1,0:T(8,128)(2,1)S(1)}, bf16[7,16,600]{2,1,0:T(8,128)(2,1)S(1)}, u32[]{:S(2)}, u32[]{:S(2)}) collective-permute-start(bf16[7,16,600]{2,1,0:T(8,128)(2,1)S(1)} %get-tuple-element.27.refs_0_), channel_id=1, source_target_pairs={{0,64},{64,128},{128,192},{192,0},{1,65},{65,129},{129,193},{193,1... | collective-permute-start | bytes 403208 | tf_op jit(solution)/shard_map/ppermute | solution.py:156
  24.8 1.1 collective-permute-start.1
  25.9 2.2 %collective-permute-start = (bf16[7,16,600]{2,1,0:T(8,128)(2,1)S(1)}, bf16[7,16,600]{2,1,0:T(8,128)(2,1)S(1)}, u32[]{:S(2)}, u32[]{:S(2)}) collective-permute-start(bf16[7,16,600]{2,1,0:T(8,128)(2,1)S(1)} %get-tuple-element.27.refs_0_), channel_id=1, source_target_pairs={{0,192},{64,0},{128,64},{192,128},{1,193},{65,1},{129,65},{193,129... | collective-permute-start | bytes 403208 | tf_op jit(solution)/shard_map/ppermute | solution.py:156
  28.0 3.5 %collective-permute-start.12 = (bf16[7,16,600]{2,1,0:T(8,128)(2,1)S(1)}, bf16[7,16,600]{2,1,0:T(8,128)(2,1)S(1)}, u32[]{:S(2)}, u32[]{:S(2)}) collective-permute-start(bf16[7,16,600]{2,1,0:T(8,128)(2,1)S(1)} %get-tuple-element.28.refs_0_), channel_id=1, source_target_pairs={{0,128},{64,192},{128,0},{192,64},{1,129},{65,193},{129,1},{193,65... | collective-permute-start | bytes 403208 | tf_op jit(solution)/shard_map/ppermute | solution.py:156
  31.7 1.3 %collective-permute-done.1.refs_2_ = bf16[7,16,600]{2,1,0:T(8,128)(2,1)S(1)} collective-permute-done((bf16[7,16,600]{2,1,0:T(8,128)(2,1)S(1)}, bf16[7,16,600]{2,1,0:T(8,128)(2,1)S(1)}, u32[]{:S(2)}, u32[]{:S(2)}) %collective-permute-start.1) | collective-permute-done | bytes 134432 | tf_op jit(solution)/shard_map/ppermute | solution.py:156
  33.0 2.8 %collective-permute-start.11 = (bf16[7,16,600]{2,1,0:T(8,128)(2,1)S(1)}, bf16[7,16,600]{2,1,0:T(8,128)(2,1)S(1)}, u32[]{:S(2)}, u32[]{:S(2)}) collective-permute-start(bf16[7,16,600]{2,1,0:T(8,128)(2,1)S(1)} %get-tuple-element.28.refs_0_), channel_id=1, source_target_pairs={{0,192},{64,0},{128,64},{192,128},{1,193},{65,1},{129,65},{193,129... | collective-permute-start | bytes 403208 | tf_op jit(solution)/shard_map/ppermute | solution.py:156
  36.4 2.9 %collective-permute-done.11.refs_1_ = bf16[7,16,600]{2,1,0:T(8,128)(2,1)S(1)} collective-permute-done((bf16[7,16,600]{2,1,0:T(8,128)(2,1)S(1)}, bf16[7,16,600]{2,1,0:T(8,128)(2,1)S(1)}, u32[]{:S(2)}, u32[]{:S(2)}) %collective-permute-start.11) | collective-permute-done | bytes 134432 | tf_op jit(solution)/shard_map/ppermute | solution.py:156
  40.2 2.4 %shard_map.56 = (bf16[4,7,16,600]{3,2,1,0:T(8,128)(2,1)S(1)}, bf16[4,7,16,600]{3,2,1,0:T(8,128)(2,1)S(1)}, f32[1,256]{1,0:T(1,128)S(1)}) custom-call(bf16[7,16,600]{2,1,0:T(8,128)(2,1)S(1)} %get-tuple-element.27.refs_0_, bf16[7,16,600]{2,1,0:T(8,128)(2,1)S(1)} %collective-permute-done.refs_1_, bf16[7,16,600]{2,1,0:T(8,128)(2,1)S(1)} %collective-permute-done.1.refs_2_, ...), custom_call_target="tpu_custom_call" | custom-call | flops 2000000000 | tf_op jit(solution)/shard_map/pallas_call | solution.py:164
  42.6 2.3 %shard_map.57 = (bf16[4,7,16,600]{3,2,1,0:T(8,128)(2,1)S(1)}, bf16[4,7,16,600]{3,2,1,0:T(8,128)(2,1)S(1)}, bf16[1,600]{1,0:T(2,128)(2,1)S(1)}) custom-call(bf16[7,16,600]{2,1,0:T(8,128)(2,1)S(1)} %get-tuple-element.28.refs_0_, bf16[7,16,600]{2,1,0:T(8,128)(2,1)S(1)} %collective-permute-done.11.refs_1_, ...), custom_call_target="tpu_custom_call" | custom-call | flops 2000000000 | tf_op jit(solution)/shard_map/pallas_call | solution.py:164
  45.5 1.5 %collective-permute-done.17 = bf16[4,7,16,600]{3,2,1,0:T(8,128)(2,1)S(1)} collective-permute-done((bf16[4,7,16,600]{3,2,1,0:T(8,128)(2,1)S(1)}, bf16[4,7,16,600]{3,2,1,0:T(8,128)(2,1)S(1)}, u32[]{:S(2)}, u32[]{:S(2)}) %collective-permute-start.17) | collective-permute-done | bytes 537632 | tf_op jit(solution)/shard_map/ppermute | solution.py:160
  47.1 1.7 %collective-permute-start.18 = (bf16[7,16,600]{2,1,0:T(8,128)(2,1)S(1)}, bf16[7,16,600]{2,1,0:T(8,128)(2,1)S(1)}, u32[]{:S(2)}, u32[]{:S(2)}) collective-permute-start(bf16[7,16,600]{2,1,0:T(8,128)(2,1)S(1)} %get-tuple-element.24), channel_id=1, source_target_pairs={{0,128},{64,192},{128,0},{192,64},{1,129},{65,193},{129,1},{193,65... | collective-permute-start | bytes 403208 | tf_op jit(solution)/shard_map/ppermute | solution.py:156
  48.8 1.4 %collective-permute-start.20 = (bf16[7,16,600]{2,1,0:T(8,128)(2,1)S(1)}, bf16[7,16,600]{2,1,0:T(8,128)(2,1)S(1)}, u32[]{:S(2)}, u32[]{:S(2)}) collective-permute-start(bf16[7,16,600]{2,1,0:T(8,128)(2,1)S(1)} %get-tuple-element.25), channel_id=1, source_target_pairs={{0,192},{64,0},{128,64},{192,128},{1,193},{65,1},{129,65},{193,129... | collective-permute-start | bytes 403208 | tf_op jit(solution)/shard_map/ppermute | solution.py:156
  50.2 0.7 collective-permute-start.19
  50.9 3.2 %collective-permute-start.8 = (bf16[7,16,600]{2,1,0:T(8,128)(2,1)S(1)}, bf16[7,16,600]{2,1,0:T(8,128)(2,1)S(1)}, u32[]{:S(2)}, u32[]{:S(2)}) collective-permute-start(bf16[7,16,600]{2,1,0:T(8,128)(2,1)S(1)} %get-tuple-element.21), channel_id=1, source_target_pairs={{0,128},{64,192},{128,0},{192,64},{1,129},{65,193},{129,1},{193,65... | collective-permute-start | bytes 403208 | tf_op jit(solution)/shard_map/ppermute | solution.py:156
  54.5 0.9 collective-permute-done.18
  55.4 0.9 collective-permute-start.9
  56.3 2.3 %collective-permute-done.20 = bf16[7,16,600]{2,1,0:T(8,128)(2,1)S(1)} collective-permute-done((bf16[7,16,600]{2,1,0:T(8,128)(2,1)S(1)}, bf16[7,16,600]{2,1,0:T(8,128)(2,1)S(1)}, u32[]{:S(2)}, u32[]{:S(2)}) %collective-permute-start.20) | collective-permute-done | bytes 134432 | tf_op jit(solution)/shard_map/ppermute | solution.py:156
  58.6 2.9 %collective-permute-done.8 = bf16[7,16,600]{2,1,0:T(8,128)(2,1)S(1)} collective-permute-done((bf16[7,16,600]{2,1,0:T(8,128)(2,1)S(1)}, bf16[7,16,600]{2,1,0:T(8,128)(2,1)S(1)}, u32[]{:S(2)}, u32[]{:S(2)}) %collective-permute-start.8) | collective-permute-done | bytes 134432 | tf_op jit(solution)/shard_map/ppermute | solution.py:156
  61.6 2.1 %collective-permute-done.10 = bf16[7,16,600]{2,1,0:T(8,128)(2,1)S(1)} collective-permute-done((bf16[7,16,600]{2,1,0:T(8,128)(2,1)S(1)}, bf16[7,16,600]{2,1,0:T(8,128)(2,1)S(1)}, u32[]{:S(2)}, u32[]{:S(2)}) %collective-permute-start.10) | collective-permute-done | bytes 134432 | tf_op jit(solution)/shard_map/ppermute | solution.py:156
  64.0 26.6 %all_to_all.11 = bf16[32,16,600]{2,1,0:T(8,128)(2,1)S(1)} all-to-all(bf16[32,16,600]{2,1,0:T(8,128)(2,1)S(1)} %bitcast.47), channel_id=1, replica_groups=mesh['x'=4,'h'=2,'c'=2,'zl'=4,'y'=4] {'h','zl','y'}, dimensions={0} | all-to-all | bytes 1228800 | tf_op jit(solution)/shard_map/all_to_all | solution.py:211
  90.6 2.1 %collective-permute-done.21 = bf16[32,16,600]{2,1,0:T(8,128)(2,1)S(1)} collective-permute-done((bf16[32,16,600]{2,1,0:T(8,128)(2,1)S(1)}, bf16[32,16,600]{2,1,0:T(8,128)(2,1)S(1)}, u32[]{:S(2)}, u32[]{:S(2)}) %collective-permute-start.21) | collective-permute-done | bytes 614432 | tf_op jit(solution)/shard_map/ppermute | solution.py:160
  93.3 1.6 %collective-permute-start.24 = (bf16[216,600]{1,0:T(8,128)(2,1)S(1)}, bf16[216,600]{1,0:T(8,128)(2,1)S(1)}, u32[]{:S(2)}, u32[]{:S(2)}) collective-permute-start(bf16[216,600]{1,0:T(8,128)(2,1)S(1)} %shard_map.58.refs_0_), channel_id=1, source_target_pairs={{0,64},{64,128},{128,192},{192,0},{1,65},{65,129},{129,193},{193,1... | collective-permute-start | bytes 777608 | tf_op jit(solution)/shard_map/ppermute | solution.py:156
  94.9 2.4 %collective-permute-start.23 = (bf16[216,600]{1,0:T(8,128)(2,1)S(1)}, bf16[216,600]{1,0:T(8,128)(2,1)S(1)}, u32[]{:S(2)}, u32[]{:S(2)}) collective-permute-start(bf16[216,600]{1,0:T(8,128)(2,1)S(1)} %shard_map.58.refs_0_), channel_id=1, source_target_pairs={{0,128},{64,192},{128,0},{192,64},{1,129},{65,193},{129,1},{193,65... | collective-permute-start | bytes 777608 | tf_op jit(solution)/shard_map/ppermute | solution.py:156
  97.3 1.3 %collective-permute-start.22 = (bf16[216,600]{1,0:T(8,128)(2,1)S(1)}, bf16[216,600]{1,0:T(8,128)(2,1)S(1)}, u32[]{:S(2)}, u32[]{:S(2)}) collective-permute-start(bf16[216,600]{1,0:T(8,128)(2,1)S(1)} %shard_map.58.refs_0_), channel_id=1, source_target_pairs={{0,192},{64,0},{128,64},{192,128},{1,193},{65,1},{129,65},{193,129... | collective-permute-start | bytes 777608 | tf_op jit(solution)/shard_map/ppermute | solution.py:156
  98.6 4.2 %collective-permute-done.24.refs_3_ = bf16[216,600]{1,0:T(8,128)(2,1)S(1)} collective-permute-done((bf16[216,600]{1,0:T(8,128)(2,1)S(1)}, bf16[216,600]{1,0:T(8,128)(2,1)S(1)}, u32[]{:S(2)}, u32[]{:S(2)}) %collective-permute-start.24) | collective-permute-done | bytes 259232 | tf_op jit(solution)/shard_map/ppermute | solution.py:156
  102.8 3.1 %collective-permute-done.23.refs_2_ = bf16[216,600]{1,0:T(8,128)(2,1)S(1)} collective-permute-done((bf16[216,600]{1,0:T(8,128)(2,1)S(1)}, bf16[216,600]{1,0:T(8,128)(2,1)S(1)}, u32[]{:S(2)}, u32[]{:S(2)}) %collective-permute-start.23) | collective-permute-done | bytes 259232 | tf_op jit(solution)/shard_map/ppermute | solution.py:156
  105.9 4.8 %collective-permute-done.22.refs_1_ = bf16[216,600]{1,0:T(8,128)(2,1)S(1)} collective-permute-done((bf16[216,600]{1,0:T(8,128)(2,1)S(1)}, bf16[216,600]{1,0:T(8,128)(2,1)S(1)}, u32[]{:S(2)}, u32[]{:S(2)}) %collective-permute-start.22) | collective-permute-done | bytes 259232 | tf_op jit(solution)/shard_map/ppermute | solution.py:156
  111.0 1.2 %collective-permute-done.26.refs_5_ = bf16[216,600]{1,0:T(8,128)(2,1)S(1)} collective-permute-done((bf16[216,600]{1,0:T(8,128)(2,1)S(1)}, bf16[216,600]{1,0:T(8,128)(2,1)S(1)}, u32[]{:S(2)}, u32[]{:S(2)}) %collective-permute-start.26) | collective-permute-done | bytes 259232 | tf_op jit(solution)/shard_map/ppermute | solution.py:160
  112.2 1.3 %shard_map.59 = bf16[4,420,600]{2,1,0:T(8,128)(2,1)S(1)} custom-call(bf16[216,600]{1,0:T(8,128)(2,1)S(1)} %shard_map.58.refs_0_, bf16[216,600]{1,0:T(8,128)(2,1)S(1)} %collective-permute-done.22.refs_1_, bf16[216,600]{1,0:T(8,128)(2,1)S(1)} %collective-permute-done.23.refs_2_, bf16[216,600]{1,0:T(8,128)(2,1)S(1)} %collective-permute-done.24.refs_3_, ...), custom_call_target="tpu_custom_call" | custom-call | tf_op jit(solution)/shard_map/pallas_call | solution.py:164
  113.5 2.2 %copy.19 = bf16[4,600,420]{1,0,2:T(4,128)(2,1)} copy(bf16[4,600,420]{1,2,0:T(8,128)(2,1)S(1)} %bitcast.40) | data formatting | bytes 4032000 | tf_op jit(solution)/shard_map/transpose | solution.py:218
  (58 shorter events, 4.7 us)
Async XLA Ops:
  0.0 40.2 %copy-start.1 = (bf16[14,600,256]{2,1,0:T(8,128)(2,1)S(1)}, bf16[14,600,256]{2,1,0:T(8,128)(2,1)}, u32[]{:S(2)}) copy-start(bf16[14,600,256]{2,1,0:T(8,128)(2,1)} %refs_9_.3) | copy-start | bytes 12902404
  2.0 38.1 %copy-start = (bf16[14,600,256]{2,1,0:T(8,128)(2,1)S(1)}, bf16[14,600,256]{2,1,0:T(8,128)(2,1)}, u32[]{:S(2)}) copy-start(bf16[14,600,256]{2,1,0:T(8,128)(2,1)} %refs_8_.3) | copy-start | bytes 12902404
  23.2 8.4 %collective-permute-start.2 = (bf16[7,16,600]{2,1,0:T(8,128)(2,1)S(1)}, bf16[7,16,600]{2,1,0:T(8,128)(2,1)S(1)}, u32[]{:S(2)}, u32[]{:S(2)}) collective-permute-start(bf16[7,16,600]{2,1,0:T(8,128)(2,1)S(1)} %get-tuple-element.27.refs_0_), channel_id=1, source_target_pairs={{0,64},{64,128},{128,192},{192,0},{1,65},{65,129},{129,193},{193,1... | collective-permute-start | bytes 403208 | tf_op jit(solution)/shard_map/ppermute | solution.py:156
  24.8 8.2 %collective-permute-start.1 = (bf16[7,16,600]{2,1,0:T(8,128)(2,1)S(1)}, bf16[7,16,600]{2,1,0:T(8,128)(2,1)S(1)}, u32[]{:S(2)}, u32[]{:S(2)}) collective-permute-start(bf16[7,16,600]{2,1,0:T(8,128)(2,1)S(1)} %get-tuple-element.27.refs_0_), channel_id=1, source_target_pairs={{0,128},{64,192},{128,0},{192,64},{1,129},{65,193},{129,1},{193,65... | collective-permute-start | bytes 403208 | tf_op jit(solution)/shard_map/ppermute | solution.py:156
  25.9 9.9 %collective-permute-start = (bf16[7,16,600]{2,1,0:T(8,128)(2,1)S(1)}, bf16[7,16,600]{2,1,0:T(8,128)(2,1)S(1)}, u32[]{:S(2)}, u32[]{:S(2)}) collective-permute-start(bf16[7,16,600]{2,1,0:T(8,128)(2,1)S(1)} %get-tuple-element.27.refs_0_), channel_id=1, source_target_pairs={{0,192},{64,0},{128,64},{192,128},{1,193},{65,1},{129,65},{193,129... | collective-permute-start | bytes 403208 | tf_op jit(solution)/shard_map/ppermute | solution.py:156
  28.0 7.9 %collective-permute-start.13 = (bf16[7,16,600]{2,1,0:T(8,128)(2,1)S(1)}, bf16[7,16,600]{2,1,0:T(8,128)(2,1)S(1)}, u32[]{:S(2)}, u32[]{:S(2)}) collective-permute-start(bf16[7,16,600]{2,1,0:T(8,128)(2,1)S(1)} %get-tuple-element.28.refs_0_), channel_id=1, source_target_pairs={{0,64},{64,128},{128,192},{192,0},{1,65},{65,129},{129,193},{193,1... | collective-permute-start | bytes 403208 | tf_op jit(solution)/shard_map/ppermute | solution.py:156
  28.0 8.3 %collective-permute-start.12 = (bf16[7,16,600]{2,1,0:T(8,128)(2,1)S(1)}, bf16[7,16,600]{2,1,0:T(8,128)(2,1)S(1)}, u32[]{:S(2)}, u32[]{:S(2)}) collective-permute-start(bf16[7,16,600]{2,1,0:T(8,128)(2,1)S(1)} %get-tuple-element.28.refs_0_), channel_id=1, source_target_pairs={{0,128},{64,192},{128,0},{192,64},{1,129},{65,193},{129,1},{193,65... | collective-permute-start | bytes 403208 | tf_op jit(solution)/shard_map/ppermute | solution.py:156
  31.6 8.6 %collective-permute-start.3 = (bf16[14,16,600]{2,1,0:T(8,128)(2,1)S(1)}, bf16[14,16,600]{2,1,0:T(8,128)(2,1)S(1)}, u32[]{:S(2)}, u32[]{:S(2)}) collective-permute-start(bf16[14,16,600]{2,1,0:T(8,128)(2,1)S(1)} %slice.79), channel_id=1, source_target_pairs={{0,16},{16,0},{1,17},{17,1},{2,18},{18,2},{3,19},{19,3},{4,20},{20... | collective-permute-start | bytes 806408 | tf_op jit(solution)/shard_map/ppermute | solution.py:160
  33.0 6.3 %collective-permute-start.11 = (bf16[7,16,600]{2,1,0:T(8,128)(2,1)S(1)}, bf16[7,16,600]{2,1,0:T(8,128)(2,1)S(1)}, u32[]{:S(2)}, u32[]{:S(2)}) collective-permute-start(bf16[7,16,600]{2,1,0:T(8,128)(2,1)S(1)} %get-tuple-element.28.refs_0_), channel_id=1, source_target_pairs={{0,192},{64,0},{128,64},{192,128},{1,193},{65,1},{129,65},{193,129... | collective-permute-start | bytes 403208 | tf_op jit(solution)/shard_map/ppermute | solution.py:156
  35.8 3.5 %collective-permute-start.6 = (bf16[7,16,600]{2,1,0:T(8,128)(2,1)S(1)}, bf16[7,16,600]{2,1,0:T(8,128)(2,1)S(1)}, u32[]{:S(2)}, u32[]{:S(2)}) collective-permute-start(bf16[7,16,600]{2,1,0:T(8,128)(2,1)S(1)} %collective-permute-done.2.refs_3_), channel_id=1, source_target_pairs={{0,16},{16,0},{1,17},{17,1},{2,18},{18,2},{3,19},{19,3},{4,20},{20... | collective-permute-start | bytes 403208 | tf_op jit(solution)/shard_map/ppermute | solution.py:160
  35.9 4.0 %collective-permute-start.5 = (bf16[7,16,600]{2,1,0:T(8,128)(2,1)S(1)}, bf16[7,16,600]{2,1,0:T(8,128)(2,1)S(1)}, u32[]{:S(2)}, u32[]{:S(2)}) collective-permute-start(bf16[7,16,600]{2,1,0:T(8,128)(2,1)S(1)} %collective-permute-done.1.refs_2_), channel_id=1, source_target_pairs={{0,16},{16,0},{1,17},{17,1},{2,18},{18,2},{3,19},{19,3},{4,20},{20... | collective-permute-start | bytes 403208 | tf_op jit(solution)/shard_map/ppermute | solution.py:160
  36.4 3.8 %collective-permute-start.4 = (bf16[7,16,600]{2,1,0:T(8,128)(2,1)S(1)}, bf16[7,16,600]{2,1,0:T(8,128)(2,1)S(1)}, u32[]{:S(2)}, u32[]{:S(2)}) collective-permute-start(bf16[7,16,600]{2,1,0:T(8,128)(2,1)S(1)} %collective-permute-done.refs_1_), channel_id=1, source_target_pairs={{0,16},{16,0},{1,17},{17,1},{2,18},{18,2},{3,19},{19,3},{4,20},{20... | collective-permute-start | bytes 403208 | tf_op jit(solution)/shard_map/ppermute | solution.py:160
  39.4 3.2 %collective-permute-start.16 = (bf16[7,16,600]{2,1,0:T(8,128)(2,1)S(1)}, bf16[7,16,600]{2,1,0:T(8,128)(2,1)S(1)}, u32[]{:S(2)}, u32[]{:S(2)}) collective-permute-start(bf16[7,16,600]{2,1,0:T(8,128)(2,1)S(1)} %collective-permute-done.13.refs_3_), channel_id=1, source_target_pairs={{0,16},{16,0},{1,17},{17,1},{2,18},{18,2},{3,19},{19,3},{4,20},{20... | collective-permute-start | bytes 403208 | tf_op jit(solution)/shard_map/ppermute | solution.py:160
  39.4 3.2 %collective-permute-start.15 = (bf16[7,16,600]{2,1,0:T(8,128)(2,1)S(1)}, bf16[7,16,600]{2,1,0:T(8,128)(2,1)S(1)}, u32[]{:S(2)}, u32[]{:S(2)}) collective-permute-start(bf16[7,16,600]{2,1,0:T(8,128)(2,1)S(1)} %collective-permute-done.12.refs_2_), channel_id=1, source_target_pairs={{0,16},{16,0},{1,17},{17,1},{2,18},{18,2},{3,19},{19,3},{4,20},{20... | collective-permute-start | bytes 403208 | tf_op jit(solution)/shard_map/ppermute | solution.py:160
  39.9 2.7 %collective-permute-start.14 = (bf16[7,16,600]{2,1,0:T(8,128)(2,1)S(1)}, bf16[7,16,600]{2,1,0:T(8,128)(2,1)S(1)}, u32[]{:S(2)}, u32[]{:S(2)}) collective-permute-start(bf16[7,16,600]{2,1,0:T(8,128)(2,1)S(1)} %collective-permute-done.11.refs_1_), channel_id=1, source_target_pairs={{0,16},{16,0},{1,17},{17,1},{2,18},{18,2},{3,19},{19,3},{4,20},{20... | collective-permute-start | bytes 403208 | tf_op jit(solution)/shard_map/ppermute | solution.py:160
  44.9 2.1 %collective-permute-start.17 = (bf16[4,7,16,600]{3,2,1,0:T(8,128)(2,1)S(1)}, bf16[4,7,16,600]{3,2,1,0:T(8,128)(2,1)S(1)}, u32[]{:S(2)}, u32[]{:S(2)}) collective-permute-start(bf16[4,7,16,600]{3,2,1,0:T(8,128)(2,1)S(1)} %get-tuple-element.18), channel_id=1, source_target_pairs={{0,16},{16,0},{1,17},{17,1},{2,18},{18,2},{3,19},{19,3},{4,20},{20... | collective-permute-start | bytes 1612808 | tf_op jit(solution)/shard_map/ppermute | solution.py:160
  45.3 5.6 %collective-permute-start.7 = (bf16[4,7,16,600]{3,2,1,0:T(8,128)(2,1)S(1)}, bf16[4,7,16,600]{3,2,1,0:T(8,128)(2,1)S(1)}, u32[]{:S(2)}, u32[]{:S(2)}) collective-permute-start(bf16[4,7,16,600]{3,2,1,0:T(8,128)(2,1)S(1)} %get-tuple-element.15), channel_id=1, source_target_pairs={{0,16},{16,0},{1,17},{17,1},{2,18},{18,2},{3,19},{19,3},{4,20},{20... | collective-permute-start | bytes 1612808 | tf_op jit(solution)/shard_map/ppermute | solution.py:160
  47.1 8.3 %collective-permute-start.18 = (bf16[7,16,600]{2,1,0:T(8,128)(2,1)S(1)}, bf16[7,16,600]{2,1,0:T(8,128)(2,1)S(1)}, u32[]{:S(2)}, u32[]{:S(2)}) collective-permute-start(bf16[7,16,600]{2,1,0:T(8,128)(2,1)S(1)} %get-tuple-element.24), channel_id=1, source_target_pairs={{0,128},{64,192},{128,0},{192,64},{1,129},{65,193},{129,1},{193,65... | collective-permute-start | bytes 403208 | tf_op jit(solution)/shard_map/ppermute | solution.py:156
  48.8 9.7 %collective-permute-start.20 = (bf16[7,16,600]{2,1,0:T(8,128)(2,1)S(1)}, bf16[7,16,600]{2,1,0:T(8,128)(2,1)S(1)}, u32[]{:S(2)}, u32[]{:S(2)}) collective-permute-start(bf16[7,16,600]{2,1,0:T(8,128)(2,1)S(1)} %get-tuple-element.25), channel_id=1, source_target_pairs={{0,192},{64,0},{128,64},{192,128},{1,193},{65,1},{129,65},{193,129... | collective-permute-start | bytes 403208 | tf_op jit(solution)/shard_map/ppermute | solution.py:156
  50.2 8.3 %collective-permute-start.19 = (bf16[7,16,600]{2,1,0:T(8,128)(2,1)S(1)}, bf16[7,16,600]{2,1,0:T(8,128)(2,1)S(1)}, u32[]{:S(2)}, u32[]{:S(2)}) collective-permute-start(bf16[7,16,600]{2,1,0:T(8,128)(2,1)S(1)} %get-tuple-element.26), channel_id=1, source_target_pairs={{0,64},{64,128},{128,192},{192,0},{1,65},{65,129},{129,193},{193,1... | collective-permute-start | bytes 403208 | tf_op jit(solution)/shard_map/ppermute | solution.py:156
  50.9 10.6 %collective-permute-start.8 = (bf16[7,16,600]{2,1,0:T(8,128)(2,1)S(1)}, bf16[7,16,600]{2,1,0:T(8,128)(2,1)S(1)}, u32[]{:S(2)}, u32[]{:S(2)}) collective-permute-start(bf16[7,16,600]{2,1,0:T(8,128)(2,1)S(1)} %get-tuple-element.21), channel_id=1, source_target_pairs={{0,128},{64,192},{128,0},{192,64},{1,129},{65,193},{129,1},{193,65... | collective-permute-start | bytes 403208 | tf_op jit(solution)/shard_map/ppermute | solution.py:156
  54.2 9.5 %collective-permute-start.10 = (bf16[7,16,600]{2,1,0:T(8,128)(2,1)S(1)}, bf16[7,16,600]{2,1,0:T(8,128)(2,1)S(1)}, u32[]{:S(2)}, u32[]{:S(2)}) collective-permute-start(bf16[7,16,600]{2,1,0:T(8,128)(2,1)S(1)} %get-tuple-element.22), channel_id=1, source_target_pairs={{0,192},{64,0},{128,64},{192,128},{1,193},{65,1},{129,65},{193,129... | collective-permute-start | bytes 403208 | tf_op jit(solution)/shard_map/ppermute | solution.py:156
  55.4 8.3 %collective-permute-start.9 = (bf16[7,16,600]{2,1,0:T(8,128)(2,1)S(1)}, bf16[7,16,600]{2,1,0:T(8,128)(2,1)S(1)}, u32[]{:S(2)}, u32[]{:S(2)}) collective-permute-start(bf16[7,16,600]{2,1,0:T(8,128)(2,1)S(1)} %get-tuple-element.23), channel_id=1, source_target_pairs={{0,64},{64,128},{128,192},{192,0},{1,65},{65,129},{129,193},{193,1... | collective-permute-start | bytes 403208 | tf_op jit(solution)/shard_map/ppermute | solution.py:156
  63.9 46.8 %copy-start.4 = (bf16[4,600,420]{1,0,2:T(4,128)(2,1)S(1)}, bf16[4,600,420]{1,0,2:T(4,128)(2,1)}, u32[]{:S(2)}) copy-start(bf16[4,600,420]{1,0,2:T(4,128)(2,1)} %param.5) | copy-start | bytes 6048004
  90.6 2.1 %collective-permute-start.21 = (bf16[32,16,600]{2,1,0:T(8,128)(2,1)S(1)}, bf16[32,16,600]{2,1,0:T(8,128)(2,1)S(1)}, u32[]{:S(2)}, u32[]{:S(2)}) collective-permute-start(bf16[32,16,600]{2,1,0:T(8,128)(2,1)S(1)} %all_to_all.11), channel_id=1, source_target_pairs={{0,16},{16,0},{1,17},{17,1},{2,18},{18,2},{3,19},{19,3},{4,20},{20... | collective-permute-start | bytes 1843208 | tf_op jit(solution)/shard_map/ppermute | solution.py:160
  93.3 9.6 %collective-permute-start.24 = (bf16[216,600]{1,0:T(8,128)(2,1)S(1)}, bf16[216,600]{1,0:T(8,128)(2,1)S(1)}, u32[]{:S(2)}, u32[]{:S(2)}) collective-permute-start(bf16[216,600]{1,0:T(8,128)(2,1)S(1)} %shard_map.58.refs_0_), channel_id=1, source_target_pairs={{0,64},{64,128},{128,192},{192,0},{1,65},{65,129},{129,193},{193,1... | collective-permute-start | bytes 777608 | tf_op jit(solution)/shard_map/ppermute | solution.py:156
  94.9 11.0 %collective-permute-start.23 = (bf16[216,600]{1,0:T(8,128)(2,1)S(1)}, bf16[216,600]{1,0:T(8,128)(2,1)S(1)}, u32[]{:S(2)}, u32[]{:S(2)}) collective-permute-start(bf16[216,600]{1,0:T(8,128)(2,1)S(1)} %shard_map.58.refs_0_), channel_id=1, source_target_pairs={{0,128},{64,192},{128,0},{192,64},{1,129},{65,193},{129,1},{193,65... | collective-permute-start | bytes 777608 | tf_op jit(solution)/shard_map/ppermute | solution.py:156
  97.3 13.4 %collective-permute-start.22 = (bf16[216,600]{1,0:T(8,128)(2,1)S(1)}, bf16[216,600]{1,0:T(8,128)(2,1)S(1)}, u32[]{:S(2)}, u32[]{:S(2)}) collective-permute-start(bf16[216,600]{1,0:T(8,128)(2,1)S(1)} %shard_map.58.refs_0_), channel_id=1, source_target_pairs={{0,192},{64,0},{128,64},{192,128},{1,193},{65,1},{129,65},{193,129... | collective-permute-start | bytes 777608 | tf_op jit(solution)/shard_map/ppermute | solution.py:156
  98.6 12.3 %collective-permute-start.25 = (bf16[216,600]{1,0:T(8,128)(2,1)S(1)}, bf16[216,600]{1,0:T(8,128)(2,1)S(1)}, u32[]{:S(2)}, u32[]{:S(2)}) collective-permute-start(bf16[216,600]{1,0:T(8,128)(2,1)S(1)} %shard_map.58.refs_0_), channel_id=1, source_target_pairs={{0,16},{16,0},{1,17},{17,1},{2,18},{18,2},{3,19},{19,3},{4,20},{20... | collective-permute-start | bytes 777608 | tf_op jit(solution)/shard_map/ppermute | solution.py:160
  102.8 8.1 %collective-permute-start.28 = (bf16[216,600]{1,0:T(8,128)(2,1)S(1)}, bf16[216,600]{1,0:T(8,128)(2,1)S(1)}, u32[]{:S(2)}, u32[]{:S(2)}) collective-permute-start(bf16[216,600]{1,0:T(8,128)(2,1)S(1)} %collective-permute-done.24.refs_3_), channel_id=1, source_target_pairs={{0,16},{16,0},{1,17},{17,1},{2,18},{18,2},{3,19},{19,3},{4,20},{20... | collective-permute-start | bytes 777608 | tf_op jit(solution)/shard_map/ppermute | solution.py:160
  105.9 5.1 %collective-permute-start.27 = (bf16[216,600]{1,0:T(8,128)(2,1)S(1)}, bf16[216,600]{1,0:T(8,128)(2,1)S(1)}, u32[]{:S(2)}, u32[]{:S(2)}) collective-permute-start(bf16[216,600]{1,0:T(8,128)(2,1)S(1)} %collective-permute-done.23.refs_2_), channel_id=1, source_target_pairs={{0,16},{16,0},{1,17},{17,1},{2,18},{18,2},{3,19},{19,3},{4,20},{20... | collective-permute-start | bytes 777608 | tf_op jit(solution)/shard_map/ppermute | solution.py:160
  110.7 1.6 %collective-permute-start.26 = (bf16[216,600]{1,0:T(8,128)(2,1)S(1)}, bf16[216,600]{1,0:T(8,128)(2,1)S(1)}, u32[]{:S(2)}, u32[]{:S(2)}) collective-permute-start(bf16[216,600]{1,0:T(8,128)(2,1)S(1)} %collective-permute-done.22.refs_1_), channel_id=1, source_target_pairs={{0,16},{16,0},{1,17},{17,1},{2,18},{18,2},{3,19},{19,3},{4,20},{20... | collective-permute-start | bytes 777608 | tf_op jit(solution)/shard_map/ppermute | solution.py:160
  (2 other events, 40.2 us)

commit v3 on v2

--- a/solution.py
+++ b/solution.py
@@ -6,6 +6,7 @@
 from jax import lax
 from jax.experimental import pallas as pl
 from jax.experimental.pallas import tpu as pltpu
+from jax.experimental.layout import Layout, with_layout_constraint
 from jax.sharding import Mesh
 from jax.sharding import PartitionSpec as P
 
@@ -25,6 +26,7 @@
 TRACE_ROW = BIN_DEV
 HALF = 208
 SPAN = 216
+SPLIT = (112, 104)
 HALF_BINS = BIN_DEV // 2
 FLOPS = 2_000_000_000
 
@@ -32,12 +34,6 @@
 f32 = jnp.float32
 bf16 = jnp.bfloat16
 VMEM = pl.BlockSpec(memory_space=pltpu.VMEM)
-
-
-def two_parts(values):
-    values = values.astype(np.float32)
-    upper = values.astype(bf16)
-    return upper, (values - upper.astype(np.float32)).astype(bf16)
 
 
 def tables():
@@ -48,17 +44,14 @@
     both = both * np.where(bins == 0, 1.0, 2.0)
     both = both.reshape(2, STEPS, BLOCKS, BIN_DEV)
     both = np.pad(both, ((0, 0), (0, HALF + SPAN - STEPS), (0, 0), (0, BIN_PAD - BIN_DEV)))
-    return np.stack(two_parts(both.reshape(2, HALF + SPAN, ROWS)), axis=1)
+    return both.reshape(2, HALF + SPAN, ROWS).astype(bf16)
 
 
 def dft_kernel(table, probes, out):
     probe = probes[lax.axis_index("x")]
     c = lax.axis_index("c")
     tn = (((0,), (0,)), ((), ()))
-    d = sum(
-        lax.dot_general(table[c, piece, :STEPS], probe, tn, preferred_element_type=f32)
-        for piece in range(2)
-    )
+    d = lax.dot_general(table[c, :STEPS], probe, tn, preferred_element_type=f32)
     row = lax.broadcasted_iota(jnp.int32, (ROWS, 1), 0)
     out[...] = (d * jnp.where(row == 0, 1.0, 0.5)).astype(bf16)
 
@@ -117,7 +110,7 @@
     return line[0, 0] + line[0, 1]
 
 
-def inverse_kernel(table, own, oth, out):
+def inverse_kernel(table, own, oth, early, late):
     c = lax.axis_index("c")
     row = lax.broadcasted_iota(jnp.int32, (ROWS, 128), 0)
     lane = lax.broadcasted_iota(jnp.int32, (ROWS, 128), 1)
@@ -128,32 +121,44 @@
     for ref, part in ((own, c), (oth, 1 - c)):
         v = ref[0].astype(f32) + ref[1].astype(f32)
         total = total + jnp.sum(jnp.where(marked, v[:, :128], 0.0))
-        v = v.astype(bf16)
-        for piece in range(2):
-            r = r + jnp.dot(table[part, piece, span], v, preferred_element_type=f32)
-    out[...] = r.astype(bf16)
-    out[SPAN - 1 : SPAN, :] = trace_line(total)
-
-
-def finish_kernel(*refs):
-    own, oth = refs[:XS], refs[XS : 2 * XS]
-    probes, out = refs[2 * XS :]
+        r = r + jnp.dot(table[part, span], v.astype(bf16), preferred_element_type=f32)
+    early[...] = r[: SPLIT[0]].astype(bf16)
+    late[...] = r[SPLIT[0] :].astype(bf16)
+    late[SPLIT[1] - 1 :, :] = trace_line(total)
+
+
+def assemble_kernel(*refs):
+    own, oth = refs[: 2 * XS], refs[2 * XS : 4 * XS]
+    out, noise = refs[4 * XS :]
     x, c = lax.axis_index("x"), lax.axis_index("c")
-    total = sum(read_trace(r, SPAN - 1) for r in own)
-    trace = total * (NOISE / (PROBES * SENSORS * STEPS))
+    total = sum(read_trace(r, SPLIT[1] - 1) for r in own[XS:])
+    noise[...] = jnp.full(noise.shape, total * (NOISE / (PROBES * SENSORS * STEPS)), f32)
+    rest = STEPS - 2 * HALF
+    first, second = SPLIT[0], HALF - SPLIT[0]
     for j in range(XS):
         p = lax.rem(x + j, XS)
-        for ref, half in ((own[j], c), (oth[j], 1 - c)):
-            rows = pl.ds(pl.multiple_of(half * HALF, 16), HALF)
-            out[p, rows, :] = (ref[0:HALF].astype(f32) + trace * probes[p, rows, :].astype(f32)).astype(bf16)
-        rest = STEPS - 2 * HALF
-        last = jnp.where(c == 1, own[j][HALF : HALF + rest].astype(f32), oth[j][HALF : HALF + rest].astype(f32))
-        out[p, 2 * HALF :, :] = (last + trace * probes[p, 2 * HALF :, :].astype(f32)).astype(bf16)
+        for refs_of, half in ((own, c), (oth, 1 - c)):
+            at = pl.multiple_of(half * HALF, 16)
+            out[p, pl.ds(at, first), :] = refs_of[j][...]
+            out[p, pl.ds(pl.multiple_of(at + first, 16), second), :] = refs_of[XS + j][:second]
+        tail = slice(second, second + rest)
+        out[p, 2 * HALF :, :] = jnp.where(c == 1, own[XS + j][tail], oth[XS + j][tail])
 
 
 def shift(value, axis, by):
     n = lax.axis_size(axis)
     return lax.ppermute(value, axis, [(i, (i + by) % n) for i in range(n)])
+
+
+def gather_ring(parts):
+    a, b = parts
+    a3 = shift(a, "x", 1)
+    b1 = shift(b, "x", -1)
+    b3 = shift(b, "x", 1)
+    a1 = shift(a, "x", -1)
+    a2 = shift(a3, "x", 1)
+    b2 = shift(b1, "x", -1)
+    return (a1, a2, a3), (b1, b2, b3)
 
 
 def swap_core(value):
@@ -179,7 +184,10 @@
     arrived = lax.all_to_all(spectra.reshape(BLOCKS, BIN_PAD, SENSORS), FREQ, 0, 0, tiled=True)
     arrived = arrived.transpose(1, 0, 2)[:BIN_DEV]
     parts = [arrived[:HALF_BINS], arrived[HALF_BINS:]]
-    away = [{j: shift(part, "x", -j) for j in (2, 1, 3)} for part in parts]
+    near = [[None] * (XS - 1) for _ in parts]
+    for at, part in enumerate(parts):
+        for j in (2, 1, 3):
+            near[at][j - 1] = shift(part, "x", -j)
     own_other = swap_core(arrived)
 
     prior = prior_var[None, :]
@@ -187,10 +195,9 @@
     trace = None
     totals = []
     for at, part in enumerate(parts):
-        near = [away[at][j] for j in range(1, XS)]
         w_own, w_oth, trace = call(
             functools.partial(middle_kernel, at * HALF_BINS),
-            [part, *near, own_other, *[swap_core(v) for v in near], map_real, map_imag, prior]
+            [part, *near[at], own_other, *[swap_core(v) for v in near[at]], map_real, map_imag, prior]
             + ([] if trace is None else [trace]),
             [block] * 2 + [((1, SENSORS), bf16) if at else (prior.shape, f32)],
             4,
@@ -210,12 +217,13 @@
     outgoing = outgoing.reshape(2 * BLOCKS, BIN_PAD, SENSORS)
     arrived = lax.all_to_all(outgoing, ("h",) + FREQ, 0, 0, tiled=True)
     pieces = [v.reshape(2, ROWS, SENSORS) for v in (arrived, swap_core(arrived))]
-    (part,) = call(inverse_kernel, (table, *pieces), [((SPAN, SENSORS), bf16)], 4)
-    away = {j: shift(part, "x", -j) for j in (2, 1, 3)}
-    own = [part] + [away[j] for j in range(1, XS)]
+    parts = call(inverse_kernel, (table, *pieces), [((n, SENSORS), bf16) for n in SPLIT], 4)
+    near = gather_ring(parts)
+    own = [v for at in range(2) for v in (parts[at], *near[at])]
     other = [swap_core(v) for v in own]
-    (out,) = call(finish_kernel, (*own, *other, probes.transpose(0, 2, 1)), [((XS, STEPS, SENSORS), bf16)], 4)
-    return out.transpose(0, 2, 1)
+    response, noise = call(assemble_kernel, (*own, *other), [((XS, STEPS, SENSORS), bf16), ((1, 128), f32)], 4)
+    response = with_layout_constraint(response.transpose(0, 2, 1), Layout((2, 0, 1))).astype(f32)
+    return (response + noise[0, 0] * probes.astype(f32)).astype(bf16)
 
 
 def solution(mesh):

time: 117 us -> 115 us (0.983)
  the two profiles are of different devices: /device:TPU:2 before, /device:TPU:1 now
where the time goes in v3:
time: 115 us
  blocking collectives  44.7 us (39%)
  starting transfers between devices  40.4 us (35%)
  waiting for transfers between devices  19 us (17%)
  Pallas kernels  5.73 us (5%)
  other arithmetic  3 us (3%)
  local copies, waits for them, and re-layouts  2.29 us (2%)
    all_to_all x1, blocking collectives, steps(): arrived = lax.all_to_all(outgoing, ('h',) + FREQ, 0, 0, tiled=True)  24.8 us
    ppermute x18, starting transfers between devices, swap_core(): return lax.ppermute(value, 'c', [(0, 1), (1, 0)])  22.7 us
    all_to_all x1, blocking collectives, steps(): lax.all_to_all(spectra.reshape(BLOCKS, BIN_PAD, SENSORS), FREQ, 0, 0, til...  19.9 us
    ppermute x18, starting transfers between devices, shift(): return lax.ppermute(value, axis, [(i, (i + by) % n) for i in range(n)])  17.8 us
    ppermute x18, waiting for transfers between devices, shift(): return lax.ppermute(value, axis, [(i, (i + by) % n) for i in range(n)])  14.7 us
    pallas_call x5, Pallas kernels, call(): pl.pallas_call(kernel, in_specs=[VMEM] * len(operands), out_specs=[VMEM]...  5.73 us
    ppermute x18, waiting for transfers between devices, swap_core(): return lax.ppermute(value, 'c', [(0, 1), (1, 0)])  4.2 us
    convert_element_type x1, other arithmetic, steps(): return (response + noise[0, 0] * probes.astype(f32)).astype(bf16)  2.52 us
  transfers between devices with their start and end apart: 36, of which 12 were waited for; matrix products, arithmetic and copies ran while one was open for 0% of the time, Pallas kernels for 2%

profile of v3, /device:TPU:1, one launch (start us, length us, event | category | flops | bytes accessed | tf_op | source)
XLA Modules:
  0.0 115.3 jit_solution(4299782011219052796)
XLA Ops:
  0.0 2.0 %copy.20 = bf16[4,600,420]{1,2,0:T(8,128)(2,1)S(1)} copy(bf16[4,600,420]{1,0,2:T(4,128)(2,1)} %param.5) | data formatting | bytes 4032000 | tf_op args[0]
  2.5 19.9 %all_to_all.10 = bf16[16,16,600]{2,1,0:T(8,128)(2,1)S(1)} all-to-all(bf16[16,16,600]{2,1,0:T(8,128)(2,1)S(1)} %bitcast.41), channel_id=1, replica_groups=mesh['x'=4,'h'=2,'c'=2,'zl'=4,'y'=4] {'zl','y'}, dimensions={0} | all-to-all | bytes 614400 | tf_op jit(solution)/shard_map/all_to_all | solution.py:184
  22.5 1.3 %collective-permute-start.2 = (bf16[7,16,600]{2,1,0:T(8,128)(2,1)S(1)}, bf16[7,16,600]{2,1,0:T(8,128)(2,1)S(1)}, u32[]{:S(2)}, u32[]{:S(2)}) collective-permute-start(bf16[7,16,600]{2,1,0:T(8,128)(2,1)S(1)} %get-tuple-element.35.refs_0_), channel_id=1, source_target_pairs={{0,64},{64,128},{128,192},{192,0},{1,65},{65,129},{129,193},{193,1... | collective-permute-start | bytes 403208 | tf_op jit(solution)/shard_map/ppermute | solution.py:150
  23.8 2.5 %collective-permute-start.1 = (bf16[7,16,600]{2,1,0:T(8,128)(2,1)S(1)}, bf16[7,16,600]{2,1,0:T(8,128)(2,1)S(1)}, u32[]{:S(2)}, u32[]{:S(2)}) collective-permute-start(bf16[7,16,600]{2,1,0:T(8,128)(2,1)S(1)} %get-tuple-element.35.refs_0_), channel_id=1, source_target_pairs={{0,128},{64,192},{128,0},{192,64},{1,129},{65,193},{129,1},{193,65... | collective-permute-start | bytes 403208 | tf_op jit(solution)/shard_map/ppermute | solution.py:150
  26.2 1.2 %collective-permute-start = (bf16[7,16,600]{2,1,0:T(8,128)(2,1)S(1)}, bf16[7,16,600]{2,1,0:T(8,128)(2,1)S(1)}, u32[]{:S(2)}, u32[]{:S(2)}) collective-permute-start(bf16[7,16,600]{2,1,0:T(8,128)(2,1)S(1)} %get-tuple-element.35.refs_0_), channel_id=1, source_target_pairs={{0,192},{64,0},{128,64},{192,128},{1,193},{65,1},{129,65},{193,129... | collective-permute-start | bytes 403208 | tf_op jit(solution)/shard_map/ppermute | solution.py:150
  28.6 4.6 %collective-permute-start.3 = (bf16[14,16,600]{2,1,0:T(8,128)(2,1)S(1)}, bf16[14,16,600]{2,1,0:T(8,128)(2,1)S(1)}, u32[]{:S(2)}, u32[]{:S(2)}) collective-permute-start(bf16[14,16,600]{2,1,0:T(8,128)(2,1)S(1)} %slice.83), channel_id=1, source_target_pairs={{0,16},{16,0},{1,17},{17,1},{2,18},{18,2},{3,19},{19,3},{4,20},{20... | collective-permute-start | bytes 806408 | tf_op jit(solution)/shard_map/ppermute | solution.py:165
  33.8 2.9 %collective-permute-start.6 = (bf16[7,16,600]{2,1,0:T(8,128)(2,1)S(1)}, bf16[7,16,600]{2,1,0:T(8,128)(2,1)S(1)}, u32[]{:S(2)}, u32[]{:S(2)}) collective-permute-start(bf16[7,16,600]{2,1,0:T(8,128)(2,1)S(1)} %collective-permute-done.2.refs_3_), channel_id=1, source_target_pairs={{0,16},{16,0},{1,17},{17,1},{2,18},{18,2},{3,19},{19,3},{4,20},{20... | collective-permute-start | bytes 403208 | tf_op jit(solution)/shard_map/ppermute | solution.py:165
  36.7 1.9 %collective-permute-start.5 = (bf16[7,16,600]{2,1,0:T(8,128)(2,1)S(1)}, bf16[7,16,600]{2,1,0:T(8,128)(2,1)S(1)}, u32[]{:S(2)}, u32[]{:S(2)}) collective-permute-start(bf16[7,16,600]{2,1,0:T(8,128)(2,1)S(1)} %collective-permute-done.1.refs_2_), channel_id=1, source_target_pairs={{0,16},{16,0},{1,17},{17,1},{2,18},{18,2},{3,19},{19,3},{4,20},{20... | collective-permute-start | bytes 403208 | tf_op jit(solution)/shard_map/ppermute | solution.py:165
  38.6 1.5 %collective-permute-start.4 = (bf16[7,16,600]{2,1,0:T(8,128)(2,1)S(1)}, bf16[7,16,600]{2,1,0:T(8,128)(2,1)S(1)}, u32[]{:S(2)}, u32[]{:S(2)}) collective-permute-start(bf16[7,16,600]{2,1,0:T(8,128)(2,1)S(1)} %collective-permute-done.refs_1_), channel_id=1, source_target_pairs={{0,16},{16,0},{1,17},{17,1},{2,18},{18,2},{3,19},{19,3},{4,20},{20... | collective-permute-start | bytes 403208 | tf_op jit(solution)/shard_map/ppermute | solution.py:165
  40.2 1.6 %collective-permute-start.16 = (bf16[7,16,600]{2,1,0:T(8,128)(2,1)S(1)}, bf16[7,16,600]{2,1,0:T(8,128)(2,1)S(1)}, u32[]{:S(2)}, u32[]{:S(2)}) collective-permute-start(bf16[7,16,600]{2,1,0:T(8,128)(2,1)S(1)} %collective-permute-done.13.refs_3_), channel_id=1, source_target_pairs={{0,16},{16,0},{1,17},{17,1},{2,18},{18,2},{3,19},{19,3},{4,20},{20... | collective-permute-start | bytes 403208 | tf_op jit(solution)/shard_map/ppermute | solution.py:165
  42.4 2.4 %shard_map.56 = (bf16[4,7,16,600]{3,2,1,0:T(8,128)(2,1)S(1)}, bf16[4,7,16,600]{3,2,1,0:T(8,128)(2,1)S(1)}, f32[1,256]{1,0:T(1,128)S(1)}) custom-call(bf16[7,16,600]{2,1,0:T(8,128)(2,1)S(1)} %get-tuple-element.35.refs_0_, bf16[7,16,600]{2,1,0:T(8,128)(2,1)S(1)} %collective-permute-done.refs_1_, bf16[7,16,600]{2,1,0:T(8,128)(2,1)S(1)} %collective-permute-done.1.refs_2_, ...), custom_call_target="tpu_custom_call" | custom-call | flops 2000000000 | tf_op jit(solution)/shard_map/pallas_call | solution.py:169
  44.7 2.3 %shard_map.57 = (bf16[4,7,16,600]{3,2,1,0:T(8,128)(2,1)S(1)}, bf16[4,7,16,600]{3,2,1,0:T(8,128)(2,1)S(1)}, bf16[1,600]{1,0:T(2,128)(2,1)S(1)}) custom-call(bf16[7,16,600]{2,1,0:T(8,128)(2,1)S(1)} %get-tuple-element.36.refs_0_, bf16[7,16,600]{2,1,0:T(8,128)(2,1)S(1)} %collective-permute-done.11.refs_1_, ...), custom_call_target="tpu_custom_call" | custom-call | flops 2000000000 | tf_op jit(solution)/shard_map/pallas_call | solution.py:169
  47.7 1.5 %collective-permute-done.17 = bf16[4,7,16,600]{3,2,1,0:T(8,128)(2,1)S(1)} collective-permute-done((bf16[4,7,16,600]{3,2,1,0:T(8,128)(2,1)S(1)}, bf16[4,7,16,600]{3,2,1,0:T(8,128)(2,1)S(1)}, u32[]{:S(2)}, u32[]{:S(2)}) %collective-permute-start.17) | collective-permute-done | bytes 537632 | tf_op jit(solution)/shard_map/ppermute | solution.py:165
  49.3 1.2 %collective-permute-start.18 = (bf16[7,16,600]{2,1,0:T(8,128)(2,1)S(1)}, bf16[7,16,600]{2,1,0:T(8,128)(2,1)S(1)}, u32[]{:S(2)}, u32[]{:S(2)}) collective-permute-start(bf16[7,16,600]{2,1,0:T(8,128)(2,1)S(1)} %get-tuple-element.32), channel_id=1, source_target_pairs={{0,128},{64,192},{128,0},{192,64},{1,129},{65,193},{129,1},{193,65... | collective-permute-start | bytes 403208 | tf_op jit(solution)/shard_map/ppermute | solution.py:150
  50.5 1.5 %collective-permute-start.20 = (bf16[7,16,600]{2,1,0:T(8,128)(2,1)S(1)}, bf16[7,16,600]{2,1,0:T(8,128)(2,1)S(1)}, u32[]{:S(2)}, u32[]{:S(2)}) collective-permute-start(bf16[7,16,600]{2,1,0:T(8,128)(2,1)S(1)} %get-tuple-element.33), channel_id=1, source_target_pairs={{0,192},{64,0},{128,64},{192,128},{1,193},{65,1},{129,65},{193,129... | collective-permute-start | bytes 403208 | tf_op jit(solution)/shard_map/ppermute | solution.py:150
  52.1 1.9 %collective-permute-start.8 = (bf16[7,16,600]{2,1,0:T(8,128)(2,1)S(1)}, bf16[7,16,600]{2,1,0:T(8,128)(2,1)S(1)}, u32[]{:S(2)}, u32[]{:S(2)}) collective-permute-start(bf16[7,16,600]{2,1,0:T(8,128)(2,1)S(1)} %get-tuple-element.29), channel_id=1, source_target_pairs={{0,128},{64,192},{128,0},{192,64},{1,129},{65,193},{129,1},{193,65... | collective-permute-start | bytes 403208 | tf_op jit(solution)/shard_map/ppermute | solution.py:150
  56.1 1.4 %collective-permute-done.20 = bf16[7,16,600]{2,1,0:T(8,128)(2,1)S(1)} collective-permute-done((bf16[7,16,600]{2,1,0:T(8,128)(2,1)S(1)}, bf16[7,16,600]{2,1,0:T(8,128)(2,1)S(1)}, u32[]{:S(2)}, u32[]{:S(2)}) %collective-permute-start.20) | collective-permute-done | bytes 134432 | tf_op jit(solution)/shard_map/ppermute | solution.py:150
  57.5 1.7 %collective-permute-done.19 = bf16[7,16,600]{2,1,0:T(8,128)(2,1)S(1)} collective-permute-done((bf16[7,16,600]{2,1,0:T(8,128)(2,1)S(1)}, bf16[7,16,600]{2,1,0:T(8,128)(2,1)S(1)}, u32[]{:S(2)}, u32[]{:S(2)}) %collective-permute-start.19) | collective-permute-done | bytes 134432 | tf_op jit(solution)/shard_map/ppermute | solution.py:150
  59.3 2.8 %collective-permute-done.8 = bf16[7,16,600]{2,1,0:T(8,128)(2,1)S(1)} collective-permute-done((bf16[7,16,600]{2,1,0:T(8,128)(2,1)S(1)}, bf16[7,16,600]{2,1,0:T(8,128)(2,1)S(1)}, u32[]{:S(2)}, u32[]{:S(2)}) %collective-permute-start.8) | collective-permute-done | bytes 134432 | tf_op jit(solution)/shard_map/ppermute | solution.py:150
  62.1 1.6 %collective-permute-done.10 = bf16[7,16,600]{2,1,0:T(8,128)(2,1)S(1)} collective-permute-done((bf16[7,16,600]{2,1,0:T(8,128)(2,1)S(1)}, bf16[7,16,600]{2,1,0:T(8,128)(2,1)S(1)}, u32[]{:S(2)}, u32[]{:S(2)}) %collective-permute-start.10) | collective-permute-done | bytes 134432 | tf_op jit(solution)/shard_map/ppermute | solution.py:150
  63.7 1.8 %collective-permute-done.9 = bf16[7,16,600]{2,1,0:T(8,128)(2,1)S(1)} collective-permute-done((bf16[7,16,600]{2,1,0:T(8,128)(2,1)S(1)}, bf16[7,16,600]{2,1,0:T(8,128)(2,1)S(1)}, u32[]{:S(2)}, u32[]{:S(2)}) %collective-permute-start.9) | collective-permute-done | bytes 134432 | tf_op jit(solution)/shard_map/ppermute | solution.py:150
  65.9 24.8 %all_to_all.11 = bf16[32,16,600]{2,1,0:T(8,128)(2,1)S(1)} all-to-all(bf16[32,16,600]{2,1,0:T(8,128)(2,1)S(1)} %bitcast.46), channel_id=1, replica_groups=mesh['x'=4,'h'=2,'c'=2,'zl'=4,'y'=4] {'h','zl','y'}, dimensions={0} | all-to-all | bytes 1228800 | tf_op jit(solution)/shard_map/all_to_all | solution.py:218
  90.7 2.5 %collective-permute-start.21 = (bf16[32,16,600]{2,1,0:T(8,128)(2,1)S(1)}, bf16[32,16,600]{2,1,0:T(8,128)(2,1)S(1)}, u32[]{:S(2)}, u32[]{:S(2)}) collective-permute-start(bf16[32,16,600]{2,1,0:T(8,128)(2,1)S(1)} %all_to_all.11), channel_id=1, source_target_pairs={{0,16},{16,0},{1,17},{17,1},{2,18},{18,2},{3,19},{19,3},{4,20},{20... | collective-permute-start | bytes 1843208 | tf_op jit(solution)/shard_map/ppermute | solution.py:165
  93.2 1.7 %collective-permute-done.21 = bf16[32,16,600]{2,1,0:T(8,128)(2,1)S(1)} collective-permute-done((bf16[32,16,600]{2,1,0:T(8,128)(2,1)S(1)}, bf16[32,16,600]{2,1,0:T(8,128)(2,1)S(1)}, u32[]{:S(2)}, u32[]{:S(2)}) %collective-permute-start.21) | collective-permute-done | bytes 614432 | tf_op jit(solution)/shard_map/ppermute | solution.py:165
  96.1 1.1 collective-permute-start.27
  97.2 1.6 %collective-permute-start.25 = (bf16[104,600]{1,0:T(8,128)(2,1)S(1)}, bf16[104,600]{1,0:T(8,128)(2,1)S(1)}, u32[]{:S(2)}, u32[]{:S(2)}) collective-permute-start(bf16[104,600]{1,0:T(8,128)(2,1)S(1)} %get-tuple-element.25.refs_4_), channel_id=1, source_target_pairs={{0,192},{64,0},{128,64},{192,128},{1,193},{65,1},{129,65},{193,129... | collective-permute-start | bytes 374408 | tf_op jit(solution)/shard_map/ppermute | solution.py:150
  99.5 1.3 %collective-permute-start.22 = (bf16[112,600]{1,0:T(8,128)(2,1)S(1)}, bf16[112,600]{1,0:T(8,128)(2,1)S(1)}, u32[]{:S(2)}, u32[]{:S(2)}) collective-permute-start(bf16[112,600]{1,0:T(8,128)(2,1)S(1)} %get-tuple-element.24.refs_0_), channel_id=1, source_target_pairs={{0,192},{64,0},{128,64},{192,128},{1,193},{65,1},{129,65},{193,129... | collective-permute-start | bytes 403208 | tf_op jit(solution)/shard_map/ppermute | solution.py:150
  101.6 2.8 %collective-permute-done.27.refs_7_ = bf16[104,600]{1,0:T(8,128)(2,1)S(1)} collective-permute-done((bf16[104,600]{1,0:T(8,128)(2,1)S(1)}, bf16[104,600]{1,0:T(8,128)(2,1)S(1)}, u32[]{:S(2)}, u32[]{:S(2)}) %collective-permute-start.27) | collective-permute-done | bytes 124832 | tf_op jit(solution)/shard_map/ppermute | solution.py:150
  104.4 1.2 %collective-permute-start.35 = (bf16[104,600]{1,0:T(8,128)(2,1)S(1)}, bf16[104,600]{1,0:T(8,128)(2,1)S(1)}, u32[]{:S(2)}, u32[]{:S(2)}) collective-permute-start(bf16[104,600]{1,0:T(8,128)(2,1)S(1)} %collective-permute-done.27.refs_7_), channel_id=1, source_target_pairs={{0,16},{16,0},{1,17},{17,1},{2,18},{18,2},{3,19},{19,3},{4,20},{20... | collective-permute-start | bytes 374408 | tf_op jit(solution)/shard_map/ppermute | solution.py:165
  105.6 1.3 %collective-permute-start.26 = (bf16[104,600]{1,0:T(8,128)(2,1)S(1)}, bf16[104,600]{1,0:T(8,128)(2,1)S(1)}, u32[]{:S(2)}, u32[]{:S(2)}) collective-permute-start(bf16[104,600]{1,0:T(8,128)(2,1)S(1)} %collective-permute-done.25.refs_5_), channel_id=1, source_target_pairs={{0,192},{64,0},{128,64},{192,128},{1,193},{65,1},{129,65},{193,129... | collective-permute-start | bytes 374408 | tf_op jit(solution)/shard_map/ppermute | solution.py:150
  107.4 2.5 %collective-permute-start.30 = (bf16[112,600]{1,0:T(8,128)(2,1)S(1)}, bf16[112,600]{1,0:T(8,128)(2,1)S(1)}, u32[]{:S(2)}, u32[]{:S(2)}) collective-permute-start(bf16[112,600]{1,0:T(8,128)(2,1)S(1)} %collective-permute-done.24.refs_2_), channel_id=1, source_target_pairs={{0,16},{16,0},{1,17},{17,1},{2,18},{18,2},{3,19},{19,3},{4,20},{20... | collective-permute-start | bytes 403208 | tf_op jit(solution)/shard_map/ppermute | solution.py:165
  112.8 2.5 %add_convert_fusion = bf16[4,600,420]{1,0,2:T(4,128)(2,1)} fusion(bf16[4,600,420]{1,0,2:T(4,128)(2,1)S(1)} %copy-done.4, bf16[4,420,600]{2,1,0:T(8,128)(2,1)S(1)} %get-tuple-element.26, f32[]{:T(128)S(1)} %bitcast.45), kind=kLoop, calls=%fused_computation | loop fusion | flops 5040000 | bytes 6048004 | tf_op jit(solution)/shard_map/convert_element_type | solution.py:226
  (71 shorter events, 12.2 us)
Async XLA Ops:
  22.5 6.1 %collective-permute-start.2 = (bf16[7,16,600]{2,1,0:T(8,128)(2,1)S(1)}, bf16[7,16,600]{2,1,0:T(8,128)(2,1)S(1)}, u32[]{:S(2)}, u32[]{:S(2)}) collective-permute-start(bf16[7,16,600]{2,1,0:T(8,128)(2,1)S(1)} %get-tuple-element.35.refs_0_), channel_id=1, source_target_pairs={{0,64},{64,128},{128,192},{192,0},{1,65},{65,129},{129,193},{193,1... | collective-permute-start | bytes 403208 | tf_op jit(solution)/shard_map/ppermute | solution.py:150
  23.8 9.5 %collective-permute-start.1 = (bf16[7,16,600]{2,1,0:T(8,128)(2,1)S(1)}, bf16[7,16,600]{2,1,0:T(8,128)(2,1)S(1)}, u32[]{:S(2)}, u32[]{:S(2)}) collective-permute-start(bf16[7,16,600]{2,1,0:T(8,128)(2,1)S(1)} %get-tuple-element.35.refs_0_), channel_id=1, source_target_pairs={{0,128},{64,192},{128,0},{192,64},{1,129},{65,193},{129,1},{193,65... | collective-permute-start | bytes 403208 | tf_op jit(solution)/shard_map/ppermute | solution.py:150
  26.2 7.6 %collective-permute-start = (bf16[7,16,600]{2,1,0:T(8,128)(2,1)S(1)}, bf16[7,16,600]{2,1,0:T(8,128)(2,1)S(1)}, u32[]{:S(2)}, u32[]{:S(2)}) collective-permute-start(bf16[7,16,600]{2,1,0:T(8,128)(2,1)S(1)} %get-tuple-element.35.refs_0_), channel_id=1, source_target_pairs={{0,192},{64,0},{128,64},{192,128},{1,193},{65,1},{129,65},{193,129... | collective-permute-start | bytes 403208 | tf_op jit(solution)/shard_map/ppermute | solution.py:150
  27.4 9.3 %collective-permute-start.13 = (bf16[7,16,600]{2,1,0:T(8,128)(2,1)S(1)}, bf16[7,16,600]{2,1,0:T(8,128)(2,1)S(1)}, u32[]{:S(2)}, u32[]{:S(2)}) collective-permute-start(bf16[7,16,600]{2,1,0:T(8,128)(2,1)S(1)} %get-tuple-element.36.refs_0_), channel_id=1, source_target_pairs={{0,64},{64,128},{128,192},{192,0},{1,65},{65,129},{129,193},{193,1... | collective-permute-start | bytes 403208 | tf_op jit(solution)/shard_map/ppermute | solution.py:150
  27.7 10.9 %collective-permute-start.12 = (bf16[7,16,600]{2,1,0:T(8,128)(2,1)S(1)}, bf16[7,16,600]{2,1,0:T(8,128)(2,1)S(1)}, u32[]{:S(2)}, u32[]{:S(2)}) collective-permute-start(bf16[7,16,600]{2,1,0:T(8,128)(2,1)S(1)} %get-tuple-element.36.refs_0_), channel_id=1, source_target_pairs={{0,128},{64,192},{128,0},{192,64},{1,129},{65,193},{129,1},{193,65... | collective-permute-start | bytes 403208 | tf_op jit(solution)/shard_map/ppermute | solution.py:150
  28.6 13.7 %collective-permute-start.3 = (bf16[14,16,600]{2,1,0:T(8,128)(2,1)S(1)}, bf16[14,16,600]{2,1,0:T(8,128)(2,1)S(1)}, u32[]{:S(2)}, u32[]{:S(2)}) collective-permute-start(bf16[14,16,600]{2,1,0:T(8,128)(2,1)S(1)} %slice.83), channel_id=1, source_target_pairs={{0,16},{16,0},{1,17},{17,1},{2,18},{18,2},{3,19},{19,3},{4,20},{20... | collective-permute-start | bytes 806408 | tf_op jit(solution)/shard_map/ppermute | solution.py:165
  33.2 6.9 %collective-permute-start.11 = (bf16[7,16,600]{2,1,0:T(8,128)(2,1)S(1)}, bf16[7,16,600]{2,1,0:T(8,128)(2,1)S(1)}, u32[]{:S(2)}, u32[]{:S(2)}) collective-permute-start(bf16[7,16,600]{2,1,0:T(8,128)(2,1)S(1)} %get-tuple-element.36.refs_0_), channel_id=1, source_target_pairs={{0,192},{64,0},{128,64},{192,128},{1,193},{65,1},{129,65},{193,129... | collective-permute-start | bytes 403208 | tf_op jit(solution)/shard_map/ppermute | solution.py:150
  33.8 8.0 %collective-permute-start.6 = (bf16[7,16,600]{2,1,0:T(8,128)(2,1)S(1)}, bf16[7,16,600]{2,1,0:T(8,128)(2,1)S(1)}, u32[]{:S(2)}, u32[]{:S(2)}) collective-permute-start(bf16[7,16,600]{2,1,0:T(8,128)(2,1)S(1)} %collective-permute-done.2.refs_3_), channel_id=1, source_target_pairs={{0,16},{16,0},{1,17},{17,1},{2,18},{18,2},{3,19},{19,3},{4,20},{20... | collective-permute-start | bytes 403208 | tf_op jit(solution)/shard_map/ppermute | solution.py:165
  36.7 5.1 %collective-permute-start.5 = (bf16[7,16,600]{2,1,0:T(8,128)(2,1)S(1)}, bf16[7,16,600]{2,1,0:T(8,128)(2,1)S(1)}, u32[]{:S(2)}, u32[]{:S(2)}) collective-permute-start(bf16[7,16,600]{2,1,0:T(8,128)(2,1)S(1)} %collective-permute-done.1.refs_2_), channel_id=1, source_target_pairs={{0,16},{16,0},{1,17},{17,1},{2,18},{18,2},{3,19},{19,3},{4,20},{20... | collective-permute-start | bytes 403208 | tf_op jit(solution)/shard_map/ppermute | solution.py:165
  38.6 3.7 %collective-permute-start.4 = (bf16[7,16,600]{2,1,0:T(8,128)(2,1)S(1)}, bf16[7,16,600]{2,1,0:T(8,128)(2,1)S(1)}, u32[]{:S(2)}, u32[]{:S(2)}) collective-permute-start(bf16[7,16,600]{2,1,0:T(8,128)(2,1)S(1)} %collective-permute-done.refs_1_), channel_id=1, source_target_pairs={{0,16},{16,0},{1,17},{17,1},{2,18},{18,2},{3,19},{19,3},{4,20},{20... | collective-permute-start | bytes 403208 | tf_op jit(solution)/shard_map/ppermute | solution.py:165
  40.2 4.6 %collective-permute-start.16 = (bf16[7,16,600]{2,1,0:T(8,128)(2,1)S(1)}, bf16[7,16,600]{2,1,0:T(8,128)(2,1)S(1)}, u32[]{:S(2)}, u32[]{:S(2)}) collective-permute-start(bf16[7,16,600]{2,1,0:T(8,128)(2,1)S(1)} %collective-permute-done.13.refs_3_), channel_id=1, source_target_pairs={{0,16},{16,0},{1,17},{17,1},{2,18},{18,2},{3,19},{19,3},{4,20},{20... | collective-permute-start | bytes 403208 | tf_op jit(solution)/shard_map/ppermute | solution.py:165
  41.8 2.9 %collective-permute-start.14 = (bf16[7,16,600]{2,1,0:T(8,128)(2,1)S(1)}, bf16[7,16,600]{2,1,0:T(8,128)(2,1)S(1)}, u32[]{:S(2)}, u32[]{:S(2)}) collective-permute-start(bf16[7,16,600]{2,1,0:T(8,128)(2,1)S(1)} %collective-permute-done.11.refs_1_), channel_id=1, source_target_pairs={{0,16},{16,0},{1,17},{17,1},{2,18},{18,2},{3,19},{19,3},{4,20},{20... | collective-permute-start | bytes 403208 | tf_op jit(solution)/shard_map/ppermute | solution.py:165
  47.5 4.5 %collective-permute-start.7 = (bf16[4,7,16,600]{3,2,1,0:T(8,128)(2,1)S(1)}, bf16[4,7,16,600]{3,2,1,0:T(8,128)(2,1)S(1)}, u32[]{:S(2)}, u32[]{:S(2)}) collective-permute-start(bf16[4,7,16,600]{3,2,1,0:T(8,128)(2,1)S(1)} %get-tuple-element.19), channel_id=1, source_target_pairs={{0,16},{16,0},{1,17},{17,1},{2,18},{18,2},{3,19},{19,3},{4,20},{20... | collective-permute-start | bytes 1612808 | tf_op jit(solution)/shard_map/ppermute | solution.py:165
  49.3 6.6 %collective-permute-start.18 = (bf16[7,16,600]{2,1,0:T(8,128)(2,1)S(1)}, bf16[7,16,600]{2,1,0:T(8,128)(2,1)S(1)}, u32[]{:S(2)}, u32[]{:S(2)}) collective-permute-start(bf16[7,16,600]{2,1,0:T(8,128)(2,1)S(1)} %get-tuple-element.32), channel_id=1, source_target_pairs={{0,128},{64,192},{128,0},{192,64},{1,129},{65,193},{129,1},{193,65... | collective-permute-start | bytes 403208 | tf_op jit(solution)/shard_map/ppermute | solution.py:150
  50.5 7.0 %collective-permute-start.20 = (bf16[7,16,600]{2,1,0:T(8,128)(2,1)S(1)}, bf16[7,16,600]{2,1,0:T(8,128)(2,1)S(1)}, u32[]{:S(2)}, u32[]{:S(2)}) collective-permute-start(bf16[7,16,600]{2,1,0:T(8,128)(2,1)S(1)} %get-tuple-element.33), channel_id=1, source_target_pairs={{0,192},{64,0},{128,64},{192,128},{1,193},{65,1},{129,65},{193,129... | collective-permute-start | bytes 403208 | tf_op jit(solution)/shard_map/ppermute | solution.py:150
  51.9 7.3 %collective-permute-start.19 = (bf16[7,16,600]{2,1,0:T(8,128)(2,1)S(1)}, bf16[7,16,600]{2,1,0:T(8,128)(2,1)S(1)}, u32[]{:S(2)}, u32[]{:S(2)}) collective-permute-start(bf16[7,16,600]{2,1,0:T(8,128)(2,1)S(1)} %get-tuple-element.34), channel_id=1, source_target_pairs={{0,64},{64,128},{128,192},{192,0},{1,65},{65,129},{129,193},{193,1... | collective-permute-start | bytes 403208 | tf_op jit(solution)/shard_map/ppermute | solution.py:150
  52.1 10.0 %collective-permute-start.8 = (bf16[7,16,600]{2,1,0:T(8,128)(2,1)S(1)}, bf16[7,16,600]{2,1,0:T(8,128)(2,1)S(1)}, u32[]{:S(2)}, u32[]{:S(2)}) collective-permute-start(bf16[7,16,600]{2,1,0:T(8,128)(2,1)S(1)} %get-tuple-element.29), channel_id=1, source_target_pairs={{0,128},{64,192},{128,0},{192,64},{1,129},{65,193},{129,1},{193,65... | collective-permute-start | bytes 403208 | tf_op jit(solution)/shard_map/ppermute | solution.py:150
  54.0 9.7 %collective-permute-start.10 = (bf16[7,16,600]{2,1,0:T(8,128)(2,1)S(1)}, bf16[7,16,600]{2,1,0:T(8,128)(2,1)S(1)}, u32[]{:S(2)}, u32[]{:S(2)}) collective-permute-start(bf16[7,16,600]{2,1,0:T(8,128)(2,1)S(1)} %get-tuple-element.30), channel_id=1, source_target_pairs={{0,192},{64,0},{128,64},{192,128},{1,193},{65,1},{129,65},{193,129... | collective-permute-start | bytes 403208 | tf_op jit(solution)/shard_map/ppermute | solution.py:150
  55.9 9.6 %collective-permute-start.9 = (bf16[7,16,600]{2,1,0:T(8,128)(2,1)S(1)}, bf16[7,16,600]{2,1,0:T(8,128)(2,1)S(1)}, u32[]{:S(2)}, u32[]{:S(2)}) collective-permute-start(bf16[7,16,600]{2,1,0:T(8,128)(2,1)S(1)} %get-tuple-element.31), channel_id=1, source_target_pairs={{0,64},{64,128},{128,192},{192,0},{1,65},{65,129},{129,193},{193,1... | collective-permute-start | bytes 403208 | tf_op jit(solution)/shard_map/ppermute | solution.py:150
  90.7 4.2 %collective-permute-start.21 = (bf16[32,16,600]{2,1,0:T(8,128)(2,1)S(1)}, bf16[32,16,600]{2,1,0:T(8,128)(2,1)S(1)}, u32[]{:S(2)}, u32[]{:S(2)}) collective-permute-start(bf16[32,16,600]{2,1,0:T(8,128)(2,1)S(1)} %all_to_all.11), channel_id=1, source_target_pairs={{0,16},{16,0},{1,17},{17,1},{2,18},{18,2},{3,19},{19,3},{4,20},{20... | collective-permute-start | bytes 1843208 | tf_op jit(solution)/shard_map/ppermute | solution.py:165
  95.3 6.2 %collective-permute-start.23 = (bf16[112,600]{1,0:T(8,128)(2,1)S(1)}, bf16[112,600]{1,0:T(8,128)(2,1)S(1)}, u32[]{:S(2)}, u32[]{:S(2)}) collective-permute-start(bf16[112,600]{1,0:T(8,128)(2,1)S(1)} %get-tuple-element.24.refs_0_), channel_id=1, source_target_pairs={{0,64},{64,128},{128,192},{192,0},{1,65},{65,129},{129,193},{193,1... | collective-permute-start | bytes 403208 | tf_op jit(solution)/shard_map/ppermute | solution.py:150
  95.4 4.1 %collective-permute-start.32 = (bf16[104,600]{1,0:T(8,128)(2,1)S(1)}, bf16[104,600]{1,0:T(8,128)(2,1)S(1)}, u32[]{:S(2)}, u32[]{:S(2)}) collective-permute-start(bf16[104,600]{1,0:T(8,128)(2,1)S(1)} %get-tuple-element.25.refs_4_), channel_id=1, source_target_pairs={{0,16},{16,0},{1,17},{17,1},{2,18},{18,2},{3,19},{19,3},{4,20},{20... | collective-permute-start | bytes 374408 | tf_op jit(solution)/shard_map/ppermute | solution.py:165
  96.1 8.3 %collective-permute-start.27 = (bf16[104,600]{1,0:T(8,128)(2,1)S(1)}, bf16[104,600]{1,0:T(8,128)(2,1)S(1)}, u32[]{:S(2)}, u32[]{:S(2)}) collective-permute-start(bf16[104,600]{1,0:T(8,128)(2,1)S(1)} %get-tuple-element.25.refs_4_), channel_id=1, source_target_pairs={{0,64},{64,128},{128,192},{192,0},{1,65},{65,129},{129,193},{193,1... | collective-permute-start | bytes 374408 | tf_op jit(solution)/shard_map/ppermute | solution.py:150
  97.2 8.5 %collective-permute-start.25 = (bf16[104,600]{1,0:T(8,128)(2,1)S(1)}, bf16[104,600]{1,0:T(8,128)(2,1)S(1)}, u32[]{:S(2)}, u32[]{:S(2)}) collective-permute-start(bf16[104,600]{1,0:T(8,128)(2,1)S(1)} %get-tuple-element.25.refs_4_), channel_id=1, source_target_pairs={{0,192},{64,0},{128,64},{192,128},{1,193},{65,1},{129,65},{193,129... | collective-permute-start | bytes 374408 | tf_op jit(solution)/shard_map/ppermute | solution.py:150
  98.8 8.2 %collective-permute-start.28 = (bf16[112,600]{1,0:T(8,128)(2,1)S(1)}, bf16[112,600]{1,0:T(8,128)(2,1)S(1)}, u32[]{:S(2)}, u32[]{:S(2)}) collective-permute-start(bf16[112,600]{1,0:T(8,128)(2,1)S(1)} %get-tuple-element.24.refs_0_), channel_id=1, source_target_pairs={{0,16},{16,0},{1,17},{17,1},{2,18},{18,2},{3,19},{19,3},{4,20},{20... | collective-permute-start | bytes 403208 | tf_op jit(solution)/shard_map/ppermute | solution.py:165
  99.5 7.7 %collective-permute-start.22 = (bf16[112,600]{1,0:T(8,128)(2,1)S(1)}, bf16[112,600]{1,0:T(8,128)(2,1)S(1)}, u32[]{:S(2)}, u32[]{:S(2)}) collective-permute-start(bf16[112,600]{1,0:T(8,128)(2,1)S(1)} %get-tuple-element.24.refs_0_), channel_id=1, source_target_pairs={{0,192},{64,0},{128,64},{192,128},{1,193},{65,1},{129,65},{193,129... | collective-permute-start | bytes 403208 | tf_op jit(solution)/shard_map/ppermute | solution.py:150
  101.5 5.9 %collective-permute-start.24 = (bf16[112,600]{1,0:T(8,128)(2,1)S(1)}, bf16[112,600]{1,0:T(8,128)(2,1)S(1)}, u32[]{:S(2)}, u32[]{:S(2)}) collective-permute-start(bf16[112,600]{1,0:T(8,128)(2,1)S(1)} %collective-permute-done.23.refs_3_), channel_id=1, source_target_pairs={{0,64},{64,128},{128,192},{192,0},{1,65},{65,129},{129,193},{193,1... | collective-permute-start | bytes 403208 | tf_op jit(solution)/shard_map/ppermute | solution.py:150
  104.4 5.5 %collective-permute-start.35 = (bf16[104,600]{1,0:T(8,128)(2,1)S(1)}, bf16[104,600]{1,0:T(8,128)(2,1)S(1)}, u32[]{:S(2)}, u32[]{:S(2)}) collective-permute-start(bf16[104,600]{1,0:T(8,128)(2,1)S(1)} %collective-permute-done.27.refs_7_), channel_id=1, source_target_pairs={{0,16},{16,0},{1,17},{17,1},{2,18},{18,2},{3,19},{19,3},{4,20},{20... | collective-permute-start | bytes 374408 | tf_op jit(solution)/shard_map/ppermute | solution.py:165
  105.6 5.1 %collective-permute-start.26 = (bf16[104,600]{1,0:T(8,128)(2,1)S(1)}, bf16[104,600]{1,0:T(8,128)(2,1)S(1)}, u32[]{:S(2)}, u32[]{:S(2)}) collective-permute-start(bf16[104,600]{1,0:T(8,128)(2,1)S(1)} %collective-permute-done.25.refs_5_), channel_id=1, source_target_pairs={{0,192},{64,0},{128,64},{192,128},{1,193},{65,1},{129,65},{193,129... | collective-permute-start | bytes 374408 | tf_op jit(solution)/shard_map/ppermute | solution.py:150
  106.9 4.7 %collective-permute-start.31 = (bf16[112,600]{1,0:T(8,128)(2,1)S(1)}, bf16[112,600]{1,0:T(8,128)(2,1)S(1)}, u32[]{:S(2)}, u32[]{:S(2)}) collective-permute-start(bf16[112,600]{1,0:T(8,128)(2,1)S(1)} %collective-permute-done.23.refs_3_), channel_id=1, source_target_pairs={{0,16},{16,0},{1,17},{17,1},{2,18},{18,2},{3,19},{19,3},{4,20},{20... | collective-permute-start | bytes 403208 | tf_op jit(solution)/shard_map/ppermute | solution.py:165
  107.2 4.4 %collective-permute-start.29 = (bf16[112,600]{1,0:T(8,128)(2,1)S(1)}, bf16[112,600]{1,0:T(8,128)(2,1)S(1)}, u32[]{:S(2)}, u32[]{:S(2)}) collective-permute-start(bf16[112,600]{1,0:T(8,128)(2,1)S(1)} %collective-permute-done.22.refs_1_), channel_id=1, source_target_pairs={{0,16},{16,0},{1,17},{17,1},{2,18},{18,2},{3,19},{19,3},{4,20},{20... | collective-permute-start | bytes 403208 | tf_op jit(solution)/shard_map/ppermute | solution.py:165
  107.4 5.1 %collective-permute-start.30 = (bf16[112,600]{1,0:T(8,128)(2,1)S(1)}, bf16[112,600]{1,0:T(8,128)(2,1)S(1)}, u32[]{:S(2)}, u32[]{:S(2)}) collective-permute-start(bf16[112,600]{1,0:T(8,128)(2,1)S(1)} %collective-permute-done.24.refs_2_), channel_id=1, source_target_pairs={{0,16},{16,0},{1,17},{17,1},{2,18},{18,2},{3,19},{19,3},{4,20},{20... | collective-permute-start | bytes 403208 | tf_op jit(solution)/shard_map/ppermute | solution.py:165
  (9 other events, 155.6 us)

commit v4 on v3

--- a/solution.py
+++ b/solution.py
@@ -110,18 +110,24 @@
     return line[0, 0] + line[0, 1]
 
 
-def inverse_kernel(table, own, oth, early, late):
+def inverse_kernel(table, arrived, kept, sent):
     c = lax.axis_index("c")
     row = lax.broadcasted_iota(jnp.int32, (ROWS, 128), 0)
     lane = lax.broadcasted_iota(jnp.int32, (ROWS, 128), 1)
+    v = arrived[0].astype(f32) + arrived[1].astype(f32)
     marked = (row % BIN_PAD == TRACE_ROW) & (lane < 2)
-    span = pl.ds(pl.multiple_of(c * HALF, 16), SPAN)
-    total = jnp.zeros((), f32)
-    r = jnp.zeros((SPAN, SENSORS), f32)
-    for ref, part in ((own, c), (oth, 1 - c)):
-        v = ref[0].astype(f32) + ref[1].astype(f32)
-        total = total + jnp.sum(jnp.where(marked, v[:, :128], 0.0))
-        r = r + jnp.dot(table[part, span], v.astype(bf16), preferred_element_type=f32)
+    total = jnp.sum(jnp.where(marked, v[:, :128], 0.0))
+    v = v.astype(bf16)
+    for half, out in ((1 - c, sent), (c, kept)):
+        span = pl.ds(pl.multiple_of(half * HALF, 16), SPAN)
+        out[...] = jnp.dot(table[c, span], v, preferred_element_type=f32).astype(out.dtype)
+    sent[SPAN - 1 :, :] = trace_line(total)
+    kept[SPAN - 1 :, :] = jnp.full((1, SENSORS), total, f32)
+
+
+def join_kernel(kept, received, early, late):
+    r = kept[...] + received[...].astype(f32)
+    total = kept[SPAN - 1, 0] + read_trace(received, SPAN - 1)
     early[...] = r[: SPLIT[0]].astype(bf16)
     late[...] = r[SPLIT[0] :].astype(bf16)
     late[SPLIT[1] - 1 :, :] = trace_line(total)
@@ -216,8 +222,10 @@
     outgoing = jnp.broadcast_to(outgoing[None], (2, BLOCKS, BIN_PAD, SENSORS))
     outgoing = outgoing.reshape(2 * BLOCKS, BIN_PAD, SENSORS)
     arrived = lax.all_to_all(outgoing, ("h",) + FREQ, 0, 0, tiled=True)
-    pieces = [v.reshape(2, ROWS, SENSORS) for v in (arrived, swap_core(arrived))]
-    parts = call(inverse_kernel, (table, *pieces), [((n, SENSORS), bf16) for n in SPLIT], 4)
+    kept, sent = call(
+        inverse_kernel, (table, arrived.reshape(2, ROWS, SENSORS)), [((SPAN, SENSORS), f32), ((SPAN, SENSORS), bf16)], 4
+    )
+    parts = call(join_kernel, (kept, swap_core(sent)), [((n, SENSORS), bf16) for n in SPLIT], 4)
     near = gather_ring(parts)
     own = [v for at in range(2) for v in (parts[at], *near[at])]
     other = [swap_core(v) for v in own]

time: 115 us -> 115 us (level)
    pallas_call x5 -> x6, Pallas kernels: 5.73 us -> 5.84 us  [call(): pl.pallas_call(kernel, in_specs=[VMEM] * len(operands), out_specs=[VMEM]...]
where the time goes in v4:
time: 115 us
  blocking collectives  44.7 us (39%)
  starting transfers between devices  40.5 us (35%)
  waiting for transfers between devices  18.4 us (16%)
  Pallas kernels  5.84 us (5%)
  other arithmetic  3 us (3%)
  local copies, waits for them, and re-layouts  2.29 us (2%)
    all_to_all x1, blocking collectives, steps(): arrived = lax.all_to_all(outgoing, ('h',) + FREQ, 0, 0, tiled=True)  24.8 us
    ppermute x18, starting transfers between devices, swap_core(): return lax.ppermute(value, 'c', [(0, 1), (1, 0)])  22.8 us
    all_to_all x1, blocking collectives, steps(): lax.all_to_all(spectra.reshape(BLOCKS, BIN_PAD, SENSORS), FREQ, 0, 0, til...  19.9 us
    ppermute x18, starting transfers between devices, shift(): return lax.ppermute(value, axis, [(i, (i + by) % n) for i in range(n)])  17.7 us
    ppermute x18, waiting for transfers between devices, shift(): return lax.ppermute(value, axis, [(i, (i + by) % n) for i in range(n)])  14.8 us
    pallas_call x6, Pallas kernels, call(): pl.pallas_call(kernel, in_specs=[VMEM] * len(operands), out_specs=[VMEM]...  5.84 us
    ppermute x18, waiting for transfers between devices, swap_core(): return lax.ppermute(value, 'c', [(0, 1), (1, 0)])  3.66 us
    convert_element_type x1, other arithmetic, steps(): return (response + noise[0, 0] * probes.astype(f32)).astype(bf16)  2.52 us
  transfers between devices with their start and end apart: 36, of which 12 were waited for; matrix products, arithmetic and copies ran while one was open for 0% of the time, Pallas kernels for 2%

profile of v4, /device:TPU:1, one launch (start us, length us, event | category | flops | bytes accessed | tf_op | source)
XLA Modules:
  0.0 115.0 jit_solution(17917066730949795842)
XLA Ops:
  0.0 2.0 %copy.20 = bf16[4,600,420]{1,2,0:T(8,128)(2,1)S(1)} copy(bf16[4,600,420]{1,0,2:T(4,128)(2,1)} %param.5) | data formatting | bytes 4032000 | tf_op args[0]
  2.5 19.9 %all_to_all.10 = bf16[16,16,600]{2,1,0:T(8,128)(2,1)S(1)} all-to-all(bf16[16,16,600]{2,1,0:T(8,128)(2,1)S(1)} %bitcast.40), channel_id=1, replica_groups=mesh['x'=4,'h'=2,'c'=2,'zl'=4,'y'=4] {'zl','y'}, dimensions={0} | all-to-all | bytes 614400 | tf_op jit(solution)/shard_map/all_to_all | solution.py:190
  22.5 1.3 %collective-permute-start.2 = (bf16[7,16,600]{2,1,0:T(8,128)(2,1)S(1)}, bf16[7,16,600]{2,1,0:T(8,128)(2,1)S(1)}, u32[]{:S(2)}, u32[]{:S(2)}) collective-permute-start(bf16[7,16,600]{2,1,0:T(8,128)(2,1)S(1)} %get-tuple-element.39.refs_0_), channel_id=1, source_target_pairs={{0,64},{64,128},{128,192},{192,0},{1,65},{65,129},{129,193},{193,1... | collective-permute-start | bytes 403208 | tf_op jit(solution)/shard_map/ppermute | solution.py:156
  23.8 2.5 %collective-permute-start.1 = (bf16[7,16,600]{2,1,0:T(8,128)(2,1)S(1)}, bf16[7,16,600]{2,1,0:T(8,128)(2,1)S(1)}, u32[]{:S(2)}, u32[]{:S(2)}) collective-permute-start(bf16[7,16,600]{2,1,0:T(8,128)(2,1)S(1)} %get-tuple-element.39.refs_0_), channel_id=1, source_target_pairs={{0,128},{64,192},{128,0},{192,64},{1,129},{65,193},{129,1},{193,65... | collective-permute-start | bytes 403208 | tf_op jit(solution)/shard_map/ppermute | solution.py:156
  26.2 1.2 %collective-permute-start = (bf16[7,16,600]{2,1,0:T(8,128)(2,1)S(1)}, bf16[7,16,600]{2,1,0:T(8,128)(2,1)S(1)}, u32[]{:S(2)}, u32[]{:S(2)}) collective-permute-start(bf16[7,16,600]{2,1,0:T(8,128)(2,1)S(1)} %get-tuple-element.39.refs_0_), channel_id=1, source_target_pairs={{0,192},{64,0},{128,64},{192,128},{1,193},{65,1},{129,65},{193,129... | collective-permute-start | bytes 403208 | tf_op jit(solution)/shard_map/ppermute | solution.py:156
  28.6 4.6 %collective-permute-start.3 = (bf16[14,16,600]{2,1,0:T(8,128)(2,1)S(1)}, bf16[14,16,600]{2,1,0:T(8,128)(2,1)S(1)}, u32[]{:S(2)}, u32[]{:S(2)}) collective-permute-start(bf16[14,16,600]{2,1,0:T(8,128)(2,1)S(1)} %slice.83), channel_id=1, source_target_pairs={{0,16},{16,0},{1,17},{17,1},{2,18},{18,2},{3,19},{19,3},{4,20},{20... | collective-permute-start | bytes 806408 | tf_op jit(solution)/shard_map/ppermute | solution.py:171
  33.8 2.9 %collective-permute-start.6 = (bf16[7,16,600]{2,1,0:T(8,128)(2,1)S(1)}, bf16[7,16,600]{2,1,0:T(8,128)(2,1)S(1)}, u32[]{:S(2)}, u32[]{:S(2)}) collective-permute-start(bf16[7,16,600]{2,1,0:T(8,128)(2,1)S(1)} %collective-permute-done.2.refs_3_), channel_id=1, source_target_pairs={{0,16},{16,0},{1,17},{17,1},{2,18},{18,2},{3,19},{19,3},{4,20},{20... | collective-permute-start | bytes 403208 | tf_op jit(solution)/shard_map/ppermute | solution.py:171
  36.7 1.9 %collective-permute-start.5 = (bf16[7,16,600]{2,1,0:T(8,128)(2,1)S(1)}, bf16[7,16,600]{2,1,0:T(8,128)(2,1)S(1)}, u32[]{:S(2)}, u32[]{:S(2)}) collective-permute-start(bf16[7,16,600]{2,1,0:T(8,128)(2,1)S(1)} %collective-permute-done.1.refs_2_), channel_id=1, source_target_pairs={{0,16},{16,0},{1,17},{17,1},{2,18},{18,2},{3,19},{19,3},{4,20},{20... | collective-permute-start | bytes 403208 | tf_op jit(solution)/shard_map/ppermute | solution.py:171
  38.6 1.5 %collective-permute-start.4 = (bf16[7,16,600]{2,1,0:T(8,128)(2,1)S(1)}, bf16[7,16,600]{2,1,0:T(8,128)(2,1)S(1)}, u32[]{:S(2)}, u32[]{:S(2)}) collective-permute-start(bf16[7,16,600]{2,1,0:T(8,128)(2,1)S(1)} %collective-permute-done.refs_1_), channel_id=1, source_target_pairs={{0,16},{16,0},{1,17},{17,1},{2,18},{18,2},{3,19},{19,3},{4,20},{20... | collective-permute-start | bytes 403208 | tf_op jit(solution)/shard_map/ppermute | solution.py:171
  40.2 1.6 %collective-permute-start.16 = (bf16[7,16,600]{2,1,0:T(8,128)(2,1)S(1)}, bf16[7,16,600]{2,1,0:T(8,128)(2,1)S(1)}, u32[]{:S(2)}, u32[]{:S(2)}) collective-permute-start(bf16[7,16,600]{2,1,0:T(8,128)(2,1)S(1)} %collective-permute-done.13.refs_3_), channel_id=1, source_target_pairs={{0,16},{16,0},{1,17},{17,1},{2,18},{18,2},{3,19},{19,3},{4,20},{20... | collective-permute-start | bytes 403208 | tf_op jit(solution)/shard_map/ppermute | solution.py:171
  42.4 2.4 %shard_map.56 = (bf16[4,7,16,600]{3,2,1,0:T(8,128)(2,1)S(1)}, bf16[4,7,16,600]{3,2,1,0:T(8,128)(2,1)S(1)}, f32[1,256]{1,0:T(1,128)S(1)}) custom-call(bf16[7,16,600]{2,1,0:T(8,128)(2,1)S(1)} %get-tuple-element.39.refs_0_, bf16[7,16,600]{2,1,0:T(8,128)(2,1)S(1)} %collective-permute-done.refs_1_, bf16[7,16,600]{2,1,0:T(8,128)(2,1)S(1)} %collective-permute-done.1.refs_2_, ...), custom_call_target="tpu_custom_call" | custom-call | flops 2000000000 | tf_op jit(solution)/shard_map/pallas_call | solution.py:175
  44.7 2.3 %shard_map.57 = (bf16[4,7,16,600]{3,2,1,0:T(8,128)(2,1)S(1)}, bf16[4,7,16,600]{3,2,1,0:T(8,128)(2,1)S(1)}, bf16[1,600]{1,0:T(2,128)(2,1)S(1)}) custom-call(bf16[7,16,600]{2,1,0:T(8,128)(2,1)S(1)} %get-tuple-element.40.refs_0_, bf16[7,16,600]{2,1,0:T(8,128)(2,1)S(1)} %collective-permute-done.11.refs_1_, ...), custom_call_target="tpu_custom_call" | custom-call | flops 2000000000 | tf_op jit(solution)/shard_map/pallas_call | solution.py:175
  47.7 1.5 %collective-permute-done.17 = bf16[4,7,16,600]{3,2,1,0:T(8,128)(2,1)S(1)} collective-permute-done((bf16[4,7,16,600]{3,2,1,0:T(8,128)(2,1)S(1)}, bf16[4,7,16,600]{3,2,1,0:T(8,128)(2,1)S(1)}, u32[]{:S(2)}, u32[]{:S(2)}) %collective-permute-start.17) | collective-permute-done | bytes 537632 | tf_op jit(solution)/shard_map/ppermute | solution.py:171
  49.3 1.2 %collective-permute-start.18 = (bf16[7,16,600]{2,1,0:T(8,128)(2,1)S(1)}, bf16[7,16,600]{2,1,0:T(8,128)(2,1)S(1)}, u32[]{:S(2)}, u32[]{:S(2)}) collective-permute-start(bf16[7,16,600]{2,1,0:T(8,128)(2,1)S(1)} %get-tuple-element.36), channel_id=1, source_target_pairs={{0,128},{64,192},{128,0},{192,64},{1,129},{65,193},{129,1},{193,65... | collective-permute-start | bytes 403208 | tf_op jit(solution)/shard_map/ppermute | solution.py:156
  50.5 1.5 %collective-permute-start.20 = (bf16[7,16,600]{2,1,0:T(8,128)(2,1)S(1)}, bf16[7,16,600]{2,1,0:T(8,128)(2,1)S(1)}, u32[]{:S(2)}, u32[]{:S(2)}) collective-permute-start(bf16[7,16,600]{2,1,0:T(8,128)(2,1)S(1)} %get-tuple-element.37), channel_id=1, source_target_pairs={{0,192},{64,0},{128,64},{192,128},{1,193},{65,1},{129,65},{193,129... | collective-permute-start | bytes 403208 | tf_op jit(solution)/shard_map/ppermute | solution.py:156
  52.1 1.9 %collective-permute-start.8 = (bf16[7,16,600]{2,1,0:T(8,128)(2,1)S(1)}, bf16[7,16,600]{2,1,0:T(8,128)(2,1)S(1)}, u32[]{:S(2)}, u32[]{:S(2)}) collective-permute-start(bf16[7,16,600]{2,1,0:T(8,128)(2,1)S(1)} %get-tuple-element.33), channel_id=1, source_target_pairs={{0,128},{64,192},{128,0},{192,64},{1,129},{65,193},{129,1},{193,65... | collective-permute-start | bytes 403208 | tf_op jit(solution)/shard_map/ppermute | solution.py:156
  56.1 1.4 %collective-permute-done.20 = bf16[7,16,600]{2,1,0:T(8,128)(2,1)S(1)} collective-permute-done((bf16[7,16,600]{2,1,0:T(8,128)(2,1)S(1)}, bf16[7,16,600]{2,1,0:T(8,128)(2,1)S(1)}, u32[]{:S(2)}, u32[]{:S(2)}) %collective-permute-start.20) | collective-permute-done | bytes 134432 | tf_op jit(solution)/shard_map/ppermute | solution.py:156
  57.5 1.7 %collective-permute-done.19 = bf16[7,16,600]{2,1,0:T(8,128)(2,1)S(1)} collective-permute-done((bf16[7,16,600]{2,1,0:T(8,128)(2,1)S(1)}, bf16[7,16,600]{2,1,0:T(8,128)(2,1)S(1)}, u32[]{:S(2)}, u32[]{:S(2)}) %collective-permute-start.19) | collective-permute-done | bytes 134432 | tf_op jit(solution)/shard_map/ppermute | solution.py:156
  59.3 2.8 %collective-permute-done.8 = bf16[7,16,600]{2,1,0:T(8,128)(2,1)S(1)} collective-permute-done((bf16[7,16,600]{2,1,0:T(8,128)(2,1)S(1)}, bf16[7,16,600]{2,1,0:T(8,128)(2,1)S(1)}, u32[]{:S(2)}, u32[]{:S(2)}) %collective-permute-start.8) | collective-permute-done | bytes 134432 | tf_op jit(solution)/shard_map/ppermute | solution.py:156
  62.1 1.6 %collective-permute-done.10 = bf16[7,16,600]{2,1,0:T(8,128)(2,1)S(1)} collective-permute-done((bf16[7,16,600]{2,1,0:T(8,128)(2,1)S(1)}, bf16[7,16,600]{2,1,0:T(8,128)(2,1)S(1)}, u32[]{:S(2)}, u32[]{:S(2)}) %collective-permute-start.10) | collective-permute-done | bytes 134432 | tf_op jit(solution)/shard_map/ppermute | solution.py:156
  63.7 1.8 %collective-permute-done.9 = bf16[7,16,600]{2,1,0:T(8,128)(2,1)S(1)} collective-permute-done((bf16[7,16,600]{2,1,0:T(8,128)(2,1)S(1)}, bf16[7,16,600]{2,1,0:T(8,128)(2,1)S(1)}, u32[]{:S(2)}, u32[]{:S(2)}) %collective-permute-start.9) | collective-permute-done | bytes 134432 | tf_op jit(solution)/shard_map/ppermute | solution.py:156
  65.9 24.8 %all_to_all.11 = bf16[32,16,600]{2,1,0:T(8,128)(2,1)S(1)} all-to-all(bf16[32,16,600]{2,1,0:T(8,128)(2,1)S(1)} %bitcast.44), channel_id=1, replica_groups=mesh['x'=4,'h'=2,'c'=2,'zl'=4,'y'=4] {'h','zl','y'}, dimensions={0} | all-to-all | bytes 1228800 | tf_op jit(solution)/shard_map/all_to_all | solution.py:224
  91.1 2.6 %collective-permute-start.21 = (bf16[216,600]{1,0:T(8,128)(2,1)S(1)}, bf16[216,600]{1,0:T(8,128)(2,1)S(1)}, u32[]{:S(2)}, u32[]{:S(2)}) collective-permute-start(bf16[216,600]{1,0:T(8,128)(2,1)S(1)} %get-tuple-element.27), channel_id=1, source_target_pairs={{0,16},{16,0},{1,17},{17,1},{2,18},{18,2},{3,19},{19,3},{4,20},{20... | collective-permute-start | bytes 777608 | tf_op jit(solution)/shard_map/ppermute | solution.py:171
  93.7 1.2 %collective-permute-done.21.received = bf16[216,600]{1,0:T(8,128)(2,1)S(1)} collective-permute-done((bf16[216,600]{1,0:T(8,128)(2,1)S(1)}, bf16[216,600]{1,0:T(8,128)(2,1)S(1)}, u32[]{:S(2)}, u32[]{:S(2)}) %collective-permute-start.21) | collective-permute-done | bytes 259232 | tf_op jit(solution)/shard_map/ppermute | solution.py:171
  95.8 1.1 collective-permute-start.27
  96.8 1.6 %collective-permute-start.25 = (bf16[104,600]{1,0:T(8,128)(2,1)S(1)}, bf16[104,600]{1,0:T(8,128)(2,1)S(1)}, u32[]{:S(2)}, u32[]{:S(2)}) collective-permute-start(bf16[104,600]{1,0:T(8,128)(2,1)S(1)} %get-tuple-element.29.refs_4_), channel_id=1, source_target_pairs={{0,192},{64,0},{128,64},{192,128},{1,193},{65,1},{129,65},{193,129... | collective-permute-start | bytes 374408 | tf_op jit(solution)/shard_map/ppermute | solution.py:156
  99.1 1.3 %collective-permute-start.22 = (bf16[112,600]{1,0:T(8,128)(2,1)S(1)}, bf16[112,600]{1,0:T(8,128)(2,1)S(1)}, u32[]{:S(2)}, u32[]{:S(2)}) collective-permute-start(bf16[112,600]{1,0:T(8,128)(2,1)S(1)} %get-tuple-element.28.refs_0_), channel_id=1, source_target_pairs={{0,192},{64,0},{128,64},{192,128},{1,193},{65,1},{129,65},{193,129... | collective-permute-start | bytes 403208 | tf_op jit(solution)/shard_map/ppermute | solution.py:156
  101.2 2.8 %collective-permute-done.27.refs_7_ = bf16[104,600]{1,0:T(8,128)(2,1)S(1)} collective-permute-done((bf16[104,600]{1,0:T(8,128)(2,1)S(1)}, bf16[104,600]{1,0:T(8,128)(2,1)S(1)}, u32[]{:S(2)}, u32[]{:S(2)}) %collective-permute-start.27) | collective-permute-done | bytes 124832 | tf_op jit(solution)/shard_map/ppermute | solution.py:156
  104.1 1.2 %collective-permute-start.35 = (bf16[104,600]{1,0:T(8,128)(2,1)S(1)}, bf16[104,600]{1,0:T(8,128)(2,1)S(1)}, u32[]{:S(2)}, u32[]{:S(2)}) collective-permute-start(bf16[104,600]{1,0:T(8,128)(2,1)S(1)} %collective-permute-done.27.refs_7_), channel_id=1, source_target_pairs={{0,16},{16,0},{1,17},{17,1},{2,18},{18,2},{3,19},{19,3},{4,20},{20... | collective-permute-start | bytes 374408 | tf_op jit(solution)/shard_map/ppermute | solution.py:171
  105.3 1.3 %collective-permute-start.26 = (bf16[104,600]{1,0:T(8,128)(2,1)S(1)}, bf16[104,600]{1,0:T(8,128)(2,1)S(1)}, u32[]{:S(2)}, u32[]{:S(2)}) collective-permute-start(bf16[104,600]{1,0:T(8,128)(2,1)S(1)} %collective-permute-done.25.refs_5_), channel_id=1, source_target_pairs={{0,192},{64,0},{128,64},{192,128},{1,193},{65,1},{129,65},{193,129... | collective-permute-start | bytes 374408 | tf_op jit(solution)/shard_map/ppermute | solution.py:156
  107.1 2.5 %collective-permute-start.30 = (bf16[112,600]{1,0:T(8,128)(2,1)S(1)}, bf16[112,600]{1,0:T(8,128)(2,1)S(1)}, u32[]{:S(2)}, u32[]{:S(2)}) collective-permute-start(bf16[112,600]{1,0:T(8,128)(2,1)S(1)} %collective-permute-done.24.refs_2_), channel_id=1, source_target_pairs={{0,16},{16,0},{1,17},{17,1},{2,18},{18,2},{3,19},{19,3},{4,20},{20... | collective-permute-start | bytes 403208 | tf_op jit(solution)/shard_map/ppermute | solution.py:171
  112.5 2.5 %add_convert_fusion = bf16[4,600,420]{1,0,2:T(4,128)(2,1)} fusion(bf16[4,600,420]{1,0,2:T(4,128)(2,1)S(1)} %copy-done.4, bf16[4,420,600]{2,1,0:T(8,128)(2,1)S(1)} %get-tuple-element.30, f32[]{:T(128)S(1)} %bitcast.43), kind=kLoop, calls=%fused_computation | loop fusion | flops 5040000 | bytes 6048004 | tf_op jit(solution)/shard_map/convert_element_type | solution.py:234
  (72 shorter events, 12.4 us)
Async XLA Ops:
  22.5 6.1 %collective-permute-start.2 = (bf16[7,16,600]{2,1,0:T(8,128)(2,1)S(1)}, bf16[7,16,600]{2,1,0:T(8,128)(2,1)S(1)}, u32[]{:S(2)}, u32[]{:S(2)}) collective-permute-start(bf16[7,16,600]{2,1,0:T(8,128)(2,1)S(1)} %get-tuple-element.39.refs_0_), channel_id=1, source_target_pairs={{0,64},{64,128},{128,192},{192,0},{1,65},{65,129},{129,193},{193,1... | collective-permute-start | bytes 403208 | tf_op jit(solution)/shard_map/ppermute | solution.py:156
  23.8 9.5 %collective-permute-start.1 = (bf16[7,16,600]{2,1,0:T(8,128)(2,1)S(1)}, bf16[7,16,600]{2,1,0:T(8,128)(2,1)S(1)}, u32[]{:S(2)}, u32[]{:S(2)}) collective-permute-start(bf16[7,16,600]{2,1,0:T(8,128)(2,1)S(1)} %get-tuple-element.39.refs_0_), channel_id=1, source_target_pairs={{0,128},{64,192},{128,0},{192,64},{1,129},{65,193},{129,1},{193,65... | collective-permute-start | bytes 403208 | tf_op jit(solution)/shard_map/ppermute | solution.py:156
  26.2 7.6 %collective-permute-start = (bf16[7,16,600]{2,1,0:T(8,128)(2,1)S(1)}, bf16[7,16,600]{2,1,0:T(8,128)(2,1)S(1)}, u32[]{:S(2)}, u32[]{:S(2)}) collective-permute-start(bf16[7,16,600]{2,1,0:T(8,128)(2,1)S(1)} %get-tuple-element.39.refs_0_), channel_id=1, source_target_pairs={{0,192},{64,0},{128,64},{192,128},{1,193},{65,1},{129,65},{193,129... | collective-permute-start | bytes 403208 | tf_op jit(solution)/shard_map/ppermute | solution.py:156
  27.4 9.3 %collective-permute-start.13 = (bf16[7,16,600]{2,1,0:T(8,128)(2,1)S(1)}, bf16[7,16,600]{2,1,0:T(8,128)(2,1)S(1)}, u32[]{:S(2)}, u32[]{:S(2)}) collective-permute-start(bf16[7,16,600]{2,1,0:T(8,128)(2,1)S(1)} %get-tuple-element.40.refs_0_), channel_id=1, source_target_pairs={{0,64},{64,128},{128,192},{192,0},{1,65},{65,129},{129,193},{193,1... | collective-permute-start | bytes 403208 | tf_op jit(solution)/shard_map/ppermute | solution.py:156
  27.7 10.9 %collective-permute-start.12 = (bf16[7,16,600]{2,1,0:T(8,128)(2,1)S(1)}, bf16[7,16,600]{2,1,0:T(8,128)(2,1)S(1)}, u32[]{:S(2)}, u32[]{:S(2)}) collective-permute-start(bf16[7,16,600]{2,1,0:T(8,128)(2,1)S(1)} %get-tuple-element.40.refs_0_), channel_id=1, source_target_pairs={{0,128},{64,192},{128,0},{192,64},{1,129},{65,193},{129,1},{193,65... | collective-permute-start | bytes 403208 | tf_op jit(solution)/shard_map/ppermute | solution.py:156
  28.6 13.7 %collective-permute-start.3 = (bf16[14,16,600]{2,1,0:T(8,128)(2,1)S(1)}, bf16[14,16,600]{2,1,0:T(8,128)(2,1)S(1)}, u32[]{:S(2)}, u32[]{:S(2)}) collective-permute-start(bf16[14,16,600]{2,1,0:T(8,128)(2,1)S(1)} %slice.83), channel_id=1, source_target_pairs={{0,16},{16,0},{1,17},{17,1},{2,18},{18,2},{3,19},{19,3},{4,20},{20... | collective-permute-start | bytes 806408 | tf_op jit(solution)/shard_map/ppermute | solution.py:171
  33.2 6.9 %collective-permute-start.11 = (bf16[7,16,600]{2,1,0:T(8,128)(2,1)S(1)}, bf16[7,16,600]{2,1,0:T(8,128)(2,1)S(1)}, u32[]{:S(2)}, u32[]{:S(2)}) collective-permute-start(bf16[7,16,600]{2,1,0:T(8,128)(2,1)S(1)} %get-tuple-element.40.refs_0_), channel_id=1, source_target_pairs={{0,192},{64,0},{128,64},{192,128},{1,193},{65,1},{129,65},{193,129... | collective-permute-start | bytes 403208 | tf_op jit(solution)/shard_map/ppermute | solution.py:156
  33.8 8.0 %collective-permute-start.6 = (bf16[7,16,600]{2,1,0:T(8,128)(2,1)S(1)}, bf16[7,16,600]{2,1,0:T(8,128)(2,1)S(1)}, u32[]{:S(2)}, u32[]{:S(2)}) collective-permute-start(bf16[7,16,600]{2,1,0:T(8,128)(2,1)S(1)} %collective-permute-done.2.refs_3_), channel_id=1, source_target_pairs={{0,16},{16,0},{1,17},{17,1},{2,18},{18,2},{3,19},{19,3},{4,20},{20... | collective-permute-start | bytes 403208 | tf_op jit(solution)/shard_map/ppermute | solution.py:171
  36.7 5.1 %collective-permute-start.5 = (bf16[7,16,600]{2,1,0:T(8,128)(2,1)S(1)}, bf16[7,16,600]{2,1,0:T(8,128)(2,1)S(1)}, u32[]{:S(2)}, u32[]{:S(2)}) collective-permute-start(bf16[7,16,600]{2,1,0:T(8,128)(2,1)S(1)} %collective-permute-done.1.refs_2_), channel_id=1, source_target_pairs={{0,16},{16,0},{1,17},{17,1},{2,18},{18,2},{3,19},{19,3},{4,20},{20... | collective-permute-start | bytes 403208 | tf_op jit(solution)/shard_map/ppermute | solution.py:171
  38.6 3.7 %collective-permute-start.4 = (bf16[7,16,600]{2,1,0:T(8,128)(2,1)S(1)}, bf16[7,16,600]{2,1,0:T(8,128)(2,1)S(1)}, u32[]{:S(2)}, u32[]{:S(2)}) collective-permute-start(bf16[7,16,600]{2,1,0:T(8,128)(2,1)S(1)} %collective-permute-done.refs_1_), channel_id=1, source_target_pairs={{0,16},{16,0},{1,17},{17,1},{2,18},{18,2},{3,19},{19,3},{4,20},{20... | collective-permute-start | bytes 403208 | tf_op jit(solution)/shard_map/ppermute | solution.py:171
  40.2 4.6 %collective-permute-start.16 = (bf16[7,16,600]{2,1,0:T(8,128)(2,1)S(1)}, bf16[7,16,600]{2,1,0:T(8,128)(2,1)S(1)}, u32[]{:S(2)}, u32[]{:S(2)}) collective-permute-start(bf16[7,16,600]{2,1,0:T(8,128)(2,1)S(1)} %collective-permute-done.13.refs_3_), channel_id=1, source_target_pairs={{0,16},{16,0},{1,17},{17,1},{2,18},{18,2},{3,19},{19,3},{4,20},{20... | collective-permute-start | bytes 403208 | tf_op jit(solution)/shard_map/ppermute | solution.py:171
  41.8 2.9 %collective-permute-start.14 = (bf16[7,16,600]{2,1,0:T(8,128)(2,1)S(1)}, bf16[7,16,600]{2,1,0:T(8,128)(2,1)S(1)}, u32[]{:S(2)}, u32[]{:S(2)}) collective-permute-start(bf16[7,16,600]{2,1,0:T(8,128)(2,1)S(1)} %collective-permute-done.11.refs_1_), channel_id=1, source_target_pairs={{0,16},{16,0},{1,17},{17,1},{2,18},{18,2},{3,19},{19,3},{4,20},{20... | collective-permute-start | bytes 403208 | tf_op jit(solution)/shard_map/ppermute | solution.py:171
  47.5 4.5 %collective-permute-start.7 = (bf16[4,7,16,600]{3,2,1,0:T(8,128)(2,1)S(1)}, bf16[4,7,16,600]{3,2,1,0:T(8,128)(2,1)S(1)}, u32[]{:S(2)}, u32[]{:S(2)}) collective-permute-start(bf16[4,7,16,600]{3,2,1,0:T(8,128)(2,1)S(1)} %get-tuple-element.21), channel_id=1, source_target_pairs={{0,16},{16,0},{1,17},{17,1},{2,18},{18,2},{3,19},{19,3},{4,20},{20... | collective-permute-start | bytes 1612808 | tf_op jit(solution)/shard_map/ppermute | solution.py:171
  49.3 6.6 %collective-permute-start.18 = (bf16[7,16,600]{2,1,0:T(8,128)(2,1)S(1)}, bf16[7,16,600]{2,1,0:T(8,128)(2,1)S(1)}, u32[]{:S(2)}, u32[]{:S(2)}) collective-permute-start(bf16[7,16,600]{2,1,0:T(8,128)(2,1)S(1)} %get-tuple-element.36), channel_id=1, source_target_pairs={{0,128},{64,192},{128,0},{192,64},{1,129},{65,193},{129,1},{193,65... | collective-permute-start | bytes 403208 | tf_op jit(solution)/shard_map/ppermute | solution.py:156
  50.5 7.0 %collective-permute-start.20 = (bf16[7,16,600]{2,1,0:T(8,128)(2,1)S(1)}, bf16[7,16,600]{2,1,0:T(8,128)(2,1)S(1)}, u32[]{:S(2)}, u32[]{:S(2)}) collective-permute-start(bf16[7,16,600]{2,1,0:T(8,128)(2,1)S(1)} %get-tuple-element.37), channel_id=1, source_target_pairs={{0,192},{64,0},{128,64},{192,128},{1,193},{65,1},{129,65},{193,129... | collective-permute-start | bytes 403208 | tf_op jit(solution)/shard_map/ppermute | solution.py:156
  51.9 7.3 %collective-permute-start.19 = (bf16[7,16,600]{2,1,0:T(8,128)(2,1)S(1)}, bf16[7,16,600]{2,1,0:T(8,128)(2,1)S(1)}, u32[]{:S(2)}, u32[]{:S(2)}) collective-permute-start(bf16[7,16,600]{2,1,0:T(8,128)(2,1)S(1)} %get-tuple-element.38), channel_id=1, source_target_pairs={{0,64},{64,128},{128,192},{192,0},{1,65},{65,129},{129,193},{193,1... | collective-permute-start | bytes 403208 | tf_op jit(solution)/shard_map/ppermute | solution.py:156
  52.1 10.0 %collective-permute-start.8 = (bf16[7,16,600]{2,1,0:T(8,128)(2,1)S(1)}, bf16[7,16,600]{2,1,0:T(8,128)(2,1)S(1)}, u32[]{:S(2)}, u32[]{:S(2)}) collective-permute-start(bf16[7,16,600]{2,1,0:T(8,128)(2,1)S(1)} %get-tuple-element.33), channel_id=1, source_target_pairs={{0,128},{64,192},{128,0},{192,64},{1,129},{65,193},{129,1},{193,65... | collective-permute-start | bytes 403208 | tf_op jit(solution)/shard_map/ppermute | solution.py:156
  54.0 9.7 %collective-permute-start.10 = (bf16[7,16,600]{2,1,0:T(8,128)(2,1)S(1)}, bf16[7,16,600]{2,1,0:T(8,128)(2,1)S(1)}, u32[]{:S(2)}, u32[]{:S(2)}) collective-permute-start(bf16[7,16,600]{2,1,0:T(8,128)(2,1)S(1)} %get-tuple-element.34), channel_id=1, source_target_pairs={{0,192},{64,0},{128,64},{192,128},{1,193},{65,1},{129,65},{193,129... | collective-permute-start | bytes 403208 | tf_op jit(solution)/shard_map/ppermute | solution.py:156
  55.9 9.6 %collective-permute-start.9 = (bf16[7,16,600]{2,1,0:T(8,128)(2,1)S(1)}, bf16[7,16,600]{2,1,0:T(8,128)(2,1)S(1)}, u32[]{:S(2)}, u32[]{:S(2)}) collective-permute-start(bf16[7,16,600]{2,1,0:T(8,128)(2,1)S(1)} %get-tuple-element.35), channel_id=1, source_target_pairs={{0,64},{64,128},{128,192},{192,0},{1,65},{65,129},{129,193},{193,1... | collective-permute-start | bytes 403208 | tf_op jit(solution)/shard_map/ppermute | solution.py:156
  91.1 3.8 %collective-permute-start.21 = (bf16[216,600]{1,0:T(8,128)(2,1)S(1)}, bf16[216,600]{1,0:T(8,128)(2,1)S(1)}, u32[]{:S(2)}, u32[]{:S(2)}) collective-permute-start(bf16[216,600]{1,0:T(8,128)(2,1)S(1)} %get-tuple-element.27), channel_id=1, source_target_pairs={{0,16},{16,0},{1,17},{17,1},{2,18},{18,2},{3,19},{19,3},{4,20},{20... | collective-permute-start | bytes 777608 | tf_op jit(solution)/shard_map/ppermute | solution.py:171
  95.0 6.2 %collective-permute-start.23 = (bf16[112,600]{1,0:T(8,128)(2,1)S(1)}, bf16[112,600]{1,0:T(8,128)(2,1)S(1)}, u32[]{:S(2)}, u32[]{:S(2)}) collective-permute-start(bf16[112,600]{1,0:T(8,128)(2,1)S(1)} %get-tuple-element.28.refs_0_), channel_id=1, source_target_pairs={{0,64},{64,128},{128,192},{192,0},{1,65},{65,129},{129,193},{193,1... | collective-permute-start | bytes 403208 | tf_op jit(solution)/shard_map/ppermute | solution.py:156
  95.1 4.1 %collective-permute-start.32 = (bf16[104,600]{1,0:T(8,128)(2,1)S(1)}, bf16[104,600]{1,0:T(8,128)(2,1)S(1)}, u32[]{:S(2)}, u32[]{:S(2)}) collective-permute-start(bf16[104,600]{1,0:T(8,128)(2,1)S(1)} %get-tuple-element.29.refs_4_), channel_id=1, source_target_pairs={{0,16},{16,0},{1,17},{17,1},{2,18},{18,2},{3,19},{19,3},{4,20},{20... | collective-permute-start | bytes 374408 | tf_op jit(solution)/shard_map/ppermute | solution.py:171
  95.8 8.3 %collective-permute-start.27 = (bf16[104,600]{1,0:T(8,128)(2,1)S(1)}, bf16[104,600]{1,0:T(8,128)(2,1)S(1)}, u32[]{:S(2)}, u32[]{:S(2)}) collective-permute-start(bf16[104,600]{1,0:T(8,128)(2,1)S(1)} %get-tuple-element.29.refs_4_), channel_id=1, source_target_pairs={{0,64},{64,128},{128,192},{192,0},{1,65},{65,129},{129,193},{193,1... | collective-permute-start | bytes 374408 | tf_op jit(solution)/shard_map/ppermute | solution.py:156
  96.8 8.5 %collective-permute-start.25 = (bf16[104,600]{1,0:T(8,128)(2,1)S(1)}, bf16[104,600]{1,0:T(8,128)(2,1)S(1)}, u32[]{:S(2)}, u32[]{:S(2)}) collective-permute-start(bf16[104,600]{1,0:T(8,128)(2,1)S(1)} %get-tuple-element.29.refs_4_), channel_id=1, source_target_pairs={{0,192},{64,0},{128,64},{192,128},{1,193},{65,1},{129,65},{193,129... | collective-permute-start | bytes 374408 | tf_op jit(solution)/shard_map/ppermute | solution.py:156
  98.4 8.2 %collective-permute-start.28 = (bf16[112,600]{1,0:T(8,128)(2,1)S(1)}, bf16[112,600]{1,0:T(8,128)(2,1)S(1)}, u32[]{:S(2)}, u32[]{:S(2)}) collective-permute-start(bf16[112,600]{1,0:T(8,128)(2,1)S(1)} %get-tuple-element.28.refs_0_), channel_id=1, source_target_pairs={{0,16},{16,0},{1,17},{17,1},{2,18},{18,2},{3,19},{19,3},{4,20},{20... | collective-permute-start | bytes 403208 | tf_op jit(solution)/shard_map/ppermute | solution.py:171
  99.1 7.7 %collective-permute-start.22 = (bf16[112,600]{1,0:T(8,128)(2,1)S(1)}, bf16[112,600]{1,0:T(8,128)(2,1)S(1)}, u32[]{:S(2)}, u32[]{:S(2)}) collective-permute-start(bf16[112,600]{1,0:T(8,128)(2,1)S(1)} %get-tuple-element.28.refs_0_), channel_id=1, source_target_pairs={{0,192},{64,0},{128,64},{192,128},{1,193},{65,1},{129,65},{193,129... | collective-permute-start | bytes 403208 | tf_op jit(solution)/shard_map/ppermute | solution.py:156
  101.2 5.9 %collective-permute-start.24 = (bf16[112,600]{1,0:T(8,128)(2,1)S(1)}, bf16[112,600]{1,0:T(8,128)(2,1)S(1)}, u32[]{:S(2)}, u32[]{:S(2)}) collective-permute-start(bf16[112,600]{1,0:T(8,128)(2,1)S(1)} %collective-permute-done.23.refs_3_), channel_id=1, source_target_pairs={{0,64},{64,128},{128,192},{192,0},{1,65},{65,129},{129,193},{193,1... | collective-permute-start | bytes 403208 | tf_op jit(solution)/shard_map/ppermute | solution.py:156
  104.1 5.5 %collective-permute-start.35 = (bf16[104,600]{1,0:T(8,128)(2,1)S(1)}, bf16[104,600]{1,0:T(8,128)(2,1)S(1)}, u32[]{:S(2)}, u32[]{:S(2)}) collective-permute-start(bf16[104,600]{1,0:T(8,128)(2,1)S(1)} %collective-permute-done.27.refs_7_), channel_id=1, source_target_pairs={{0,16},{16,0},{1,17},{17,1},{2,18},{18,2},{3,19},{19,3},{4,20},{20... | collective-permute-start | bytes 374408 | tf_op jit(solution)/shard_map/ppermute | solution.py:171
  105.3 5.1 %collective-permute-start.26 = (bf16[104,600]{1,0:T(8,128)(2,1)S(1)}, bf16[104,600]{1,0:T(8,128)(2,1)S(1)}, u32[]{:S(2)}, u32[]{:S(2)}) collective-permute-start(bf16[104,600]{1,0:T(8,128)(2,1)S(1)} %collective-permute-done.25.refs_5_), channel_id=1, source_target_pairs={{0,192},{64,0},{128,64},{192,128},{1,193},{65,1},{129,65},{193,129... | collective-permute-start | bytes 374408 | tf_op jit(solution)/shard_map/ppermute | solution.py:156
  106.6 4.7 %collective-permute-start.31 = (bf16[112,600]{1,0:T(8,128)(2,1)S(1)}, bf16[112,600]{1,0:T(8,128)(2,1)S(1)}, u32[]{:S(2)}, u32[]{:S(2)}) collective-permute-start(bf16[112,600]{1,0:T(8,128)(2,1)S(1)} %collective-permute-done.23.refs_3_), channel_id=1, source_target_pairs={{0,16},{16,0},{1,17},{17,1},{2,18},{18,2},{3,19},{19,3},{4,20},{20... | collective-permute-start | bytes 403208 | tf_op jit(solution)/shard_map/ppermute | solution.py:171
  106.9 4.4 %collective-permute-start.29 = (bf16[112,600]{1,0:T(8,128)(2,1)S(1)}, bf16[112,600]{1,0:T(8,128)(2,1)S(1)}, u32[]{:S(2)}, u32[]{:S(2)}) collective-permute-start(bf16[112,600]{1,0:T(8,128)(2,1)S(1)} %collective-permute-done.22.refs_1_), channel_id=1, source_target_pairs={{0,16},{16,0},{1,17},{17,1},{2,18},{18,2},{3,19},{19,3},{4,20},{20... | collective-permute-start | bytes 403208 | tf_op jit(solution)/shard_map/ppermute | solution.py:171
  107.1 5.1 %collective-permute-start.30 = (bf16[112,600]{1,0:T(8,128)(2,1)S(1)}, bf16[112,600]{1,0:T(8,128)(2,1)S(1)}, u32[]{:S(2)}, u32[]{:S(2)}) collective-permute-start(bf16[112,600]{1,0:T(8,128)(2,1)S(1)} %collective-permute-done.24.refs_2_), channel_id=1, source_target_pairs={{0,16},{16,0},{1,17},{17,1},{2,18},{18,2},{3,19},{19,3},{4,20},{20... | collective-permute-start | bytes 403208 | tf_op jit(solution)/shard_map/ppermute | solution.py:171
  (9 other events, 155.3 us)
